TPU v7x, 32 devices: a whole 2x2x4 slice. The times are simulated.
32 devices in a mesh: grp: 4 (over y, x), dev: 8 (over z, core).
Axes of the slice: x: 2, y: 2, z: 4, core: 2. Of those that a mesh axis runs over, the one named last changes fastest.
Arguments:
- load: float32 [1024, 256, 128], P('grp', 'dev'), may hold values from -11 to 11
- east_class: int32 [1024, 256], P('grp', 'dev'), may hold values from 0 to 7
- north_class: int32 [1024, 256], P('grp', 'dev'), may hold values from 0 to 7
- cond_table: float32 [8], replicated, may hold values from 0.25 to 4
- taps: int32 [128, 16], replicated, may hold values from 0 to 262143
- tap_current: float32 [128, 16], replicated, may hold values from -16 to 16
Outputs:
- potential: float32 [1024, 256, 128], P('grp', 'dev')
Inputs may be any that keep to these rules, and one draw needn't show every extreme that they name: `taps`: tap number i * 256 + j stands for node (i, j).
All inputs are finite; a program needn't handle non-finite values.
Results may differ from a plain program's by a relative error of at most 0.0001.
Values sent between devices are 32-bit elements; how exact they have to be, the bound alone decides.
No kernel may reach another device: no remote copies, remote signals or barrier semaphores. Data moves between devices by JAX's collectives and lax.ppermute only.
A program may use at most 128 MiB of HBM per device.

v0:
```python
import jax
import jax.numpy as jnp
from jax import lax
from jax.sharding import PartitionSpec as P

LEVELS = 5


RELAXATION = 0.8
SHUNT_CONDUCT = 0.01


def with_halo(cells, sides, width):
    for axis, dim in sides:
        count = lax.axis_size(axis)
        ends = count - 1
        head = lax.slice_in_dim(cells, 0, width, axis=dim)
        tail = lax.slice_in_dim(cells, cells.shape[dim] - width, cells.shape[dim], axis=dim)
        cells = jnp.concatenate(
            [
                lax.ppermute(tail, axis, [(i, (i + 1) % count) for i in range(ends)]),
                cells,
                lax.ppermute(head, axis, [((i + 1) % count, i) for i in range(ends)]),
            ],
            axis=dim,
        )
    return cells


def shifted(shard, axis, by):
    size = lax.axis_size(axis)
    pairs = [(i, i + by) for i in range(size) if 0 <= i + by < size]
    return lax.ppermute(shard, axis, pairs)


def pad_diagonal(coef_pad, shunt):
    east_cond = coef_pad[0]
    north_cond = coef_pad[1]
    return (
        shunt
        + east_cond[1:-1, 1:-1]
        + east_cond[:-2, 1:-1]
        + north_cond[1:-1, 1:-1]
        + north_cond[1:-1, :-2]
    )


def operate_padded(padded, coef_pad, shunt):
    east_cond = coef_pad[0]
    north_cond = coef_pad[1]
    diagonal = pad_diagonal(coef_pad, shunt)
    applied = (
        diagonal[..., None] * padded[1:-1, 1:-1]
        - east_cond[1:-1, 1:-1, None] * padded[2:, 1:-1]
        - east_cond[:-2, 1:-1, None] * padded[:-2, 1:-1]
        - north_cond[1:-1, 1:-1, None] * padded[1:-1, 2:]
        - north_cond[1:-1, :-2, None] * padded[1:-1, :-2]
    )
    return (applied, diagonal)


def relax(padded, coef_pad, source, shunt):
    applied, diagonal = operate_padded(padded, coef_pad, shunt)
    return padded[1:-1, 1:-1] + RELAXATION * (source - applied) / diagonal[..., None]


def operate_lead(padded, coef_pad, shunt):
    east_cond = coef_pad[0]
    north_cond = coef_pad[1]
    diagonal = pad_diagonal(coef_pad, shunt)
    applied = (
        diagonal[None] * padded[:, 1:-1, 1:-1]
        - east_cond[None, 1:-1, 1:-1] * padded[:, 2:, 1:-1]
        - east_cond[None, :-2, 1:-1] * padded[:, :-2, 1:-1]
        - north_cond[None, 1:-1, 1:-1] * padded[:, 1:-1, 2:]
        - north_cond[None, 1:-1, :-2] * padded[:, 1:-1, :-2]
    )
    return (applied, diagonal)


def relax_lead(padded, coef_pad, source, shunt):
    applied, diagonal = operate_lead(padded, coef_pad, shunt)
    return padded[:, 1:-1, 1:-1] + RELAXATION * (source - applied) / diagonal[None]


def restrict(values):
    row_count, col_count, cand_count = values.shape
    return values.reshape(row_count // 2, 2, col_count // 2, 2, cand_count).sum(axis=(1, 3))


def restrict_lead(values):
    cand_count, row_count, col_count = values.shape
    return values.reshape(cand_count, row_count // 2, 2, col_count // 2, 2).sum(axis=(2, 4))


def prolong(values):
    return jnp.repeat(jnp.repeat(values, 2, axis=0), 2, axis=1)


def prolong_lead(values):
    return jnp.repeat(jnp.repeat(values, 2, axis=1), 2, axis=2)


def coarsen_conduct(conduct):
    pairs, row_count, col_count = conduct.shape
    coarse_east = conduct[0].reshape(row_count // 2, 2, col_count // 2, 2)[:, 1].sum(axis=-1)
    coarse_north = conduct[1].reshape(row_count // 2, 2, col_count // 2, 2)[:, :, :, 1].sum(axis=1)
    return jnp.stack([coarse_east, coarse_north])


def coarse_factor(east_cond, north_cond, shunt):
    row_count, col_count = east_cond.shape
    node_count = row_count * col_count
    west_cond = jnp.pad(east_cond, ((1, 0), (0, 0)))[:-1]
    south_cond = jnp.pad(north_cond, ((0, 0), (1, 0)))[:, :-1]
    diagonal = (shunt + east_cond + west_cond + north_cond + south_cond).reshape(-1)
    east_flat = east_cond.reshape(-1)
    north_flat = north_cond.reshape(-1)
    matrix = (
        jnp.diag(diagonal)
        - jnp.diag(east_flat[: node_count - col_count], col_count)
        - jnp.diag(east_flat[: node_count - col_count], -col_count)
        - jnp.diag(north_flat[: node_count - 1], 1)
        - jnp.diag(north_flat[: node_count - 1], -1)
    )
    return jnp.linalg.cholesky(matrix)


def space_rim(values):
    return with_halo(values, (("grp", 0), ("dev", 1)), 1)


def group_rim(values):
    padded = with_halo(values, (("grp", 1),), 1)
    return jnp.pad(padded, ((0, 0), (0, 0), (1, 1)))


def group_coef(conduct):
    from_below = shifted(conduct[:, -1:, :], "grp", 1)
    taller = jnp.concatenate([from_below, conduct, jnp.zeros_like(from_below)], axis=1)
    return jnp.pad(taller, ((0, 0), (0, 0), (1, 1)))


def body(load, east_class, north_class, cond_table, taps, tap_current):
    row_count, col_count, cand_count = load.shape
    row_start = lax.axis_index("grp") * row_count
    col_start = lax.axis_index("dev") * col_count
    all_rows = lax.axis_size("grp") * row_count
    all_cols = lax.axis_size("dev") * col_count
    class_ids = jnp.arange(cond_table.shape[0], dtype=jnp.int32)
    east_cond = jnp.sum(jnp.where(east_class[..., None] == class_ids, cond_table, 0.0), axis=-1)
    north_cond = jnp.sum(jnp.where(north_class[..., None] == class_ids, cond_table, 0.0), axis=-1)
    row_ids = row_start + jnp.arange(row_count, dtype=jnp.int32)
    col_ids = col_start + jnp.arange(col_count, dtype=jnp.int32)
    east_cond = jnp.where((row_ids < all_rows - 1)[:, None], east_cond, 0.0)
    north_cond = jnp.where((col_ids < all_cols - 1)[None, :], north_cond, 0.0)
    conduct = jnp.stack([east_cond, north_cond])
    tap_rows = taps // all_cols - row_start
    tap_cols = taps % all_cols - col_start
    row_hits = jnp.where(
        tap_rows[None] == jnp.arange(row_count, dtype=jnp.int32)[:, None, None],
        tap_current[None],
        0.0,
    )
    col_hits = (tap_cols[None] == jnp.arange(col_count, dtype=jnp.int32)[:, None, None]).astype(
        jnp.float32
    )
    injected = jnp.einsum("ick,jck->ijc", row_hits, col_hits, precision=lax.Precision.HIGHEST)
    source = injected - load
    switch = 3
    stored = []
    for height in range(LEVELS):
        shunt = SHUNT_CONDUCT * 4.0**height
        if height == switch:
            source = lax.all_to_all(
                jnp.moveaxis(source, 2, 0), "dev", split_axis=0, concat_axis=2, tiled=True
            )
            conduct = lax.all_gather(conduct, "dev", axis=2, tiled=True)
        if height < switch:
            coef_pad = with_halo(conduct, (("grp", 1), ("dev", 2)), 2)
            coef_thin = coef_pad[:, 1 : coef_pad.shape[1] - 1, 1 : coef_pad.shape[2] - 1]
            rhs_pad = with_halo(source, (("grp", 0), ("dev", 1)), 1)
            initial = RELAXATION * rhs_pad / pad_diagonal(coef_pad, shunt)[..., None]
            potential = relax(initial, coef_thin, source, shunt)
            applied = operate_padded(space_rim(potential), coef_thin, shunt)[0]
            stored.append((potential, source, rhs_pad, coef_pad, coef_thin))
            source = restrict(source - applied)
        else:
            coef_pad = group_coef(conduct)
            initial = RELAXATION * source / pad_diagonal(coef_pad, shunt)[None]
            potential = relax_lead(group_rim(initial), coef_pad, source, shunt)
            applied = operate_lead(group_rim(potential), coef_pad, shunt)[0]
            stored.append((potential, source, source, coef_pad, coef_pad))
            source = restrict_lead(source - applied)
        conduct = coarsen_conduct(conduct)
    whole_source, whole_conduct = (
        lax.all_gather(source, "grp", axis=1, tiled=True),
        lax.all_gather(conduct, "grp", axis=1, tiled=True),
    )
    factor = coarse_factor(whole_conduct[0], whole_conduct[1], SHUNT_CONDUCT * 4.0**LEVELS)
    cand_width, whole_rows, whole_cols = whole_source.shape
    solved = jax.scipy.linalg.cho_solve(
        (factor, True), whole_source.reshape(cand_width, whole_rows * whole_cols).T
    )
    solved = jnp.moveaxis(solved.reshape(whole_rows, whole_cols, cand_width), 2, 0)
    portion = source.shape[1]
    correction = lax.dynamic_slice_in_dim(solved, lax.axis_index("grp") * portion, portion, 1)
    for height in reversed(range(LEVELS)):
        shunt = SHUNT_CONDUCT * 4.0**height
        potential, source, rhs_pad, coef_pad, coef_thin = stored[height]
        if height < switch:
            potential = potential + prolong(correction)
            padded = with_halo(potential, (("grp", 0), ("dev", 1)), 2)
            middle = relax(padded, coef_pad, rhs_pad, shunt)
            potential = relax(middle, coef_thin, source, shunt)
        else:
            potential = potential + prolong_lead(correction)
            for iteration in range(2):
                potential = relax_lead(group_rim(potential), coef_pad, source, shunt)
            if height == switch:
                potential = jnp.moveaxis(
                    lax.all_to_all(potential, "dev", split_axis=2, concat_axis=0, tiled=True), 0, 2
                )
        correction = potential
    return correction


def solution(mesh):
    return jax.shard_map(
        body,
        mesh=mesh,
        in_specs=(P("grp", "dev", None), P("grp", "dev"), P("grp", "dev"), P(), P(), P()),
        out_specs=P("grp", "dev", None),
        check_vma=False,
    )
```

profile of v0, /device:TPU:1, one launch (start us, length us, event | category | flops | bytes accessed | tf_op | source)
XLA Modules:
  0.0 606.1 jit_solution(14267979730713967248)
XLA Ops:
  1.2 3.9 collective-permute-start.4
  14.8 4.0 collective-permute-start.16
  20.3 4.0 collective-permute-start.28
  24.9 15.9 %all_gather.9 = f32[2,32,32]{1,0,2:T(2,128)S(1)} all-gather(f32[2,32,4]{1,0,2:T(2,128)S(1)} %copy.248), channel_id=1, replica_groups=mesh['grp'=4,'dev'=8] {'dev'}, dimensions={2}, use_global_device_ids=true | all-gather | bytes 9216 | tf_op jit(solution)/shard_map/all_gather | solution.py:178
  44.7 5.5 all_gather.10
  51.1 11.7 %cholesky.49 = f32[128,128]{1,0:T(8,128)S(1)} custom-call(f32[128,128]{1,0:T(8,128)S(1)} %cholesky.115), custom_call_target="Cholesky" | custom-call | tf_op jit(solution)/shard_map/jit(cholesky)/cholesky | solution.py:126
  63.8 9.8 %custom-call.18 = f32[1,128,128]{1,2,0:T(8,128)S(1)} custom-call(f32[1,128,128]{2,1,0:T(8,128)S(1)} %get-tuple-element.86), custom_call_target="InvertDiagBlocksLowerTriangular" | custom-call | tf_op jit(solution)/shard_map/jit(cholesky)/cholesky | solution.py:126
  74.1 11.7 %cholesky.103 = f32[128,128]{1,0:T(8,128)S(1)} custom-call(f32[128,128]{1,0:T(8,128)S(1)} %convolution_subtract_fusion), custom_call_target="Cholesky" | custom-call | tf_op jit(solution)/shard_map/jit(cholesky)/cholesky | solution.py:126
  86.5 5.7 copy.220
  92.2 5.5 bitcast_subtract_fusion
  111.4 4.2 collective-permute-start.36
  118.0 4.3 collective-permute-start
  122.3 8.1 %collective-permute-start.30 = (f32[2,68,2]{1,2,0:T(2,128)S(1)}, f32[2,68,2]{1,2,0:T(2,128)S(1)}, u32[]{:S(2)}, u32[]{:S(2)}) collective-permute-start(f32[2,68,2]{1,2,0:T(2,128)S(1)} %get-tuple-element.119), channel_id=1, source_target_pairs={{0,1},{1,2},{2,3},{3,4},{4,5},{5,6},{6,7},{8,9},{9,10},{10,11},{11... | collective-permute-start | bytes 3272 | tf_op jit(solution)/shard_map/ppermute | solution.py:21
  160.4 4.4 collective-permute-done.3
  164.8 5.4 multiply_divide_fusion
  170.2 5.9 fusion.31
  176.1 4.3 fusion.212
  185.6 5.2 collective-permute-start.9
  209.2 11.5 %fusion.20 = f32[256,32,128]{0,1,2:T(8,128)} fusion(f32[256,32,128]{0,1,2:T(8,128)S(1)} %copy-done.2, f32[258,1,128]{0,1,2:T(1,128)S(1)} %collective-permute-done.11, f32[1,32,128]{0,1,2:T(8,128)} %copy.226, f32[256,32,128]{0,1,2:T(8,128)S(1)} %copy-done.6, f32[1,32,128]{0,1,2:T(8,128)} %copy.228, f32[258,1,128]{0,1,2:T(1,128)S(1)} %collective-permute-done.10, ...), kind=kLoop, calls=%fused_computation.38 | loop fusion | flops 18874368 | bytes 13043712 | tf_op jit(solution)/shard_map/sub | solution.py:187
  220.7 5.9 copy.231
  226.6 5.7 reduce_sum.165
  232.3 4.3 collective-permute-start.12
  238.0 4.2 collective-permute-done.13
  242.3 5.5 collective-permute-start.14
  256.3 4.5 collective-permute-start.21
  284.4 5.7 collective-permute-start.26
  304.9 3.8 collective-permute-start.35
  311.2 5.8 all-to-all-start
  317.1 4.9 all-to-all-done
  331.4 6.6 %collective-permute-done.37 = f32[16,1,32]{1,0,2:T(8,128)S(1)} collective-permute-done((f32[16,1,32]{1,0,2:T(8,128)S(1)}, f32[16,1,32]{1,0,2:T(8,128)S(1)}, u32[]{:S(2)}, u32[]{:S(2)}) %collective-permute-start.37) | collective-permute-done | bytes 2080 | tf_op jit(solution)/shard_map/ppermute | solution.py:23
  344.7 6.6 %collective-permute-done.39 = f32[16,1,32]{1,0,2:T(8,128)S(1)} collective-permute-done((f32[16,1,32]{1,0,2:T(8,128)S(1)}, f32[16,1,32]{1,0,2:T(8,128)S(1)}, u32[]{:S(2)}, u32[]{:S(2)}) %collective-permute-start.39) | collective-permute-done | bytes 2080 | tf_op jit(solution)/shard_map/ppermute | solution.py:23
  369.1 5.2 while.1
  374.2 20.5 %custom-call.19 = f32[2,128,128]{1,2,0:T(8,128)S(1)} custom-call(f32[2,128,128]{2,1,0:T(8,128)} %get-tuple-element.12), custom_call_target="InvertDiagBlocksLowerTriangular" | custom-call | tf_op jit(solution)/shard_map/jit(_cho_solve)/triangular_solve | solution.py:202
  398.8 7.9 %all_gather.11 = f32[16,32,8]{0,2,1:T(8,128)} all-gather(f32[16,8,8]{0,2,1:T(8,128)} %reduce_sum.181), channel_id=1, replica_groups=mesh['grp'=4,'dev'=8] {'grp'}, dimensions={1}, use_global_device_ids=true | all-gather | bytes 20480 | tf_op jit(solution)/shard_map/all_gather | solution.py:197
  420.1 4.0 collective-permute-start.49
  436.1 3.8 collective-permute-done.50
  447.1 5.8 collective-permute-done.52
  453.8 17.1 %all_to_all.36 = f32[8,1,2048]{2,1,0:T(1,128)S(1)} all-to-all(f32[8,1,2048]{2,1,0:T(1,128)S(1)} %reshape.247), channel_id=1, replica_groups=mesh['grp'=4,'dev'=8] {'dev'}, dimensions={0} | all-to-all | bytes 131072 | tf_op jit(solution)/shard_map/all_to_all | solution.py:222
  479.3 4.2 collective-permute-start.57
  510.0 3.7 fusion.42
  519.4 3.8 broadcast_in_dim.187
  523.2 6.0 reshape.223
  529.2 4.4 add.454
  556.2 5.4 collective-permute-start.64
  566.3 4.0 pad_maximum_fusion.7
  570.4 22.8 %fusion.5 = f32[258,34,128]{0,1,2:T(8,128)S(1)} fusion(f32[260,2,128]{0,1,2:T(2,128)S(1)} %collective-permute-done.64, f32[2,32,128]{0,1,2:T(8,128)} %copy.274, f32[256,32,128]{0,1,2:T(8,128)} %copy-done.4, f32[2,32,128]{0,1,2:T(8,128)} %copy-done.9, f32[260,2,128]{0,1,2:T(2,128)S(1)} %collective-permute-done.65, f32[260,36,128]{0,1,2:T(8,128)S(1)} %pad_maximum_fusion.7, ...), kind=kLoop, calls=%fused_computation.8 | loop fusion | flops 25824768 | bytes 27424080 | tf_op jit(solution)/shard_map/add | solution.py:64
  593.2 6.6 %fusion.14 = f32[256,32,128]{0,1,2:T(8,128)} fusion(f32[256,32,128]{0,1,2:T(8,128)S(1)} %copy-done.3, f32[258,34,128]{0,1,2:T(8,128)S(1)} %fusion.5, f32[256,32]{0,1:T(8,128)} %copy-done.43, f32[256,32]{0,1:T(8,128)} %copy-done.44, f32[256,32]{0,1:T(8,128)} %copy-done.41, f32[256,32]{0,1:T(8,128)} %copy-done.42, f32[256,32]{0,1:T(8,128)S(1)} %copy-done.40), kind=kLoop, calls=%fused_computation.28 | loop fusion | flops 13631488 | bytes 29523968 | tf_op jit(solution)/shard_map/add | solution.py:64
  599.8 5.9 copy.275
  (492 shorter events, 281.4 us)
Async XLA Ops:
  1.2 129.3 %collective-permute-start.4 = (f32[2,2,32]{1,2,0:T(8,128)S(1)}, f32[2,2,32]{1,2,0:T(8,128)S(1)}, u32[]{:S(2)}, u32[]{:S(2)}) collective-permute-start(f32[2,2,32]{1,2,0:T(8,128)S(1)} %get-tuple-element.87), channel_id=1, source_target_pairs={{0,8},{8,16},{16,24},{1,9},{9,17},{17,25},{2,10},{10,18},{18,26},{... | collective-permute-start | bytes 1544 | tf_op jit(solution)/shard_map/ppermute | solution.py:21
  5.1 127.4 %collective-permute-start.5 = (f32[2,2,32]{1,2,0:T(8,128)S(1)}, f32[2,2,32]{1,2,0:T(8,128)S(1)}, u32[]{:S(2)}, u32[]{:S(2)}) collective-permute-start(f32[2,2,32]{1,2,0:T(8,128)S(1)} %get-tuple-element.88), channel_id=1, source_target_pairs={{8,0},{16,8},{24,16},{9,1},{17,9},{25,17},{10,2},{18,10},{26,18},{... | collective-permute-start | bytes 1544 | tf_op jit(solution)/shard_map/ppermute | solution.py:23
  14.8 103.2 %collective-permute-start.16 = (f32[2,2,16]{1,2,0:T(8,128)S(1)}, f32[2,2,16]{1,2,0:T(8,128)S(1)}, u32[]{:S(2)}, u32[]{:S(2)}) collective-permute-start(f32[2,2,16]{1,2,0:T(8,128)S(1)} %get-tuple-element.135), channel_id=1, source_target_pairs={{0,8},{8,16},{16,24},{1,9},{9,17},{17,25},{2,10},{10,18},{18,26},{... | collective-permute-start | bytes 776 | tf_op jit(solution)/shard_map/ppermute | solution.py:21
  20.3 88.7 %collective-permute-start.28 = (f32[2,2,8]{1,2,0:T(8,128)S(1)}, f32[2,2,8]{1,2,0:T(8,128)S(1)}, u32[]{:S(2)}, u32[]{:S(2)}) collective-permute-start(f32[2,2,8]{1,2,0:T(8,128)S(1)} %get-tuple-element.152), channel_id=1, source_target_pairs={{0,8},{8,16},{16,24},{1,9},{9,17},{17,25},{2,10},{10,18},{18,26},{... | collective-permute-start | bytes 392 | tf_op jit(solution)/shard_map/ppermute | solution.py:21
  41.7 65.3 %collective-permute-start.41 = (f32[2,1,16]{2,1,0:T(1,128)S(1)}, f32[2,1,16]{2,1,0:T(1,128)S(1)}, u32[]{:S(2)}, u32[]{:S(2)}) collective-permute-start(f32[2,1,16]{2,1,0:T(1,128)S(1)} %pad_maximum_fusion.112), channel_id=1, source_target_pairs={{0,8},{8,16},{16,24},{1,9},{9,17},{17,25},{2,10},{10,18},{18,26},{... | collective-permute-start | bytes 392 | tf_op jit(solution)/shard_map/ppermute | solution.py:33
  109.0 13.3 %collective-permute-start.17 = (f32[2,2,16]{1,2,0:T(8,128)S(1)}, f32[2,2,16]{1,2,0:T(8,128)S(1)}, u32[]{:S(2)}, u32[]{:S(2)}) collective-permute-start(f32[2,2,16]{1,2,0:T(8,128)S(1)} %get-tuple-element.136), channel_id=1, source_target_pairs={{8,0},{16,8},{24,16},{9,1},{17,9},{25,17},{10,2},{18,10},{26,18},{... | collective-permute-start | bytes 776 | tf_op jit(solution)/shard_map/ppermute | solution.py:23
  111.4 5.2 collective-permute-start.36
  116.6 33.1 %collective-permute-start.1 = (f32[1,32,128]{2,1,0:T(8,128)S(1)}, f32[1,32,128]{2,1,0:T(8,128)S(1)}, u32[]{:S(2)}, u32[]{:S(2)}) collective-permute-start(f32[1,32,128]{2,1,0:T(8,128)S(1)} %copy.222), channel_id=1, source_target_pairs={{8,0},{16,8},{24,16},{9,1},{17,9},{25,17},{10,2},{18,10},{26,18},{... | collective-permute-start | bytes 49160 | tf_op jit(solution)/shard_map/ppermute | solution.py:23
  118.0 29.8 %collective-permute-start = (f32[1,32,128]{2,1,0:T(8,128)S(1)}, f32[1,32,128]{2,1,0:T(8,128)S(1)}, u32[]{:S(2)}, u32[]{:S(2)}) collective-permute-start(f32[1,32,128]{2,1,0:T(8,128)S(1)} %copy.221), channel_id=1, source_target_pairs={{0,8},{8,16},{16,24},{1,9},{9,17},{17,25},{2,10},{10,18},{18,26},{... | collective-permute-start | bytes 49160 | tf_op jit(solution)/shard_map/ppermute | solution.py:21
  122.3 13.9 %collective-permute-start.30 = (f32[2,68,2]{1,2,0:T(2,128)S(1)}, f32[2,68,2]{1,2,0:T(2,128)S(1)}, u32[]{:S(2)}, u32[]{:S(2)}) collective-permute-start(f32[2,68,2]{1,2,0:T(2,128)S(1)} %get-tuple-element.119), channel_id=1, source_target_pairs={{0,1},{1,2},{2,3},{3,4},{4,5},{5,6},{6,7},{8,9},{9,10},{10,11},{11... | collective-permute-start | bytes 3272 | tf_op jit(solution)/shard_map/ppermute | solution.py:21
  130.6 7.6 %collective-permute-start.31 = (f32[2,68,2]{1,2,0:T(2,128)S(1)}, f32[2,68,2]{1,2,0:T(2,128)S(1)}, u32[]{:S(2)}, u32[]{:S(2)}) collective-permute-start(f32[2,68,2]{1,2,0:T(2,128)S(1)} %get-tuple-element.120), channel_id=1, source_target_pairs={{1,0},{2,1},{3,2},{4,3},{5,4},{6,5},{7,6},{9,8},{10,9},{11,10},{12... | collective-permute-start | bytes 3272 | tf_op jit(solution)/shard_map/ppermute | solution.py:23
  132.5 9.4 %collective-permute-start.18 = (f32[2,132,2]{1,2,0:T(2,128)S(1)}, f32[2,132,2]{1,2,0:T(2,128)S(1)}, u32[]{:S(2)}, u32[]{:S(2)}) collective-permute-start(f32[2,132,2]{1,2,0:T(2,128)S(1)} %get-tuple-element.103), channel_id=1, source_target_pairs={{0,1},{1,2},{2,3},{3,4},{4,5},{5,6},{6,7},{8,9},{9,10},{10,11},{11... | collective-permute-start | bytes 6344 | tf_op jit(solution)/shard_map/ppermute | solution.py:21
  136.2 7.6 %collective-permute-start.19 = (f32[2,132,2]{1,2,0:T(2,128)S(1)}, f32[2,132,2]{1,2,0:T(2,128)S(1)}, u32[]{:S(2)}, u32[]{:S(2)}) collective-permute-start(f32[2,132,2]{1,2,0:T(2,128)S(1)} %get-tuple-element.104), channel_id=1, source_target_pairs={{1,0},{2,1},{3,2},{4,3},{5,4},{6,5},{7,6},{9,8},{10,9},{11,10},{12... | collective-permute-start | bytes 6344 | tf_op jit(solution)/shard_map/ppermute | solution.py:23
  138.2 5.8 collective-permute-start.6
  141.9 4.9 collective-permute-start.7
  157.8 7.0 %collective-permute-start.3 = (f32[258,1,128]{0,1,2:T(1,128)S(1)}, f32[258,1,128]{0,1,2:T(1,128)S(1)}, u32[]{:S(2)}, u32[]{:S(2)}) collective-permute-start(f32[258,1,128]{0,1,2:T(1,128)S(1)} %get-tuple-element.30), channel_id=1, source_target_pairs={{1,0},{2,1},{3,2},{4,3},{5,4},{6,5},{7,6},{9,8},{10,9},{11,10},{12... | collective-permute-start | bytes 396296 | tf_op jit(solution)/shard_map/ppermute | solution.py:23
  184.3 10.2 %collective-permute-start.8 = (f32[1,32,128]{2,1,0:T(8,128)S(1)}, f32[1,32,128]{2,1,0:T(8,128)S(1)}, u32[]{:S(2)}, u32[]{:S(2)}) collective-permute-start(f32[1,32,128]{2,1,0:T(8,128)S(1)} %copy.225), channel_id=1, source_target_pairs={{8,0},{16,8},{24,16},{9,1},{17,9},{25,17},{10,2},{18,10},{26,18},{... | collective-permute-start | bytes 49160 | tf_op jit(solution)/shard_map/ppermute | solution.py:23
  185.6 6.0 collective-permute-start.9
  200.9 7.1 %collective-permute-start.10 = (f32[258,1,128]{0,1,2:T(1,128)S(1)}, f32[258,1,128]{0,1,2:T(1,128)S(1)}, u32[]{:S(2)}, u32[]{:S(2)}) collective-permute-start(f32[258,1,128]{0,1,2:T(1,128)S(1)} %get-tuple-element.27), channel_id=1, source_target_pairs={{1,0},{2,1},{3,2},{4,3},{5,4},{6,5},{7,6},{9,8},{10,9},{11,10},{12... | collective-permute-start | bytes 396296 | tf_op jit(solution)/shard_map/ppermute | solution.py:23
  202.9 6.2 %collective-permute-start.11 = (f32[258,1,128]{0,1,2:T(1,128)S(1)}, f32[258,1,128]{0,1,2:T(1,128)S(1)}, u32[]{:S(2)}, u32[]{:S(2)}) collective-permute-start(f32[258,1,128]{0,1,2:T(1,128)S(1)} %get-tuple-element.28), channel_id=1, source_target_pairs={{0,1},{1,2},{2,3},{3,4},{4,5},{5,6},{6,7},{8,9},{9,10},{10,11},{11... | collective-permute-start | bytes 396296 | tf_op jit(solution)/shard_map/ppermute | solution.py:21
  232.3 5.6 collective-permute-start.12
  236.6 5.6 collective-permute-start.13
  242.3 8.2 %collective-permute-start.14 = (f32[130,1,128]{2,1,0:T(1,128)S(1)}, f32[130,1,128]{2,1,0:T(1,128)S(1)}, u32[]{:S(2)}, u32[]{:S(2)}) collective-permute-start(f32[130,1,128]{2,1,0:T(1,128)S(1)} %get-tuple-element.41), channel_id=1, source_target_pairs={{0,1},{1,2},{2,3},{3,4},{4,5},{5,6},{6,7},{8,9},{9,10},{10,11},{11... | collective-permute-start | bytes 199688 | tf_op jit(solution)/shard_map/ppermute | solution.py:21
  247.8 5.6 collective-permute-start.15
  256.3 5.9 collective-permute-start.21
  265.3 6.3 %collective-permute-start.22 = (f32[130,1,128]{2,1,0:T(1,128)S(1)}, f32[130,1,128]{2,1,0:T(1,128)S(1)}, u32[]{:S(2)}, u32[]{:S(2)}) collective-permute-start(f32[130,1,128]{2,1,0:T(1,128)S(1)} %get-tuple-element.39), channel_id=1, source_target_pairs={{1,0},{2,1},{3,2},{4,3},{5,4},{6,5},{7,6},{9,8},{10,9},{11,10},{12... | collective-permute-start | bytes 199688 | tf_op jit(solution)/shard_map/ppermute | solution.py:23
  267.2 5.0 collective-permute-start.23
  284.4 8.3 %collective-permute-start.26 = (f32[66,1,128]{2,1,0:T(1,128)S(1)}, f32[66,1,128]{2,1,0:T(1,128)S(1)}, u32[]{:S(2)}, u32[]{:S(2)}) collective-permute-start(f32[66,1,128]{2,1,0:T(1,128)S(1)} %get-tuple-element.53), channel_id=1, source_target_pairs={{0,1},{1,2},{2,3},{3,4},{4,5},{5,6},{6,7},{8,9},{9,10},{10,11},{11... | collective-permute-start | bytes 101384 | tf_op jit(solution)/shard_map/ppermute | solution.py:21
  290.1 5.2 collective-permute-start.27
  303.0 5.8 collective-permute-start.34
  311.2 10.8 %all-to-all-start = ((f32[8,1,2048]{2,1,0:T(1,128)}), f32[8,1,2048]{2,1,0:T(1,128)S(1)}, u32[]{:S(2)}, u32[]{:S(2)}) async-start(f32[8,1,2048]{2,1,0:T(1,128)} %reshape.245), calls=%async_computation | async-start | bytes 131072 | tf_op jit(solution)/shard_map/all_to_all | solution.py:175
  323.8 7.6 %collective-permute-start.38 = (f32[16,1,32]{1,0,2:T(8,128)S(1)}, f32[16,1,32]{1,0,2:T(8,128)S(1)}, u32[]{:S(2)}, u32[]{:S(2)}) collective-permute-start(f32[16,1,32]{1,0,2:T(8,128)S(1)} %get-tuple-element.63), channel_id=1, source_target_pairs={{0,8},{8,16},{16,24},{1,9},{9,17},{17,25},{2,10},{10,18},{18,26},{... | collective-permute-start | bytes 6152 | tf_op jit(solution)/shard_map/ppermute | solution.py:21
  326.6 11.4 %collective-permute-start.37 = (f32[16,1,32]{1,0,2:T(8,128)S(1)}, f32[16,1,32]{1,0,2:T(8,128)S(1)}, u32[]{:S(2)}, u32[]{:S(2)}) collective-permute-start(f32[16,1,32]{1,0,2:T(8,128)S(1)} %get-tuple-element.64), channel_id=1, source_target_pairs={{8,0},{16,8},{24,16},{9,1},{17,9},{25,17},{10,2},{18,10},{26,18},{... | collective-permute-start | bytes 6152 | tf_op jit(solution)/shard_map/ppermute | solution.py:23
  338.8 5.9 collective-permute-start.40
  340.5 10.8 %collective-permute-start.39 = (f32[16,1,32]{1,0,2:T(8,128)S(1)}, f32[16,1,32]{1,0,2:T(8,128)S(1)}, u32[]{:S(2)}, u32[]{:S(2)}) collective-permute-start(f32[16,1,32]{1,0,2:T(8,128)S(1)} %get-tuple-element.62), channel_id=1, source_target_pairs={{8,0},{16,8},{24,16},{9,1},{17,9},{25,17},{10,2},{18,10},{26,18},{... | collective-permute-start | bytes 6152 | tf_op jit(solution)/shard_map/ppermute | solution.py:23
  363.7 31.1 %collective-permute-start.45 = (f32[16,1,16]{0,2,1:T(8,128)}, f32[16,1,16]{0,2,1:T(8,128)}, u32[]{:S(2)}, u32[]{:S(2)}) collective-permute-start(f32[16,1,16]{0,2,1:T(8,128)} %get-tuple-element.73), channel_id=1, source_target_pairs={{0,8},{8,16},{16,24},{1,9},{9,17},{17,25},{2,10},{10,18},{18,26},{... | collective-permute-start | bytes 3080 | tf_op jit(solution)/shard_map/ppermute | solution.py:21
  367.1 27.7 %collective-permute-start.44 = (f32[16,1,16]{0,2,1:T(8,128)}, f32[16,1,16]{0,2,1:T(8,128)}, u32[]{:S(2)}, u32[]{:S(2)}) collective-permute-start(f32[16,1,16]{0,2,1:T(8,128)} %get-tuple-element.74), channel_id=1, source_target_pairs={{8,0},{16,8},{24,16},{9,1},{17,9},{25,17},{10,2},{18,10},{26,18},{... | collective-permute-start | bytes 3080 | tf_op jit(solution)/shard_map/ppermute | solution.py:23
  420.1 5.3 collective-permute-start.49
  430.0 6.1 %collective-permute-start.51 = (f32[16,1,32]{1,0,2:T(8,128)S(1)}, f32[16,1,32]{1,0,2:T(8,128)S(1)}, u32[]{:S(2)}, u32[]{:S(2)}) collective-permute-start(f32[16,1,32]{1,0,2:T(8,128)S(1)} %get-tuple-element.59), channel_id=1, source_target_pairs={{0,8},{8,16},{16,24},{1,9},{9,17},{17,25},{2,10},{10,18},{18,26},{... | collective-permute-start | bytes 6152 | tf_op jit(solution)/shard_map/ppermute | solution.py:21
  432.8 7.1 %collective-permute-start.50 = (f32[16,1,32]{1,0,2:T(8,128)S(1)}, f32[16,1,32]{1,0,2:T(8,128)S(1)}, u32[]{:S(2)}, u32[]{:S(2)}) collective-permute-start(f32[16,1,32]{1,0,2:T(8,128)S(1)} %get-tuple-element.60), channel_id=1, source_target_pairs={{8,0},{16,8},{24,16},{9,1},{17,9},{25,17},{10,2},{18,10},{26,18},{... | collective-permute-start | bytes 6152 | tf_op jit(solution)/shard_map/ppermute | solution.py:23
  440.8 6.3 %collective-permute-start.53 = (f32[16,1,32]{1,0,2:T(8,128)S(1)}, f32[16,1,32]{1,0,2:T(8,128)S(1)}, u32[]{:S(2)}, u32[]{:S(2)}) collective-permute-start(f32[16,1,32]{1,0,2:T(8,128)S(1)} %get-tuple-element.57), channel_id=1, source_target_pairs={{0,8},{8,16},{16,24},{1,9},{9,17},{17,25},{2,10},{10,18},{18,26},{... | collective-permute-start | bytes 6152 | tf_op jit(solution)/shard_map/ppermute | solution.py:21
  443.6 9.4 %collective-permute-start.52 = (f32[16,1,32]{1,0,2:T(8,128)S(1)}, f32[16,1,32]{1,0,2:T(8,128)S(1)}, u32[]{:S(2)}, u32[]{:S(2)}) collective-permute-start(f32[16,1,32]{1,0,2:T(8,128)S(1)} %get-tuple-element.58), channel_id=1, source_target_pairs={{8,0},{16,8},{24,16},{9,1},{17,9},{25,17},{10,2},{18,10},{26,18},{... | collective-permute-start | bytes 6152 | tf_op jit(solution)/shard_map/ppermute | solution.py:23
  479.3 10.9 %collective-permute-start.57 = (f32[68,2,128]{2,1,0:T(2,128)S(1)}, f32[68,2,128]{2,1,0:T(2,128)S(1)}, u32[]{:S(2)}, u32[]{:S(2)}) collective-permute-start(f32[68,2,128]{2,1,0:T(2,128)S(1)} %get-tuple-element.49), channel_id=1, source_target_pairs={{1,0},{2,1},{3,2},{4,3},{5,4},{6,5},{7,6},{9,8},{10,9},{11,10},{12... | collective-permute-start | bytes 208904 | tf_op jit(solution)/shard_map/ppermute | solution.py:23
  483.5 6.7 %collective-permute-start.56 = (f32[68,2,128]{2,1,0:T(2,128)S(1)}, f32[68,2,128]{2,1,0:T(2,128)S(1)}, u32[]{:S(2)}, u32[]{:S(2)}) collective-permute-start(f32[68,2,128]{2,1,0:T(2,128)S(1)} %get-tuple-element.50), channel_id=1, source_target_pairs={{0,1},{1,2},{2,3},{3,4},{4,5},{5,6},{6,7},{8,9},{9,10},{10,11},{11... | collective-permute-start | bytes 208904 | tf_op jit(solution)/shard_map/ppermute | solution.py:21
  501.9 6.5 %collective-permute-start.61 = (f32[132,2,128]{2,1,0:T(2,128)S(1)}, f32[132,2,128]{2,1,0:T(2,128)S(1)}, u32[]{:S(2)}, u32[]{:S(2)}) collective-permute-start(f32[132,2,128]{2,1,0:T(2,128)S(1)} %get-tuple-element.37), channel_id=1, source_target_pairs={{1,0},{2,1},{3,2},{4,3},{5,4},{6,5},{7,6},{9,8},{10,9},{11,10},{12... | collective-permute-start | bytes 405512 | tf_op jit(solution)/shard_map/ppermute | solution.py:23
  538.9 5.5 collective-permute-start.62
  553.8 11.0 %collective-permute-start.65 = (f32[260,2,128]{0,1,2:T(2,128)S(1)}, f32[260,2,128]{0,1,2:T(2,128)S(1)}, u32[]{:S(2)}, u32[]{:S(2)}) collective-permute-start(f32[260,2,128]{0,1,2:T(2,128)S(1)} %get-tuple-element.25), channel_id=1, source_target_pairs={{1,0},{2,1},{3,2},{4,3},{5,4},{6,5},{7,6},{9,8},{10,9},{11,10},{12... | collective-permute-start | bytes 798728 | tf_op jit(solution)/shard_map/ppermute | solution.py:23
  556.2 10.1 %collective-permute-start.64 = (f32[260,2,128]{0,1,2:T(2,128)S(1)}, f32[260,2,128]{0,1,2:T(2,128)S(1)}, u32[]{:S(2)}, u32[]{:S(2)}) collective-permute-start(f32[260,2,128]{0,1,2:T(2,128)S(1)} %get-tuple-element.26), channel_id=1, source_target_pairs={{0,1},{1,2},{2,3},{3,4},{4,5},{5,6},{6,7},{8,9},{9,10},{10,11},{11... | collective-permute-start | bytes 798728 | tf_op jit(solution)/shard_map/ppermute | solution.py:21
  (94 other events, 1746.2 us)
where the time goes:
time: 615 us; the launch traced here: 606 us
  starting transfers between devices  182 us (30%)
  other arithmetic  175 us (28%)
  local copies, waits for them, and re-layouts  98.8 us (16%)
  waiting for transfers between devices  92 us (15%)
  blocking collectives  46.4 us (8%)
  matrix products  8.55 us (1%)
    ppermute x32, starting transfers between devices, with_halo(): lax.ppermute(tail, axis, [(i, (i + 1) % count) for i in range(ends)])  115 us
    ppermute x32, waiting for transfers between devices, with_halo(): lax.ppermute(head, axis, [((i + 1) % count, i) for i in range(ends)])  70.8 us
    ppermute x32, starting transfers between devices, with_halo(): lax.ppermute(head, axis, [((i + 1) % count, i) for i in range(ends)])  53.9 us
    add x9, other arithmetic, relax(): padded[1:-1, 1:-1] + RELAXATION * (source - applied) / diagonal[..., None]  46.7 us
    another operation x7, other arithmetic, coarse_factor(): return jnp.linalg.cholesky(matrix)  34.6 us
    another operation x4, other arithmetic, body(): jax.scipy.linalg.cho_solve((factor, True), whole_source.reshape(cand_widt...  21.1 us
    slice x20, local copies, waits for them, and re-layouts, with_halo(): lax.slice_in_dim(cells, cells.shape[dim] - width, cells.shape[dim], axis=...  18 us
    all_to_all x1, blocking collectives, body(): lax.all_to_all(potential, 'dev', split_axis=2, concat_axis=0, tiled=True)  17.1 us
  transfers between devices with their start and end apart: 67, of which 34 were waited for; matrix products, arithmetic and copies ran while one was open for 18% of the time, Pallas kernels for 0%

commit v1 on v0

v1 whole, which is shorter than its diff:
```python
import functools

import jax
import jax.numpy as jnp
from jax import lax
from jax.experimental import pallas as pl
from jax.experimental.pallas import tpu as pltpu
from jax.sharding import PartitionSpec as P

LEVELS = 5
RELAXATION = 0.8
KEEP = 1.0 - RELAXATION
SHUNT_CONDUCT = 0.01
AXES = ("grp", "dev")
HIGH = lax.Precision.HIGHEST

HALO = 10
PAD = 16
LANES = 128
GROUP = 8


def exchange(tail, head, axis):
    count = lax.axis_size(axis)
    up = [(i, i + 1) for i in range(count - 1)]
    down = [(i + 1, i) for i in range(count - 1)]
    return lax.ppermute(tail, axis, up), lax.ppermute(head, axis, down)


def pack(rows, extra):
    flat = extra.reshape(-1)
    size = -flat.shape[0] % LANES
    return jnp.concatenate([rows.reshape(-1, LANES), jnp.pad(flat, (0, size)).reshape(-1, LANES)])


def unpack(packed, rows, extra):
    count = rows.size // LANES
    flat = packed[count:].reshape(-1)[: extra.size]
    return packed[:count].reshape(rows.shape), flat.reshape(extra.shape)


def pair_matrix(count, half, first=0, odd_only=False):
    fine = jnp.arange(count)[:, None] - first
    coarse = jnp.arange(half)[None, :]
    hit = fine == 2 * coarse + 1 if odd_only else fine // 2 == coarse
    return hit.astype(jnp.float32)


def stencil_coefs(east, north, shunt):
    west = east[:, :-1]
    east = east[:, 1:]
    north = north[:, 1:]
    south = jnp.pad(north, ((1, 0), (0, 0)))[:-1]
    diag = shunt + east + west + north + south
    coefs = jnp.stack([east, west, north, south, RELAXATION / diag, diag])
    rows = coefs.shape[2]
    tiles = -(-rows // LANES)
    coefs = jnp.pad(coefs, ((0, 0), (0, 0), (0, tiles * LANES - rows)))
    return jnp.moveaxis(coefs.reshape(6, coefs.shape[1], tiles, LANES), 2, 1)


def row_coefs(ref, kinds, g):
    per_tile = LANES // GROUP
    shift = lax.rem(LANES - lax.rem(g, per_tile) * GROUP, LANES)
    return [pltpu.roll(ref[k, g // per_tile], shift, 1) for k in kinds]


def spread(coef, r):
    return jnp.broadcast_to(coef[:, r : r + 1], coef.shape)


def around(ref, row, cols, coefs):
    east, west, north, south = coefs
    here = ref[row, cols, :]
    count = here.shape[0]
    total = east * ref[row + 1, cols, :] + west * ref[row - 1, cols, :]
    total += north * pltpu.roll(here, count - 1, 0) + south * pltpu.roll(here, 1, 0)
    return here, total


def down_kernel(
    dims, tap_count, tap_code, tap_amps, own, west, east, north, south, corners, coef0, coef1,
    s0, p0, s1, p1, slab, u0, u1, s2, pair, pair1,
):
    rows, cols, nd, pc = dims
    wide = cols + 2 * PAD
    everything = slice(None)

    zero_side = jnp.zeros((s0.shape[0], PAD, LANES), jnp.float32)
    s0[:, 0:PAD, :] = zero_side
    s0[:, PAD + cols :, :] = zero_side
    tail = s0.shape[0] - (rows + 2 * HALO)
    s0[rows + 2 * HALO :, :, :] = jnp.zeros((tail, wide, LANES), jnp.float32)
    s0[HALO : HALO + rows, PAD : PAD + cols, :] = -own[...]
    s0[0:HALO, PAD : PAD + cols, :] = -north[...]
    s0[HALO + rows : rows + 2 * HALO, PAD : PAD + cols, :] = -south[...]
    flat = s0.reshape(s0.shape[0] * wide, LANES)
    for j in range(HALO):
        for side, (strip, first) in enumerate(((west, PAD - HALO), (east, PAD + cols))):
            flat[pl.ds(HALO * wide + first + j, rows, stride=wide), :] = -strip[j]
            for end, base in enumerate((0, HALO + rows)):
                block = corners[side, end, j * HALO : (j + 1) * HALO, :]
                flat[pl.ds(base * wide + first + j, HALO, stride=wide), :] = -block

    lane = lax.broadcasted_iota(jnp.int32, (GROUP, LANES), 1)
    sub = lax.broadcasted_iota(jnp.int32, (GROUP, LANES), 0)

    def add_tap(k, carry):
        code = tap_code[k]
        node = code // LANES
        base = pl.multiple_of(node // GROUP * GROUP, GROUP)
        hit = (lane == lax.rem(code, LANES)) & (sub == node - base)
        flat[pl.ds(base, GROUP), :] += jnp.where(hit, tap_amps[k], 0.0)
        return carry

    lax.fori_loop(0, tap_count[0], add_tap, 0)

    def smooth_and_restrict(source, start, pre, coef, pair, store):
        width = source.shape[1]
        groups = source.shape[0] // GROUP
        zero = jnp.zeros((width, LANES), jnp.float32)
        last = pre.shape[0] - 1
        for ref in (start, pre):
            ref[0] = zero
            ref[last] = zero

        def first(g, carry):
            (weight,) = row_coefs(coef, (4,), g)
            for r in range(GROUP):
                row = g * GROUP + r
                start[row + 1] = spread(weight, r) * source[row]
            return carry

        def second(g, carry):
            found = row_coefs(coef, (0, 1, 2, 3, 4), g)
            for r in range(GROUP):
                row = g * GROUP + r
                c = [spread(x, r) for x in found]
                _, total = around(start, row + 1, everything, c[:4])
                pre[row + 1] = c[4] * ((2.0 - RELAXATION) * source[row] + total)
            return carry

        def third(g, carry):
            found = row_coefs(coef, (0, 1, 2, 3, 5), g)
            for m in range(GROUP // 2):
                both = None
                for r in (2 * m, 2 * m + 1):
                    row = g * GROUP + r
                    c = [spread(x, r) for x in found]
                    here, total = around(pre, row + 1, everything, c[:4])
                    rest = source[row] - c[4] * here + total
                    both = rest if both is None else both + rest
                pair[m] = both
                store(g * (GROUP // 2) + m, m)
            return carry

        lax.fori_loop(0, groups, first, 0)
        lax.fori_loop(0, groups, second, 0)
        lax.fori_loop(0, groups, third, 0)

    half = (cols + 2 * (HALO - 2)) // 2
    s1[...] = jnp.zeros_like(s1)

    def store1(k, m):
        first = PAD - (HALO - 2)
        s1[k + 1] = pair[m, pl.ds(first, half, stride=2), :] + pair[m, pl.ds(first + 1, half, stride=2), :]

    smooth_and_restrict(s0, u0, p0, coef0, pair, store1)
    quarter = cols // 4

    def store2(k, m):
        s2[pl.ds(pl.multiple_of(k * quarter, quarter), quarter), :] = (
            pair1[m, pl.ds(4, quarter, stride=2), :] + pair1[m, pl.ds(5, quarter, stride=2), :]
        )

    smooth_and_restrict(s1, u1, p1, coef1, pair1, store2)
    rows2 = rows // 4
    per = LANES // rows2
    groups = quarter // per
    for jp in range(groups):
        parts = [
            s2[pl.ds(3 * quarter + jl * groups + jp, rows2, stride=quarter), :] for jl in range(per)
        ]
        turned = jnp.concatenate(parts, axis=0).T
        for p in range(pc):
            slab[pl.ds(jp * pc + p, nd, stride=groups * pc), :] = turned[p * nd : (p + 1) * nd]


def up_kernel(dims, back, s0, p0, s1, p1, coef0, coef1, out, x2, v1a, v1b, wide1, v0a, v0b):
    rows, cols, nd, pc = dims
    quarter = cols // 4
    wide2 = quarter + 4
    pitch2 = x2.shape[0] // (rows // 4 + 4)
    for jw in range(wide2):
        parts = [back[pl.ds(jw * pc + p, nd, stride=wide2 * pc), :] for p in range(pc)]
        turned = jnp.concatenate(parts, axis=0).T
        x2[pl.ds(jw, rows // 4 + 4, stride=pitch2), :] = turned[: rows // 4 + 4]

    def step(source, old, new, coef, cols_at, source_cols, lo, hi):
        def go(g, carry):
            found = row_coefs(coef, (0, 1, 2, 3, 4), g)
            found = [f[cols_at] for f in found]
            for r in range(GROUP):
                row = g * GROUP + r
                c = [spread(x, r) for x in found]
                here, total = around(old, row + 1, slice(None), c[:4])
                new[row + 1] = KEEP * here + c[4] * (source[row, source_cols, :] + total)
            return carry

        lax.fori_loop(lo, hi, go, 0)

    v1a[...] = jnp.zeros_like(v1a)
    v1b[...] = jnp.zeros_like(v1b)
    width1 = 2 * wide2

    def lift1(k, carry):
        x = x2[pl.ds(k * pitch2, pitch2), :][:wide2]
        wide1[pl.ds(0, wide2, stride=2), :] = x
        wide1[pl.ds(1, wide2, stride=2), :] = x
        both = wide1[0:width1, :]
        for r in range(2):
            row = 2 * k + 3 + r
            v1a[row] = p1[row] + both
        return carry

    lax.fori_loop(0, rows // 4 + 4, lift1, 0)
    whole = slice(None)
    step(s1, v1a, v1b, coef1, whole, whole, 0, s1.shape[0] // GROUP)
    step(s1, v1b, v1a, coef1, whole, whole, 0, s1.shape[0] // GROUP)

    width0 = 2 * width1
    left = PAD - (HALO - 2)
    window = slice(left, left + width0)
    first = HALO // GROUP
    last = -(-(HALO + rows + 1) // GROUP)

    def lift0(k, carry):
        x = v1a[k + 6]
        wide1[pl.ds(0, width1, stride=2), :] = x
        wide1[pl.ds(1, width1, stride=2), :] = x
        both = wide1[...]
        for r in range(2):
            row = 2 * k + HALO - 2 + r + 1
            v0a[row] = p0[row, window, :] + both
        return carry

    v0a[first * GROUP] = jnp.zeros((width0, LANES), jnp.float32)
    for row in range(rows + HALO + 2 + 1, v0a.shape[0]):
        v0a[row] = jnp.zeros((width0, LANES), jnp.float32)
    lax.fori_loop(0, rows // 2 + 2, lift0, 0)
    v0b[first * GROUP] = jnp.zeros((width0, LANES), jnp.float32)
    step(s0, v0a, v0b, coef0, window, window, first, last)
    v0b[last * GROUP + 1] = jnp.zeros((width0, LANES), jnp.float32)

    own = slice(PAD - left, PAD - left + cols)

    def finish(g, carry):
        found = [f[window] for f in row_coefs(coef0, (0, 1, 2, 3, 4), g)]
        for r in range(GROUP):
            row = g * GROUP + r
            c = [spread(x, r) for x in found]
            here, total = around(v0b, row + 1, slice(None), c[:4])
            done = KEEP * here + c[4] * (s0[row, window, :] + total)

            @pl.when((row >= HALO) & (row < HALO + rows))
            def _():
                out[row - HALO] = done[own]

        return carry

    lax.fori_loop(first, last, finish, 0)


VMEM = pl.BlockSpec(memory_space=pltpu.VMEM)
SMEM = pl.BlockSpec(memory_space=pltpu.SMEM)
PARAMS = pltpu.CompilerParams(vmem_limit_bytes=60 * 2**20)


def shape(*dims):
    return jax.ShapeDtypeStruct(dims, jnp.float32)


def vmem(*dims):
    return pltpu.VMEM(dims, jnp.float32)


def operate_lead(v, east, north, shunt):
    padded = jnp.pad(v, ((0, 0), (1, 1), (1, 1)))
    west = jnp.pad(east, ((0, 0), (1, 0)))[:, :-1]
    south = jnp.pad(north, ((1, 0), (0, 0)))[:-1]
    diag = shunt + east + west + north + south
    applied = (
        diag * v
        - east * padded[:, 1:-1, 2:]
        - west * padded[:, 1:-1, :-2]
        - north * padded[:, 2:, 1:-1]
        - south * padded[:, :-2, 1:-1]
    )
    return applied, diag


def relax_lead(v, source, east, north, shunt):
    applied, diag = operate_lead(v, east, north, shunt)
    return v + RELAXATION * (source - applied) / diag


def coarse_cycle(source, east, north, level):
    shunt = SHUNT_CONDUCT * 4.0**level
    count, nj, ni = source.shape
    if level == LEVELS:
        size = nj * ni
        west = jnp.pad(east, ((0, 0), (1, 0)))[:, :-1]
        south = jnp.pad(north, ((1, 0), (0, 0)))[:-1]
        diag = (shunt + east + west + north + south).reshape(-1)
        e = east.reshape(-1)[: size - 1]
        n = north.reshape(-1)[: size - ni]
        matrix = (
            jnp.diag(diag) - jnp.diag(e, 1) - jnp.diag(e, -1) - jnp.diag(n, ni) - jnp.diag(n, -ni)
        )
        factor = jnp.linalg.cholesky(matrix)
        solved = jax.scipy.linalg.cho_solve((factor, True), source.reshape(count, size).T)
        return solved.T.reshape(source.shape)
    _, diag = operate_lead(source, east, north, shunt)
    pre = relax_lead(RELAXATION * source / diag, source, east, north, shunt)
    rest = source - operate_lead(pre, east, north, shunt)[0]
    pi = pair_matrix(ni, ni // 2)
    pj = pair_matrix(nj, nj // 2)
    dot = functools.partial(jnp.einsum, precision=HIGH)
    coarse = dot("pji,jJ,iI->pJI", rest, pj, pi)
    east1 = dot("ji,jJ,iI->JI", east, pj, pair_matrix(ni, ni // 2, odd_only=True))
    north1 = dot("ji,jJ,iI->JI", north, pair_matrix(nj, nj // 2, odd_only=True), pi)
    fix = coarse_cycle(coarse, east1, north1, level + 1)
    v = pre + dot("pJI,jJ,iI->pji", fix, pj, pi)
    v = relax_lead(v, source, east, north, shunt)
    return relax_lead(v, source, east, north, shunt)


def live_taps(taps, tap_current, rows, cols, row_start, col_start, all_cols):
    i = taps // all_cols - row_start
    j = taps % all_cols - col_start
    inside = (i >= -HALO) & (i < rows + HALO) & (j >= -HALO) & (j < cols + HALO)
    cand = lax.broadcasted_iota(jnp.int32, taps.shape, 0)
    code = ((i + HALO) * (cols + 2 * PAD) + j + PAD) * LANES + cand
    count = taps.size
    lead = count // LANES
    flags = inside.reshape(lead, LANES).astype(jnp.float32)
    upto = jnp.dot(flags, jnp.triu(jnp.ones((LANES, LANES), jnp.float32)), precision=HIGH)
    before = jnp.dot(
        jnp.tril(jnp.ones((lead, lead), jnp.float32), -1), upto[:, -1:], precision=HIGH
    )
    place = (upto + before).astype(jnp.int32).reshape(-1)
    place = jnp.where(inside.reshape(-1), place - 1, -1)
    pick = place[None, :] == jnp.arange(count, dtype=jnp.int32)[:, None]
    codes = jnp.sum(jnp.where(pick, code.reshape(-1)[None], 0), axis=1)
    amps = jnp.sum(jnp.where(pick, tap_current.reshape(-1)[None], 0.0), axis=1)
    return jnp.sum(inside.astype(jnp.int32)).reshape(1), codes, amps


def body(load, east_class, north_class, cond_table, taps, tap_current):
    rows, cols, cands = load.shape
    ng, nd_axis = lax.axis_size("grp"), lax.axis_size("dev")
    nd = ng * nd_axis
    pc = cands // nd
    row_start = lax.axis_index("grp") * rows
    col_start = lax.axis_index("dev") * cols
    all_rows, all_cols = ng * rows, nd_axis * cols
    edge = HALO + 1
    dims = (rows, cols, nd, pc)

    classes = jnp.stack([east_class.T, north_class.T]).astype(jnp.float32)
    strip_w = jnp.swapaxes(load[:, :HALO], 0, 1)
    strip_e = jnp.swapaxes(load[:, cols - HALO :], 0, 1)
    from_w, from_e = exchange(
        pack(strip_e, classes[:, cols - edge :]), pack(strip_w, classes[:, :edge]), "dev"
    )
    from_n, from_s = exchange(
        pack(load[rows - HALO :], classes[:, :, rows - edge :]),
        pack(load[:HALO], classes[:, :, :edge]),
        "grp",
    )
    west, west_class = unpack(from_w, strip_w, classes[:, :edge])
    east, east_class_x = unpack(from_e, strip_w, classes[:, :edge])
    north, north_class_x = unpack(from_n, load[:HALO], classes[:, :, :edge])
    south, south_class_x = unpack(from_s, load[:HALO], classes[:, :, :edge])

    def corner_load(first):
        return jnp.stack(
            [jnp.swapaxes(x[:, first : first + HALO], 0, 1) for x in (north, south)]
        )

    def corner_class(first):
        return jnp.stack([x[:, first : first + edge] for x in (north_class_x, south_class_x)])

    corner_w, corner_e = exchange(
        pack(corner_load(cols - HALO), corner_class(cols - edge)),
        pack(corner_load(0), corner_class(0)),
        "dev",
    )
    cw, cw_class = unpack(corner_w, corner_load(0), corner_class(0))
    ce, ce_class = unpack(corner_e, corner_load(0), corner_class(0))
    corners = jnp.stack([cw, ce]).reshape(2, 2, HALO * HALO, LANES)
    whole = jnp.concatenate(
        [
            jnp.concatenate([cw_class[0], north_class_x, ce_class[0]], axis=1),
            jnp.concatenate([west_class, classes, east_class_x], axis=1),
            jnp.concatenate([cw_class[1], south_class_x, ce_class[1]], axis=1),
        ],
        axis=2,
    )
    side = PAD - edge
    whole = jnp.pad(whole, ((0, 0), (side, side), (0, 0)))
    cond = jnp.zeros_like(whole)
    for k in range(cond_table.shape[0]):
        cond = jnp.where(whole == k, cond_table[k], cond)
    col_ids = (col_start - PAD + jnp.arange(cols + 2 * PAD))[:, None]
    row_ids = (row_start - edge + jnp.arange(rows + 2 * edge))[None]
    in_cols = (col_ids >= 0) & (col_ids < all_cols)
    in_rows = (row_ids >= 0) & (row_ids < all_rows)
    inside = in_cols & in_rows
    near = (jnp.abs(jnp.arange(cols + 2 * PAD) * 2 - (cols + 2 * PAD - 1)) < cols + 2 * edge)[:, None]
    inside = inside & near
    east0 = jnp.where(inside & (row_ids < all_rows - 1), cond[0], 0.0)
    north0 = jnp.where(inside & (col_ids < all_cols - 1), cond[1], 0.0)
    ext_rows = -(-(rows + 2 * HALO) // GROUP) * GROUP
    grow = ext_rows + 1 - (rows + 2 * edge)

    def fit(x):
        return jnp.pad(x, ((0, 0), (0, grow))) if grow >= 0 else x[:, :grow]

    coef0 = stencil_coefs(fit(east0), fit(north0), SHUNT_CONDUCT)

    half_rows, half_cols = rows // 2, cols // 2
    wide1 = half_cols + HALO - 2
    rows1 = -(-(half_rows + 16) // GROUP) * GROUP
    dot = functools.partial(jnp.dot, precision=HIGH)

    def lead(count, half, first, odd):
        return pair_matrix(count, half, first, odd)

    c_first = PAD - (HALO - 2)
    n0c, n0r = cols + 2 * PAD, rows + 2 * edge
    r_first = edge - 14
    sum_c = lead(n0c, wide1, c_first, False).T
    odd_c = lead(n0c, wide1, c_first, True).T
    sum_r = lead(n0r, rows1 + 1, r_first, False)
    odd_r = lead(n0r, rows1 + 1, r_first, True)
    east1 = dot(dot(sum_c, east0), odd_r)
    north1 = dot(dot(odd_c, north0), sum_r)
    coef1 = stencil_coefs(east1, north1, SHUNT_CONDUCT * 4.0)

    q_rows, q_cols = rows // 4, cols // 4
    east2 = dot(dot(pair_matrix(wide1, q_cols, 4).T, east1), pair_matrix(rows1 + 1, q_rows, 7, True))
    north2 = dot(
        dot(pair_matrix(wide1, q_cols, 4, True).T, north1), pair_matrix(rows1 + 1, q_rows, 7)
    )
    mine = jnp.stack([east2, north2]).reshape(1, -1, LANES)
    spread_out = jnp.broadcast_to(mine, (nd,) + mine.shape[1:])
    gathered = lax.all_to_all(spread_out, AXES, split_axis=0, concat_axis=0, tiled=True)
    cond2 = gathered.reshape(ng, nd_axis, 2, q_cols, q_rows)
    cond2 = cond2.transpose(2, 1, 3, 0, 4).reshape(2, nd_axis * q_cols, ng * q_rows)

    tap_count, tap_code, tap_amps = live_taps(
        taps, tap_current, rows, cols, row_start, col_start, all_cols
    )
    wide0 = cols + 2 * PAD
    s2_rows = rows1 // 2 * q_cols
    slab_rows = pc * q_rows * q_cols // LANES
    s0, p0, s1, p1, slab = pl.pallas_call(
        functools.partial(down_kernel, dims),
        out_shape=[
            shape(ext_rows, wide0, LANES),
            shape(ext_rows + 2, wide0, LANES),
            shape(rows1, wide1, LANES),
            shape(rows1 + 2, wide1, LANES),
            shape(nd * slab_rows, LANES),
        ],
        in_specs=[SMEM] * 3 + [VMEM] * 8,
        out_specs=[VMEM] * 5,
        scratch_shapes=[
            vmem(ext_rows + 2, wide0, LANES),
            vmem(rows1 + 2, wide1, LANES),
            vmem(s2_rows, LANES),
            vmem(GROUP // 2, wide0, LANES),
            vmem(GROUP // 2, wide1, LANES),
        ],
        compiler_params=PARAMS,
        name="fine_down",
    )(tap_count, tap_code, tap_amps, load, west, east, north, south, corners, coef0, coef1)

    got = lax.all_to_all(
        slab.reshape(nd, slab_rows, LANES), AXES, split_axis=0, concat_axis=0, tiled=True
    )
    per = LANES // q_rows
    source2 = got.reshape(ng, nd_axis, q_cols // per, pc, per, q_rows)
    source2 = source2.transpose(3, 1, 4, 2, 0, 5).reshape(pc, nd_axis * q_cols, ng * q_rows)

    fix = coarse_cycle(source2, cond2[0], cond2[1], 2)

    padded = jnp.pad(fix, ((0, 0), (2, 2), (2, LANES)))
    pieces = [
        padded[:, d * q_cols : d * q_cols + q_cols + 4, g * q_rows : g * q_rows + LANES]
        for g in range(ng)
        for d in range(nd_axis)
    ]
    back = jnp.stack(pieces).transpose(0, 2, 1, 3).reshape(nd, (q_cols + 4) * pc, LANES)
    back = lax.all_to_all(back, AXES, split_axis=0, concat_axis=0, tiled=True)
    pitch2 = -(-(q_cols + 4) // GROUP) * GROUP
    return pl.pallas_call(
        functools.partial(up_kernel, dims),
        out_shape=shape(rows, cols, LANES),
        in_specs=[VMEM] * 7,
        out_specs=VMEM,
        scratch_shapes=[
            vmem((q_rows + 4) * pitch2, LANES),
            vmem(rows1 + 2, wide1, LANES),
            vmem(rows1 + 2, wide1, LANES),
            vmem(2 * wide1, LANES),
            vmem(ext_rows + 2, 2 * wide1, LANES),
            vmem(ext_rows + 2, 2 * wide1, LANES),
        ],
        compiler_params=PARAMS,
        name="fine_up",
    )(back.reshape(-1, LANES), s0, p0, s1, p1, coef0, coef1)


def solution(mesh):
    return jax.shard_map(
        body,
        mesh=mesh,
        in_specs=(P("grp", "dev", None), P("grp", "dev"), P("grp", "dev"), P(), P(), P()),
        out_specs=P("grp", "dev", None),
        check_vma=False,
    )
```

time: 615 us -> 338 us (0.55); the launches traced: 606 us -> 337 us
  starting transfers between devices: 182 us -> 29 us
  Pallas kernels: 0 us -> 136 us
  waiting for transfers between devices: 92 us -> 2.35 us
  other arithmetic: 175 us -> 87.3 us
  local copies, waits for them, and re-layouts: 98.8 us -> 38.6 us
  blocking collectives: 46.4 us -> 27.1 us
    ppermute x66 -> x6, starting transfers between devices: 176 us -> 17.4 us  [exchange(): return (lax.ppermute(tail, axis, up), lax.ppermute(head, axis, down))]
    pallas_call x0 -> x2, Pallas kernels: none -> 136 us  [the longest x1 73.5 us: body(): pl.pallas_call(functools.partial(down_kernel, dims), out_shape=[shape(ext...]
    ppermute x66 -> x6, waiting for transfers between devices: 87.1 us -> 2.34 us  [exchange(): return (lax.ppermute(tail, axis, up), lax.ppermute(head, axis, down))]
    add x26 -> x19, other arithmetic: 56 us -> 4.35 us  [the longest x7 3.16 us: pair_matrix(): hit = fine == 2 * coarse + 1 if odd_only else fine // 2 == coarse]
    all_gather x3 -> x0, blocking collectives: 29.3 us -> none  [the longest x1 15.9 us: body(): conduct = lax.all_gather(conduct, 'dev', axis=2, tiled=True)]
    ppermute x6 -> x0, local copies, waits for them, and re-layouts: 15.2 us -> none  [the longest x3 8.6 us: with_halo(): lax.ppermute(head, axis, [((i + 1) % count, i) for i in range(ends)])]
    slice x48 -> x26, local copies, waits for them, and re-layouts: 27.9 us -> 12.9 us  [the longest x6 5.95 us: unpack(): return (packed[:count].reshape(rows.shape), flat.reshape(extra.shape))]
    sub x6 -> x4, other arithmetic: 16.9 us -> 2.3 us  [pair_matrix(): fine = jnp.arange(count)[:, None] - first]
  transfers between devices with their start and end apart: 67 -> 8, of which waited for: 34 -> 1; matrix products, arithmetic and copies ran while one was open for 18% -> 33% of each run, Pallas kernels for 0% -> 22%
where the time goes in v1:
time: 338 us; the launch traced here: 337 us
  Pallas kernels  136 us (40%)
  other arithmetic  87.3 us (26%)
  local copies, waits for them, and re-layouts  38.6 us (11%)
  starting transfers between devices  29 us (9%)
  blocking collectives  27.1 us (8%)
  matrix products  14.2 us (4%)
    pallas_call x1, Pallas kernels, body(): pl.pallas_call(functools.partial(down_kernel, dims), out_shape=[shape(ext...  73.5 us
    pallas_call x1, Pallas kernels, body(): pl.pallas_call(functools.partial(up_kernel, dims), out_shape=shape(rows,...  62.4 us
    another operation x7, other arithmetic, coarse_cycle(): factor = jnp.linalg.cholesky(matrix)  34.6 us
    all_to_all x1, blocking collectives, body(): back = lax.all_to_all(back, AXES, split_axis=0, concat_axis=0, tiled=True)  27.1 us
    another operation x3, other arithmetic, coarse_cycle(): jax.scipy.linalg.cho_solve((factor, True), source.reshape(count, size).T)  21.2 us
    ppermute x6, starting transfers between devices, exchange(): return (lax.ppermute(tail, axis, up), lax.ppermute(head, axis, down))  17.4 us
    unnamed x70, local copies, waits for them, and re-layouts  7.96 us
  transfers between devices with their start and end apart: 8, of which 1 were waited for; matrix products, arithmetic and copies ran while one was open for 33% of the time, Pallas kernels for 22%

profile of v1, /device:TPU:1, one launch (start us, length us, event | category | flops | bytes accessed | tf_op | source)
XLA Modules:
  0.0 336.5 jit_solution(18267153546848170285)
XLA Ops:
  0.0 0.8 add_convert_fusion
  1.0 1.0 fusion.338
  2.7 4.6 %collective-permute-start.2 = (f32[326,128]{1,0:T(8,128)}, f32[326,128]{1,0:T(8,128)}, u32[]{:S(2)}, u32[]{:S(2)}) collective-permute-start(f32[326,128]{1,0:T(8,128)} %pad_maximum_fusion.3), channel_id=1, source_target_pairs={{0,8},{8,16},{16,24},{1,9},{9,17},{17,25},{2,10},{10,18},{18,26},{... | collective-permute-start | bytes 500744 | tf_op jit(solution)/shard_map/ppermute | solution.py:27
  8.1 1.3 collective-permute-start.3
  9.4 4.0 %fusion.339 = (f32[256,10,128]{2,1,0:T(8,128)S(1)}, f32[256,10,128]{2,1,0:T(8,128)}) fusion(f32[256,32,128]{2,1,0:T(8,128)} %own.1), kind=kLoop, calls=%fused_computation.627 | loop fusion | bytes 5242880 | tf_op jit(solution)/shard_map/slice | solution.py:371
  13.4 2.0 copy.74
  15.4 1.2 pad_maximum_fusion
  16.6 4.0 %collective-permute-start = (f32[2604,128]{1,0:T(8,128)}, f32[2604,128]{1,0:T(8,128)S(1)}, u32[]{:S(2)}, u32[]{:S(2)}) collective-permute-start(f32[2604,128]{1,0:T(8,128)} %pad_maximum_fusion), channel_id=1, source_target_pairs={{0,1},{1,2},{2,3},{3,4},{4,5},{5,6},{6,7},{8,9},{9,10},{10,11},{11... | collective-permute-start | bytes 3999752 | tf_op jit(solution)/shard_map/ppermute | solution.py:27
  21.1 1.2 pad_maximum_fusion.1
  22.3 1.9 collective-permute-start.1
  36.7 2.4 select_reduce_fusion.1.tap_code
  39.1 2.3 select_reduce_fusion.tap_amps
  43.5 0.9 slice.732
  46.3 0.9 slice.734
  47.2 1.0 pad_maximum_fusion.5
  48.9 0.9 reshape.666
  50.5 3.6 %collective-permute-start.4 = (f32[204,128]{1,0:T(8,128)}, f32[204,128]{1,0:T(8,128)}, u32[]{:S(2)}, u32[]{:S(2)}) collective-permute-start(f32[204,128]{1,0:T(8,128)} %pad_maximum_fusion.7), channel_id=1, source_target_pairs={{0,1},{1,2},{2,3},{3,4},{4,5},{5,6},{6,7},{8,9},{9,10},{10,11},{11... | collective-permute-start | bytes 313352 | tf_op jit(solution)/shard_map/ppermute | solution.py:27
  54.3 1.9 collective-permute-start.5
  57.0 0.9 slice.741
  58.1 2.3 collective-permute-done.5
  60.4 0.9 slice.746
  63.0 5.2 %select_select_fusion.1 = f32[2,64,278]{2,1,0:T(8,128)S(1)} fusion(f32[2,11,11]{2,1,0:T(8,128)S(1)} %slice.603, f32[2,32,11]{2,1,0:T(8,128)S(1)} %reshape.670, f32[2,11,11]{2,1,0:T(8,128)S(1)} %slice.601, f32[2,11,256]{2,1,0:T(8,128)S(1)} %reshape_reshape.7, f32[2,32,256]{2,1,0:T(8,128)S(1)} %add_convert_fusion, f32[2,11,256]{2,1,0:T(8,128)S(1)} %reshape_reshape.6, ...), kind=kLoop, calls=%fused_computation.153 | loop fusion | flops 1281024 | bytes 262464 | tf_op jit(solution)/shard_map/jit(_where)/select_n | solution.py:414
  68.2 0.8 fusion.74
  69.1 0.9 fusion.246
  70.1 1.0 fusion.3
  71.1 0.7 bitcast_dynamic-update-slice_fusion.6
  71.9 0.9 fusion.245
  72.7 1.0 fusion.4
  73.8 0.9 fusion.277
  74.7 0.9 fusion.278
  75.7 0.8 convolution_bitcast_fusion.6
  76.5 0.9 convolution_bitcast_fusion.7
  78.1 5.8 %all-to-all-start.1 = ((f32[32,8,128]{2,1,0:T(8,128)}), f32[32,8,128]{2,1,0:T(8,128)S(1)}, u32[]{:S(2)}, u32[]{:S(2)}) async-start(f32[32,8,128]{2,1,0:T(8,128)} %broadcast_in_dim.290), calls=%async_computation.1 | async-start | bytes 262144 | tf_op jit(solution)/shard_map/all_to_all | solution.py:458
  86.2 0.8 bitcast_dynamic-update-slice_fusion.2
  87.6 1.1 slice.728
  88.7 1.1 slice.730
  90.5 0.9 bitcast_bitcast_fusion.coef0
  91.4 73.5 %fine_down.1 = (f32[280,64,128]{2,1,0:T(8,128)}, f32[282,64,128]{2,1,0:T(8,128)}, f32[144,24,128]{2,1,0:T(8,128)}, f32[146,24,128]{2,1,0:T(8,128)}, f32[512,128]{1,0:T(8,128)}) custom-call(s32[1]{0:T(128)} %bitcast.tap_count, s32[2048]{0:T(1024)} %select_reduce_fusion.1.tap_code, f32[2048]{0:T(1024)} %select_reduce_fusion.tap_amps, f32[256,32,128]{2,1,0:T(8,128)} %own.1, ...), custom_call_target="tpu_custom_call" | custom-call | tf_op jit(solution)/shard_map/fine_down/pallas_call | solution.py:468
  165.0 5.8 %all-to-all-start = ((f32[32,16,128]{2,1,0:T(8,128)}), f32[32,16,128]{2,1,0:T(8,128)S(1)}, u32[]{:S(2)}, u32[]{:S(2)}) async-start(f32[32,16,128]{2,1,0:T(8,128)} %bitcast.386), calls=%async_computation | async-start | bytes 524288 | tf_op jit(solution)/shard_map/all_to_all | solution.py:490
  174.3 11.7 %cholesky.44 = f32[128,128]{1,0:T(8,128)S(1)} custom-call(f32[128,128]{1,0:T(8,128)S(1)} %cholesky.104), custom_call_target="Cholesky" | custom-call | tf_op jit(solution)/shard_map/jit(cholesky)/cholesky | solution.py:320
  186.7 9.8 %custom-call.18 = f32[1,128,128]{1,2,0:T(8,128)S(1)} custom-call(f32[1,128,128]{2,1,0:T(8,128)S(1)} %get-tuple-element.54), custom_call_target="InvertDiagBlocksLowerTriangular" | custom-call | tf_op jit(solution)/shard_map/jit(cholesky)/cholesky | solution.py:320
  197.0 11.7 %cholesky.92 = f32[128,128]{1,0:T(8,128)S(1)} custom-call(f32[128,128]{1,0:T(8,128)S(1)} %convolution_subtract_fusion), custom_call_target="Cholesky" | custom-call | tf_op jit(solution)/shard_map/jit(cholesky)/cholesky | solution.py:320
  210.8 5.3 %while.1 = (s32[]{:T(128)}, f32[256,256]{1,0:T(8,128)S(1)}, s32[2,2]{1,0:T(2,128)S(1)}, f32[2,128,128]{2,1,0:T(8,128)}, s32[]{:T(128)}) while((s32[]{:T(128)}, f32[256,256]{1,0:T(8,128)S(1)}, s32[2,2]{1,0:T(2,128)S(1)}, f32[2,128,128]{2,1,0:T(8,128)}, s32[]{:T(128)}) %tuple.60), condition=%wide.while_cond, body=%wide.while_body.sunk | while | flops 2 | bytes 132205 | solution.py:321
  211.4 2.0 bitcast_dynamic-update-slice_fusion.8
  214.1 2.0 bitcast_dynamic-update-slice_fusion.8
  216.2 20.6 %custom-call.19 = f32[2,128,128]{1,2,0:T(8,128)S(1)} custom-call(f32[2,128,128]{2,1,0:T(8,128)} %get-tuple-element.22), custom_call_target="InvertDiagBlocksLowerTriangular" | custom-call | tf_op jit(solution)/shard_map/jit(_cho_solve)/triangular_solve | solution.py:321
  247.0 27.1 %all_to_all.15 = f32[32,48,128]{2,1,0:T(8,128)} all-to-all(f32[32,48,128]{2,1,0:T(8,128)S(1)} %copy.73), channel_id=1, replica_groups=mesh['grp'=4,'dev'=8] {'grp','dev'}, dimensions={0} | all-to-all | bytes 1572864 | tf_op jit(solution)/shard_map/all_to_all | solution.py:506
  274.1 62.4 %fine_up.1 = f32[256,32,128]{2,1,0:T(8,128)} custom-call(f32[1536,128]{1,0:T(8,128)} %bitcast.375, f32[280,64,128]{2,1,0:T(8,128)} %get-tuple-element.11.s0, f32[282,64,128]{2,1,0:T(8,128)} %get-tuple-element.12.p0, f32[144,24,128]{2,1,0:T(8,128)} %get-tuple-element.13.s1, f32[146,24,128]{2,1,0:T(8,128)} %get-tuple-element.14.p1, ...), custom_call_target="tpu_custom_call" | custom-call | tf_op jit(solution)/shard_map/fine_up/pallas_call | solution.py:508
  (246 shorter events, 43.8 us)
Async XLA Ops:
  2.7 40.0 %collective-permute-start.2 = (f32[326,128]{1,0:T(8,128)}, f32[326,128]{1,0:T(8,128)}, u32[]{:S(2)}, u32[]{:S(2)}) collective-permute-start(f32[326,128]{1,0:T(8,128)} %pad_maximum_fusion.3), channel_id=1, source_target_pairs={{0,8},{8,16},{16,24},{1,9},{9,17},{17,25},{2,10},{10,18},{18,26},{... | collective-permute-start | bytes 500744 | tf_op jit(solution)/shard_map/ppermute | solution.py:27
  8.1 37.0 %collective-permute-start.3 = (f32[326,128]{1,0:T(8,128)}, f32[326,128]{1,0:T(8,128)}, u32[]{:S(2)}, u32[]{:S(2)}) collective-permute-start(f32[326,128]{1,0:T(8,128)} %pad_maximum_fusion.4), channel_id=1, source_target_pairs={{8,0},{16,8},{24,16},{9,1},{17,9},{25,17},{10,2},{18,10},{26,18},{... | collective-permute-start | bytes 500744 | tf_op jit(solution)/shard_map/ppermute | solution.py:27
  16.6 46.4 %collective-permute-start = (f32[2604,128]{1,0:T(8,128)}, f32[2604,128]{1,0:T(8,128)S(1)}, u32[]{:S(2)}, u32[]{:S(2)}) collective-permute-start(f32[2604,128]{1,0:T(8,128)} %pad_maximum_fusion), channel_id=1, source_target_pairs={{0,1},{1,2},{2,3},{3,4},{4,5},{5,6},{6,7},{8,9},{9,10},{10,11},{11... | collective-permute-start | bytes 3999752 | tf_op jit(solution)/shard_map/ppermute | solution.py:27
  21.1 12.4 %copy-start.5 = (s32[128,16]{0,1:T(8,128)S(1)}, s32[128,16]{0,1:T(8,128)}, u32[]{:S(2)}) copy-start(s32[128,16]{0,1:T(8,128)} %param.10) | copy-start | bytes 24580
  21.1 15.2 %copy-start.4 = (f32[128,16]{0,1:T(8,128)S(1)}, f32[128,16]{0,1:T(8,128)}, u32[]{:S(2)}) copy-start(f32[128,16]{0,1:T(8,128)} %param.11) | copy-start | bytes 24580
  21.1 20.9 %copy-start.3 = (f32[8]{0:T(128)S(1)}, f32[8]{0:T(128)}, u32[]{:S(2)}) copy-start(f32[8]{0:T(128)} %param.9) | copy-start | bytes 100
  22.3 40.7 %collective-permute-start.1 = (f32[2604,128]{1,0:T(8,128)}, f32[2604,128]{1,0:T(8,128)S(1)}, u32[]{:S(2)}, u32[]{:S(2)}) collective-permute-start(f32[2604,128]{1,0:T(8,128)} %pad_maximum_fusion.1), channel_id=1, source_target_pairs={{1,0},{2,1},{3,2},{4,3},{5,4},{6,5},{7,6},{9,8},{10,9},{11,10},{12... | collective-permute-start | bytes 3999752 | tf_op jit(solution)/shard_map/ppermute | solution.py:27
  44.4 16.9 %copy-start = (f32[320,128]{1,0:T(8,128)}, f32[320,128]{1,0:T(8,128)S(1)}, u32[]{:S(2)}) copy-start(f32[320,128]{1,0:T(8,128)S(1)} %slice.732) | copy-start | bytes 491524
  47.2 15.8 %copy-start.1 = (f32[320,128]{1,0:T(8,128)}, f32[320,128]{1,0:T(8,128)S(1)}, u32[]{:S(2)}) copy-start(f32[320,128]{1,0:T(8,128)S(1)} %slice.734) | copy-start | bytes 491524
  50.5 5.7 %collective-permute-start.4 = (f32[204,128]{1,0:T(8,128)}, f32[204,128]{1,0:T(8,128)}, u32[]{:S(2)}, u32[]{:S(2)}) collective-permute-start(f32[204,128]{1,0:T(8,128)} %pad_maximum_fusion.7), channel_id=1, source_target_pairs={{0,1},{1,2},{2,3},{3,4},{4,5},{5,6},{6,7},{8,9},{9,10},{10,11},{11... | collective-permute-start | bytes 313352 | tf_op jit(solution)/shard_map/ppermute | solution.py:27
  54.3 6.1 %collective-permute-start.5 = (f32[204,128]{1,0:T(8,128)S(1)}, f32[204,128]{1,0:T(8,128)}, u32[]{:S(2)}, u32[]{:S(2)}) collective-permute-start(f32[204,128]{1,0:T(8,128)S(1)} %pad_maximum_fusion.8), channel_id=1, source_target_pairs={{1,0},{2,1},{3,2},{4,3},{5,4},{6,5},{7,6},{9,8},{10,9},{11,10},{12... | collective-permute-start | bytes 313352 | tf_op jit(solution)/shard_map/ppermute | solution.py:27
  78.1 86.8 %all-to-all-start.1 = ((f32[32,8,128]{2,1,0:T(8,128)}), f32[32,8,128]{2,1,0:T(8,128)S(1)}, u32[]{:S(2)}, u32[]{:S(2)}) async-start(f32[32,8,128]{2,1,0:T(8,128)} %broadcast_in_dim.290), calls=%async_computation.1 | async-start | bytes 262144 | tf_op jit(solution)/shard_map/all_to_all | solution.py:458
  88.7 1.8 copy-start.2
  91.4 79.9 %copy-start.6 = (s32[128]{0:T(128)S(1)}, s32[128]{0:T(128)}, u32[]{:S(2)}) copy-start(s32[128]{0:T(128)} %multiply_add_fusion.3) | copy-start | bytes 1540
  91.4 80.2 %copy-start.11 = (s32[64]{0:T(128)S(1)}, s32[64]{0:T(128)}, u32[]{:S(2)}) copy-start(s32[64]{0:T(128)} %fusion.324) | copy-start | bytes 772
  164.9 7.6 %copy-start.13 = (s32[256]{0:T(256)S(1)}, s32[256]{0:T(256)}, u32[]{:S(2)}) copy-start(s32[256]{0:T(256)} %and_select_fusion.4) | copy-start | bytes 3076
  164.9 7.9 %copy-start.10 = (s32[16]{0:T(128)S(1)}, s32[16]{0:T(128)}, u32[]{:S(2)}) copy-start(s32[16]{0:T(128)} %multiply_add_fusion.1) | copy-start | bytes 196
  164.9 8.1 %copy-start.7 = (s32[128]{0:T(128)S(1)}, s32[128]{0:T(128)}, u32[]{:S(2)}) copy-start(s32[128]{0:T(128)} %and_select_fusion.2) | copy-start | bytes 1540
  164.9 8.2 %copy-start.9 = (s32[8]{0:T(128)S(1)}, s32[8]{0:T(128)}, u32[]{:S(2)}) copy-start(s32[8]{0:T(128)} %multiply_add_fusion.4) | copy-start | bytes 100
  165.0 8.9 %copy-start.8 = (pred[256]{0:T(512)(128)(4,1)S(1)}, pred[256]{0:T(512)(128)(4,1)}, u32[]{:S(2)}) copy-start(pred[256]{0:T(512)(128)(4,1)} %constant.344.clone.1) | copy-start | bytes 772
  165.0 72.0 %all-to-all-start = ((f32[32,16,128]{2,1,0:T(8,128)}), f32[32,16,128]{2,1,0:T(8,128)S(1)}, u32[]{:S(2)}, u32[]{:S(2)}) async-start(f32[32,16,128]{2,1,0:T(8,128)} %bitcast.386), calls=%async_computation | async-start | bytes 524288 | tf_op jit(solution)/shard_map/all_to_all | solution.py:490
  170.8 39.9 %copy-start.12 = (s32[2]{0:T(128)S(1)}, s32[2]{0:T(128)}, u32[]{:S(2)}) copy-start(s32[2]{0:T(128)} %iota_multiply_fusion) | copy-start | bytes 28

commit v2 on v1

v2 whole, which is shorter than its diff:
```python
import functools

import jax
import jax.numpy as jnp
from jax import lax
from jax.experimental import pallas as pl
from jax.experimental.pallas import tpu as pltpu
from jax.sharding import PartitionSpec as P

LEVELS = 5
RELAXATION = 0.8
KEEP = 1.0 - RELAXATION
SHUNT_CONDUCT = 0.01
AXES = ("grp", "dev")
HIGH = lax.Precision.HIGHEST

HALO = 10
PAD = 12
ROW_PAD = 16
LANES = 128
GROUP = 8


def exchange(tail, head, axis):
    count = lax.axis_size(axis)
    up = [(i, i + 1) for i in range(count - 1)]
    down = [(i + 1, i) for i in range(count - 1)]
    return lax.ppermute(tail, axis, up), lax.ppermute(head, axis, down)


def pack(rows, extra):
    flat = extra.reshape(-1)
    size = -flat.shape[0] % LANES
    return jnp.concatenate([rows.reshape(-1, LANES), jnp.pad(flat, (0, size)).reshape(-1, LANES)])


def unpack(packed, rows, extra):
    count = rows.size // LANES
    flat = packed[count:].reshape(-1)[: extra.size]
    return packed[:count].reshape(rows.shape), flat.reshape(extra.shape)


def pair_matrix(count, half, first=0, odd_only=False):
    fine = jnp.arange(count)[:, None] - first
    coarse = jnp.arange(half)[None, :]
    hit = fine == 2 * coarse + 1 if odd_only else fine // 2 == coarse
    return hit.astype(jnp.float32)


def stencil_coefs(east, north, shunt):
    west = east[:, :-1]
    east = east[:, 1:]
    north = north[:, 1:]
    south = jnp.pad(north, ((1, 0), (0, 0)))[:-1]
    diag = shunt + east + west + north + south
    coefs = jnp.stack([east, north, RELAXATION / diag])
    rows = coefs.shape[2]
    tiles = -(-rows // LANES)
    coefs = jnp.pad(coefs, ((0, 0), (0, 0), (0, tiles * LANES - rows)))
    return jnp.moveaxis(coefs.reshape(3, coefs.shape[1], tiles, LANES), 2, 1)


RING = 4 * GROUP


def wave(groups, stop, width, coef, coef_first, shunt, rings, fill, source, middle, finish):
    ring_e, ring_n, ring_w, ring_a, ring_b, flux_b, again_b, flux_c, turn = rings
    low, high = groups
    per_tile = LANES // GROUP
    for ref in rings:
        ref[...] = jnp.zeros_like(ref)

    def at(ref, row, ahead=0):
        base = pl.multiple_of(lax.rem(row, RING) * width, GROUP)
        return ref[pl.ds(base + ahead, width), :]

    def put(ref, row, value):
        base = pl.multiple_of(lax.rem(row, RING) * width, GROUP)
        ref[pl.ds(base, width), :] = value

    def balance(ring, row, before, slot):
        here = at(ring, row)
        east = at(ring_e, row) * (at(ring, row + 1) - here)
        north = at(ring_n, row) * (at(ring, row, 1) - here)
        turn[slot, pl.ds(GROUP, width), :] = north
        south = turn[slot, pl.ds(GROUP - 1, width), :]
        total = (east - before) + (north - south) + (source(row) - shunt * here)
        return here, east, total

    def go(t, carry):
        g = jnp.minimum(t, high - 1)
        shift = lax.rem(LANES - lax.rem(g, per_tile) * GROUP, LANES)
        found = [
            pltpu.roll(coef[k, g // per_tile, pl.ds(coef_first, width), :], shift, 1)
            for k in range(3)
        ]
        for r in range(GROUP):
            row = g * GROUP + r
            east, north, weight = (
                jnp.broadcast_to(x[:, r : r + 1], (width, LANES)) for x in found
            )
            put(ring_e, row, east)
            put(ring_n, row, north)
            put(ring_w, row, weight)
            put(ring_a, row, fill(r, row, weight))
        g = jnp.clip(t - 1, low, high - 1)
        flux = jnp.where(t > high, again_b[...], flux_b[...])
        again_b[...] = flux
        for r in range(GROUP):
            row = g * GROUP + r
            here, flux, total = balance(ring_a, row, flux, r)
            value = here + at(ring_w, row) * total
            put(ring_b, row, value)
            middle(row, value)
        flux_b[...] = flux
        g = jnp.clip(t - 2, low, high - 1)
        flux = flux_c[...]
        for r in range(GROUP):
            row = g * GROUP + r
            here, flux, total = balance(ring_b, row, flux, GROUP + r)
            finish(g, r, row, here, total, lambda row=row: at(ring_w, row))
        flux_c[...] = flux
        return carry

    lax.fori_loop(low, stop + 2, go, 0)


def rings_for(width):
    ring = vmem(RING * width + GROUP, LANES)
    return [ring] * 5 + [vmem(width, LANES)] * 3 + [vmem(2 * GROUP, width + GROUP, LANES)]


def down_kernel(
    dims, shunts, tap_count, tap_code, tap_amps, own, west, east, north, south, corners,
    coef0, coef1, s0, p0, s1, p1, slab, s2, pair, pair1, *rings,
):
    rows, cols, nd, pc = dims
    wide = cols + 2 * PAD
    ext = s0.shape[0] // wide
    rings0, rings1 = rings[:9], rings[9:]

    s0[...] = jnp.zeros_like(s0)
    first = ROW_PAD - HALO

    def copy_own(i, carry):
        s0[pl.ds((i + ROW_PAD) * wide + PAD, cols), :] = -own[i]
        return carry

    lax.fori_loop(0, rows, copy_own, 0, unroll=8)
    for i in range(HALO):
        s0[pl.ds((first + i) * wide + PAD, cols), :] = -north[i]
        s0[pl.ds((ROW_PAD + rows + i) * wide + PAD, cols), :] = -south[i]
    for j in range(HALO):
        for side, (strip, col) in enumerate(((west, PAD - HALO), (east, PAD + cols))):
            s0[pl.ds(ROW_PAD * wide + col + j, rows, stride=wide), :] = -strip[j]
            for end, base in enumerate((first, ROW_PAD + rows)):
                block = corners[side, end, j * HALO : (j + 1) * HALO, :]
                s0[pl.ds(base * wide + col + j, HALO, stride=wide), :] = -block

    lane = lax.broadcasted_iota(jnp.int32, (GROUP, LANES), 1)
    sub = lax.broadcasted_iota(jnp.int32, (GROUP, LANES), 0)

    def add_tap(k, carry):
        code = tap_code[k]
        node = code // LANES
        base = pl.multiple_of(node // GROUP * GROUP, GROUP)
        hit = (lane == lax.rem(code, LANES)) & (sub == node - base)
        s0[pl.ds(base, GROUP), :] += jnp.where(hit, tap_amps[k], 0.0)
        return carry

    lax.fori_loop(0, tap_count[0], add_tap, 0)

    def smooth_and_restrict(source, pre, coef, shunt, pair, rings, store):
        width = pair.shape[1]
        held = []

        def row_of(ref, row):
            return ref[pl.ds(pl.multiple_of(row * width, GROUP), width), :]

        def middle(row, value):
            pre[pl.ds(pl.multiple_of(row * width, GROUP), width), :] = value

        def finish(g, r, row, here, total, weight):
            if r % 2 == 0:
                held.append(total)
            else:
                pair[r // 2] = held.pop() + total
                store(g * (GROUP // 2) + r // 2, r // 2)

        groups = source.shape[0] // width // GROUP
        wave(
            (0, groups), groups - 1, width, coef, 0, shunt, rings,
            lambda r, row, weight: weight * row_of(source, row),
            lambda row: row_of(source, row), middle, finish,
        )

    half = pair1.shape[1]
    start = PAD - (HALO - 2)

    def store1(k, m):
        s1[pl.ds(pl.multiple_of(k * half, GROUP), half), :] = (
            pair[m, pl.ds(start, half, stride=2), :] + pair[m, pl.ds(start + 1, half, stride=2), :]
        )

    smooth_and_restrict(s0, p0, coef0, shunts[0], pair, rings0, store1)
    quarter = cols // 4

    def store2(k, m):
        s2[pl.ds(pl.multiple_of(k * quarter, quarter), quarter), :] = (
            pair1[m, pl.ds(4, quarter, stride=2), :] + pair1[m, pl.ds(5, quarter, stride=2), :]
        )

    smooth_and_restrict(s1, p1, coef1, shunts[1], pair1, rings1, store2)
    rows2 = rows // 4
    per = LANES // rows2
    groups = quarter // per
    for jp in range(groups):
        parts = [
            s2[pl.ds(ROW_PAD // 4 * quarter + jl * groups + jp, rows2, stride=quarter), :]
            for jl in range(per)
        ]
        turned = jnp.concatenate(parts, axis=0).T
        for p in range(pc):
            slab[pl.ds(jp * pc + p, nd, stride=groups * pc), :] = turned[p * nd : (p + 1) * nd]


def up_kernel(dims, shunts, back, s0, p0, s1, p1, coef0, coef1, out, x2, c1, twice1, twice0, *rings):
    rows, cols, nd, pc = dims
    wide = cols + 2 * PAD
    quarter = cols // 4
    wide2 = quarter + 4
    width1 = 2 * wide2
    width0 = 2 * width1
    rows2 = rows // 4 + 4
    pitch2 = x2.shape[0] // rows2
    rings0, rings1 = rings[:9], rings[9:]
    for jw in range(wide2):
        parts = [back[pl.ds(jw * pc + p, nd, stride=wide2 * pc), :] for p in range(pc)]
        turned = jnp.concatenate(parts, axis=0).T
        x2[pl.ds(jw, rows2, stride=pitch2), :] = turned[:rows2]

    def lifted(twice, slot, x):
        count = x.shape[0]
        twice[slot, pl.ds(0, count, stride=2), :] = x
        twice[slot, pl.ds(1, count, stride=2), :] = x
        return twice[slot]

    def fill1(r, row, weight):
        k = jnp.clip(row // 2 - 2, 0, rows2 - 1)
        x = x2[pl.ds(pl.multiple_of(k * pitch2, GROUP), pitch2), :][:wide2]
        return p1[pl.ds(pl.multiple_of(row * width1, GROUP), width1), :] + lifted(
            twice1, r, x
        )

    def source1(row):
        return s1[pl.ds(pl.multiple_of(row * width1, GROUP), width1), :]

    def finish1(g, r, row, here, total, weight):
        c1[pl.ds(pl.multiple_of(row * width1, GROUP), width1), :] = here + weight() * total

    groups1 = s1.shape[0] // width1 // GROUP
    wave(
        (0, groups1), groups1, width1, coef1, 0, shunts[1], rings1,
        fill1, source1, lambda row, value: None, finish1,
    )

    start = PAD - (HALO - 2)

    def fill0(r, row, weight):
        x = c1[pl.ds(pl.multiple_of(row // 2 * width1, GROUP), width1), :]
        return p0[pl.ds(row * wide + start, width0), :] + lifted(twice0, r, x)

    def source0(row):
        return s0[pl.ds(row * wide + start, width0), :]

    first, last = ROW_PAD // GROUP, (ROW_PAD + rows) // GROUP

    def finish0(g, r, row, here, total, weight):
        done = here + weight() * total
        row = jnp.clip(row - ROW_PAD, r, rows - GROUP + r)
        out[row] = done[HALO - 2 : HALO - 2 + cols]

    wave(
        (first - 1, last + 1), last, width0, coef0, start, shunts[0], rings0,
        fill0, source0, lambda row, value: None, finish0,
    )


VMEM = pl.BlockSpec(memory_space=pltpu.VMEM)
SMEM = pl.BlockSpec(memory_space=pltpu.SMEM)
PARAMS = pltpu.CompilerParams(vmem_limit_bytes=40 * 2**20)


SMALL = pltpu.CompilerParams(vmem_limit_bytes=16 * 2**20)


def shape(*dims):
    return jax.ShapeDtypeStruct(dims, jnp.float32)


def vmem(*dims):
    return pltpu.VMEM(dims, jnp.float32)


def lane_chunks(x):
    return [x[:, i : i + LANES] for i in range(0, x.shape[1], LANES)]


def block_column(x, k):
    size = x.shape[0]
    lane = lax.broadcasted_iota(jnp.int32, (size, LANES), 1)
    at = lane // size * size + k
    take = functools.partial(jnp.take_along_axis, axis=1, mode="promise_in_bounds")
    return jnp.concatenate([take(c, at) for c in lane_chunks(x)], axis=1)


def block_rows(held, x):
    held[...] = x

    def row(k):
        return jnp.broadcast_to(held[pl.ds(k, 1), :], x.shape)

    return row


def over(size, step, start):
    return lax.fori_loop(0, size, step, start, unroll=size <= GROUP)


def block_product(held, x, *others):
    rows = [block_rows(h, y) for h, y in zip(held, others)]

    def step(k, totals):
        column = block_column(x, k)
        return tuple(t + column * row(k) for t, row in zip(totals, rows))

    return over(x.shape[0], step, tuple(jnp.zeros_like(x) for _ in others))


def block_inverse(held, x):
    size, count = x.shape
    inner = lax.broadcasted_iota(jnp.int32, x.shape, 1) % size
    row_id = lax.broadcasted_iota(jnp.int32, x.shape, 0)

    def step(k, x):
        row = block_rows(held[0], x)(k)
        column = block_column(x, k)
        pivot = block_rows(held[1], column)(k)
        scaled = jnp.where(inner == k, 1.0, row) / pivot
        rest = jnp.where(inner == k, 0.0, x) - column * scaled
        return jnp.where(row_id == k, scaled, rest)

    return over(size, step, x)


def ahead(x, blocks):
    lanes = x.shape[1]
    return pltpu.roll(x, (-blocks * x.shape[0]) % lanes, 1)


def factor_kernel(diag, right, parts, last, *held):
    size, count = diag.shape
    d, c, ct = diag[...], right[...], right[...]
    stride = 1
    level = 0
    while stride * size < count:
        inverse = block_inverse(held, d)
        (r,) = block_product(held, c, ahead(inverse, stride))
        (lx,) = block_product(held, ct, inverse)
        left, lead = ahead(lx, -stride), ahead(lx, stride)
        for i, part in enumerate((r, left, inverse, c, ahead(ct, -stride))):
            parts[level, i] = part
        first, new_c = block_product(held, r, ct, ahead(c, stride))
        (second,) = block_product(held, left, ahead(c, -stride))
        (new_ct,) = block_product(held, lead, ct)
        d = d - first - second
        c, ct = -new_c, -new_ct
        stride *= 2
        level += 1
    last[...] = block_inverse(held, d)


def solve_kernel(source, parts, last, out, *held):
    size, count = source.shape
    block = lax.broadcasted_iota(jnp.int32, source.shape, 1) // size
    f = source[...]
    levels = parts.shape[0]
    for level in range(levels):
        s = 2**level
        (a,) = block_product(held, parts[level, 0], ahead(f, s))
        (b,) = block_product(held, parts[level, 1], ahead(f, -s))
        f = jnp.where(block % (2 * s) == 0, f - a - b, f)
    (x,) = block_product(held, last[...], f)
    for level in reversed(range(levels)):
        s = 2**level
        (a,) = block_product(held, parts[level, 3], ahead(x, s))
        (b,) = block_product(held, parts[level, 4], ahead(x, -s))
        (new,) = block_product(held, parts[level, 2], f - a - b)
        x = jnp.where(block % (2 * s) == s, new, x)
    out[...] = x


def coarse_factor(east, north, shunt):
    size, blocks = east.shape
    west = jnp.pad(east, ((0, 0), (1, 0)))[:, :-1]
    south = jnp.pad(north, ((1, 0), (0, 0)))[:-1]
    diag = shunt + east + west + north + south
    row, col = jnp.arange(size)[:, None, None], jnp.arange(size)[None, None, :]
    flat = (size, blocks * size)
    main = jnp.where(row == col, diag[:, :, None], 0.0)
    main = main - jnp.where(col == row + 1, north[:, :, None], 0.0)
    main = (main - jnp.where(col == row - 1, south[:, :, None], 0.0)).reshape(flat)
    right = jnp.where(row == col, -east[:, :, None], 0.0).reshape(flat)
    levels = blocks.bit_length() - 1
    return pl.pallas_call(
        factor_kernel,
        out_shape=[shape(levels, 5, *flat), shape(*flat)],
        in_specs=[VMEM] * 2,
        out_specs=[VMEM] * 2,
        scratch_shapes=[vmem(*flat)] * 2,
        compiler_params=SMALL,
        name="coarse_factor",
    )(main, right)


def coarse_solve(source, factor):
    cands, size, blocks = source.shape
    flat = (size, blocks * size)
    laid = jnp.pad(source.transpose(1, 2, 0), ((0, 0), (0, 0), (0, size - cands))).reshape(flat)
    solved = pl.pallas_call(
        solve_kernel,
        out_shape=shape(*flat),
        in_specs=[VMEM] * 3,
        out_specs=VMEM,
        scratch_shapes=[vmem(*flat)] * 2,
        compiler_params=SMALL,
        name="coarse_solve",
    )(laid, *factor)
    return solved.reshape(size, blocks, size)[:, :, :cands].transpose(2, 0, 1)


def operate_lead(v, east, north, shunt):
    padded = jnp.pad(v, ((0, 0), (1, 1), (1, 1)))
    west = jnp.pad(east, ((0, 0), (1, 0)))[:, :-1]
    south = jnp.pad(north, ((1, 0), (0, 0)))[:-1]
    diag = shunt + east + west + north + south
    applied = (
        diag * v
        - east * padded[:, 1:-1, 2:]
        - west * padded[:, 1:-1, :-2]
        - north * padded[:, 2:, 1:-1]
        - south * padded[:, :-2, 1:-1]
    )
    return applied, diag


def relax_lead(v, source, east, north, shunt):
    applied, diag = operate_lead(v, east, north, shunt)
    return v + RELAXATION * (source - applied) / diag


def coarse_levels(east, north, level):
    dot = functools.partial(jnp.dot, precision=HIGH)
    levels = []
    while level < LEVELS:
        nj, ni = east.shape
        levels.append((east, north))
        pi, pj = pair_matrix(ni, ni // 2), pair_matrix(nj, nj // 2)
        odd_i = pair_matrix(ni, ni // 2, odd_only=True)
        odd_j = pair_matrix(nj, nj // 2, odd_only=True)
        east, north = dot(pj.T, dot(east, odd_i)), dot(odd_j.T, dot(north, pi))
        level += 1
    return levels, coarse_factor(east, north, SHUNT_CONDUCT * 4.0**LEVELS)


def coarse_cycle(source, levels, factor, level):
    if level == LEVELS:
        return coarse_solve(source, factor)
    shunt = SHUNT_CONDUCT * 4.0**level
    east, north = levels[0]
    count, nj, ni = source.shape
    _, diag = operate_lead(source, east, north, shunt)
    pre = relax_lead(RELAXATION * source / diag, source, east, north, shunt)
    rest = source - operate_lead(pre, east, north, shunt)[0]
    pi = pair_matrix(ni, ni // 2)
    pj = pair_matrix(nj, nj // 2)
    dot = functools.partial(jnp.einsum, precision=HIGH)
    coarse = dot("pji,jJ,iI->pJI", rest, pj, pi)
    fix = coarse_cycle(coarse, levels[1:], factor, level + 1)
    v = pre + dot("pJI,jJ,iI->pji", fix, pj, pi)
    v = relax_lead(v, source, east, north, shunt)
    return relax_lead(v, source, east, north, shunt)


def live_taps(taps, tap_current, rows, cols, row_start, col_start, all_cols):
    i = taps // all_cols - row_start
    j = taps % all_cols - col_start
    inside = (i >= -HALO) & (i < rows + HALO) & (j >= -HALO) & (j < cols + HALO)
    cand = lax.broadcasted_iota(jnp.int32, taps.shape, 0)
    code = ((i + ROW_PAD) * (cols + 2 * PAD) + j + PAD) * LANES + cand
    count = taps.size
    lead = count // LANES
    flags = inside.reshape(lead, LANES).astype(jnp.float32)
    upto = jnp.dot(flags, jnp.triu(jnp.ones((LANES, LANES), jnp.float32)), precision=HIGH)
    before = jnp.dot(
        jnp.tril(jnp.ones((lead, lead), jnp.float32), -1), upto[:, -1:], precision=HIGH
    )
    place = (upto + before).astype(jnp.int32).reshape(-1)
    place = jnp.where(inside.reshape(-1), place - 1, -1)
    pick = place[None, :] == jnp.arange(count, dtype=jnp.int32)[:, None]
    codes = jnp.sum(jnp.where(pick, code.reshape(-1)[None], 0), axis=1)
    amps = jnp.sum(jnp.where(pick, tap_current.reshape(-1)[None], 0.0), axis=1)
    return jnp.sum(inside.astype(jnp.int32)).reshape(1), codes, amps


def body(load, east_class, north_class, cond_table, taps, tap_current):
    rows, cols, cands = load.shape
    ng, nd_axis = lax.axis_size("grp"), lax.axis_size("dev")
    nd = ng * nd_axis
    pc = cands // nd
    row_start = lax.axis_index("grp") * rows
    col_start = lax.axis_index("dev") * cols
    all_rows, all_cols = ng * rows, nd_axis * cols
    edge = HALO + 1
    dims = (rows, cols, nd, pc)

    classes = jnp.stack([east_class.T, north_class.T]).astype(jnp.float32)
    strip_w = jnp.swapaxes(load[:, :HALO], 0, 1)
    strip_e = jnp.swapaxes(load[:, cols - HALO :], 0, 1)
    from_w, from_e = exchange(
        pack(strip_e, classes[:, cols - edge :]), pack(strip_w, classes[:, :edge]), "dev"
    )
    from_n, from_s = exchange(
        pack(load[rows - HALO :], classes[:, :, rows - edge :]),
        pack(load[:HALO], classes[:, :, :edge]),
        "grp",
    )
    west, west_class = unpack(from_w, strip_w, classes[:, :edge])
    east, east_class_x = unpack(from_e, strip_w, classes[:, :edge])
    north, north_class_x = unpack(from_n, load[:HALO], classes[:, :, :edge])
    south, south_class_x = unpack(from_s, load[:HALO], classes[:, :, :edge])

    def corner_load(first):
        return jnp.stack(
            [jnp.swapaxes(x[:, first : first + HALO], 0, 1) for x in (north, south)]
        )

    def corner_class(first):
        return jnp.stack([x[:, first : first + edge] for x in (north_class_x, south_class_x)])

    corner_w, corner_e = exchange(
        pack(corner_load(cols - HALO), corner_class(cols - edge)),
        pack(corner_load(0), corner_class(0)),
        "dev",
    )
    cw, cw_class = unpack(corner_w, corner_load(0), corner_class(0))
    ce, ce_class = unpack(corner_e, corner_load(0), corner_class(0))
    corners = jnp.stack([cw, ce]).reshape(2, 2, HALO * HALO, LANES)
    whole = jnp.concatenate(
        [
            jnp.concatenate([cw_class[0], north_class_x, ce_class[0]], axis=1),
            jnp.concatenate([west_class, classes, east_class_x], axis=1),
            jnp.concatenate([cw_class[1], south_class_x, ce_class[1]], axis=1),
        ],
        axis=2,
    )
    side = PAD - edge
    whole = jnp.pad(whole, ((0, 0), (side, side), (0, 0)))
    cond = jnp.zeros_like(whole)
    for k in range(cond_table.shape[0]):
        cond = jnp.where(whole == k, cond_table[k], cond)
    col_ids = (col_start - PAD + jnp.arange(cols + 2 * PAD))[:, None]
    row_ids = (row_start - edge + jnp.arange(rows + 2 * edge))[None]
    in_cols = (col_ids >= 0) & (col_ids < all_cols)
    in_rows = (row_ids >= 0) & (row_ids < all_rows)
    inside = in_cols & in_rows
    near = (jnp.abs(jnp.arange(cols + 2 * PAD) * 2 - (cols + 2 * PAD - 1)) < cols + 2 * edge)[:, None]
    inside = inside & near
    east0 = jnp.where(inside & (row_ids < all_rows - 1), cond[0], 0.0)
    north0 = jnp.where(inside & (col_ids < all_cols - 1), cond[1], 0.0)
    wide0 = cols + 2 * PAD
    ext_rows = rows + 2 * ROW_PAD
    grow = ROW_PAD + 1 - edge
    fit = ((0, 0), (grow, ROW_PAD - edge))
    coef0 = stencil_coefs(jnp.pad(east0, fit), jnp.pad(north0, fit), SHUNT_CONDUCT)

    half_rows, half_cols = rows // 2, cols // 2
    wide1 = half_cols + HALO - 2
    rows1 = half_rows + ROW_PAD
    dot = functools.partial(jnp.dot, precision=HIGH)
    c_first = PAD - (HALO - 2)
    n0r = rows + 2 * edge
    r_first = edge - ROW_PAD - 2
    sum_c = pair_matrix(wide0, wide1, c_first).T
    odd_c = pair_matrix(wide0, wide1, c_first, True).T
    sum_r = pair_matrix(n0r, rows1 + 1, r_first)
    odd_r = pair_matrix(n0r, rows1 + 1, r_first, True)
    east1 = dot(dot(sum_c, east0), odd_r)
    north1 = dot(dot(odd_c, north0), sum_r)
    coef1 = stencil_coefs(east1, north1, SHUNT_CONDUCT * 4.0)

    q_rows, q_cols = rows // 4, cols // 4
    east2 = dot(dot(pair_matrix(wide1, q_cols, 4).T, east1), pair_matrix(rows1 + 1, q_rows, 9, True))
    north2 = dot(
        dot(pair_matrix(wide1, q_cols, 4, True).T, north1), pair_matrix(rows1 + 1, q_rows, 9)
    )
    mine = jnp.stack([east2, north2]).reshape(1, -1, LANES)
    spread_out = jnp.broadcast_to(mine, (nd,) + mine.shape[1:])
    gathered = lax.all_to_all(spread_out, AXES, split_axis=0, concat_axis=0, tiled=True)
    cond2 = gathered.reshape(ng, nd_axis, 2, q_cols, q_rows)
    cond2 = cond2.transpose(2, 1, 3, 0, 4).reshape(2, nd_axis * q_cols, ng * q_rows)

    levels, factor = coarse_levels(cond2[0], cond2[1], 2)

    tap_count, tap_code, tap_amps = live_taps(
        taps, tap_current, rows, cols, row_start, col_start, all_cols
    )
    s2_rows = rows1 // 2 * q_cols
    slab_rows = pc * q_rows * q_cols // LANES
    shunts = (SHUNT_CONDUCT, SHUNT_CONDUCT * 4.0)
    s0, p0, s1, p1, slab = pl.pallas_call(
        functools.partial(down_kernel, dims, shunts),
        out_shape=[
            shape(ext_rows * wide0, LANES),
            shape(ext_rows * wide0, LANES),
            shape(rows1 * wide1, LANES),
            shape(rows1 * wide1, LANES),
            shape(nd * slab_rows, LANES),
        ],
        in_specs=[SMEM] * 3 + [VMEM] * 8,
        out_specs=[VMEM] * 5,
        scratch_shapes=[
            vmem(s2_rows, LANES),
            vmem(GROUP // 2, wide0, LANES),
            vmem(GROUP // 2, wide1, LANES),
        ]
        + rings_for(wide0)
        + rings_for(wide1),
        compiler_params=PARAMS,
        name="fine_down",
    )(tap_count, tap_code, tap_amps, load, west, east, north, south, corners, coef0, coef1)

    got = lax.all_to_all(
        slab.reshape(nd, slab_rows, LANES), AXES, split_axis=0, concat_axis=0, tiled=True
    )
    per = LANES // q_rows
    source2 = got.reshape(ng, nd_axis, q_cols // per, pc, per, q_rows)
    source2 = source2.transpose(3, 1, 4, 2, 0, 5).reshape(pc, nd_axis * q_cols, ng * q_rows)

    fix = coarse_cycle(source2, levels, factor, 2)

    padded = jnp.pad(fix, ((0, 0), (2, 2), (2, LANES)))
    pieces = [
        padded[:, d * q_cols : d * q_cols + q_cols + 4, g * q_rows : g * q_rows + LANES]
        for g in range(ng)
        for d in range(nd_axis)
    ]
    back = jnp.stack(pieces).transpose(0, 2, 1, 3).reshape(nd, (q_cols + 4) * pc, LANES)
    back = lax.all_to_all(back, AXES, split_axis=0, concat_axis=0, tiled=True)
    pitch2 = -(-(q_cols + 4) // GROUP) * GROUP
    return pl.pallas_call(
        functools.partial(up_kernel, dims, shunts),
        out_shape=shape(rows, cols, LANES),
        in_specs=[VMEM] * 7,
        out_specs=VMEM,
        scratch_shapes=[
            vmem((q_rows + 4) * pitch2, LANES),
            vmem(rows1 * wide1, LANES),
            vmem(GROUP, wide1, LANES),
            vmem(GROUP, 2 * wide1, LANES),
        ]
        + rings_for(2 * wide1)
        + rings_for(wide1),
        compiler_params=PARAMS,
        name="fine_up",
    )(back.reshape(-1, LANES), s0, p0, s1, p1, coef0, coef1)


def solution(mesh):
    return jax.shard_map(
        body,
        mesh=mesh,
        in_specs=(P("grp", "dev", None), P("grp", "dev"), P("grp", "dev"), P(), P(), P()),
        out_specs=P("grp", "dev", None),
        check_vma=False,
    )
```

time: 338 us -> 199 us (0.59)
  other arithmetic: 87.3 us -> 17.7 us
  Pallas kernels: 136 us -> 79.6 us
  local copies, waits for them, and re-layouts: 38.6 us -> 25.9 us
  waiting for transfers between devices: 2.35 us -> 6.03 us
    pallas_call x2 -> x4, Pallas kernels: 136 us -> 79.6 us  [the longest x1 41.9 us: body(): pl.pallas_call(functools.partial(down_kernel, dims, shunts), out_shape=[s...]
    another operation x10 -> x2, other arithmetic: 55.8 us -> 0.25 us  [stencil_coefs(): coefs = jnp.stack([east, north, RELAXATION / diag])]
    another operation x11 -> x2, local copies, waits for them, and re-layouts: 6.02 us -> 0.18 us  [stencil_coefs(): coefs = jnp.stack([east, north, RELAXATION / diag])]
    slice x6, local copies, waits for them, and re-layouts: 5.95 us -> 1.68 us  [unpack(): return (packed[:count].reshape(rows.shape), flat.reshape(extra.shape))]
    unnamed x70 -> x76, local copies, waits for them, and re-layouts: 7.96 us -> 8.1 us
  transfers between devices with their start and end apart: 8 -> 8, of which waited for: 1 -> 2; matrix products, arithmetic and copies ran while one was open for 33% -> 12% of each run, Pallas kernels for 22% -> 24%
where the time goes in v2:
time: 199 us; the launch traced here: 196 us
  Pallas kernels  79.6 us (40%)
  starting transfers between devices  28.4 us (14%)
  blocking collectives  26.1 us (13%)
  local copies, waits for them, and re-layouts  25.9 us (13%)
  other arithmetic  17.7 us (9%)
  matrix products  11.5 us (6%)
  waiting for transfers between devices  6.03 us (3%)
    pallas_call x1, Pallas kernels, body(): pl.pallas_call(functools.partial(down_kernel, dims, shunts), out_shape=[s...  41.9 us
    pallas_call x1, Pallas kernels, body(): pl.pallas_call(functools.partial(up_kernel, dims, shunts), out_shape=shap...  31 us
    all_to_all x1, blocking collectives, body(): back = lax.all_to_all(back, AXES, split_axis=0, concat_axis=0, tiled=True)  26.1 us
    ppermute x6, starting transfers between devices, exchange(): return (lax.ppermute(tail, axis, up), lax.ppermute(head, axis, down))  16.7 us
    unnamed x76, local copies, waits for them, and re-layouts  8.1 us
    all_to_all x1, starting transfers between devices, body(): lax.all_to_all(spread_out, AXES, split_axis=0, concat_axis=0, tiled=True)  5.84 us
    all_to_all x1, starting transfers between devices, body(): lax.all_to_all(slab.reshape(nd, slab_rows, LANES), AXES, split_axis=0, co...  5.82 us
    pallas_call x1, Pallas kernels, coarse_factor(): pl.pallas_call(factor_kernel, out_shape=[shape(levels, 5, *flat), shape(*...  5.54 us
  transfers between devices with their start and end apart: 8, of which 2 were waited for; matrix products, arithmetic and copies ran while one was open for 12% of the time, Pallas kernels for 24%

profile of v2, /device:TPU:1, one launch (start us, length us, event | category | flops | bytes accessed | tf_op | source)
XLA Modules:
  0.0 196.4 jit_solution(4145793478384443619)
XLA Ops:
  0.0 0.8 add_convert_fusion
  1.0 1.0 fusion.336
  2.1 3.9 %collective-permute-start.2 = (f32[326,128]{1,0:T(8,128)S(1)}, f32[326,128]{1,0:T(8,128)S(1)}, u32[]{:S(2)}, u32[]{:S(2)}) collective-permute-start(f32[326,128]{1,0:T(8,128)S(1)} %pad_maximum_fusion.3), channel_id=1, source_target_pairs={{0,8},{8,16},{16,24},{1,9},{9,17},{17,25},{2,10},{10,18},{18,26},{... | collective-permute-start | bytes 500744 | tf_op jit(solution)/shard_map/ppermute | solution.py:28
  6.2 1.3 collective-permute-start.3
  7.5 4.0 %fusion.337 = (f32[256,10,128]{2,1,0:T(8,128)S(1)}, f32[256,10,128]{2,1,0:T(8,128)}) fusion(f32[256,32,128]{2,1,0:T(8,128)} %own.1), kind=kLoop, calls=%fused_computation.591 | loop fusion | bytes 5242880 | tf_op jit(solution)/shard_map/slice | solution.py:528
  11.4 2.0 %copy.82 = f32[256,10,128]{2,0,1:T(8,128)S(1)} copy(f32[256,10,128]{2,1,0:T(8,128)} %get-tuple-element.24) | data formatting | bytes 2621440
  13.5 1.2 pad_maximum_fusion
  14.6 4.0 %collective-permute-start = (f32[2604,128]{1,0:T(8,128)}, f32[2604,128]{1,0:T(8,128)}, u32[]{:S(2)}, u32[]{:S(2)}) collective-permute-start(f32[2604,128]{1,0:T(8,128)} %pad_maximum_fusion), channel_id=1, source_target_pairs={{0,1},{1,2},{2,3},{3,4},{4,5},{5,6},{6,7},{8,9},{9,10},{10,11},{11... | collective-permute-start | bytes 3999752 | tf_op jit(solution)/shard_map/ppermute | solution.py:28
  19.1 1.2 pad_maximum_fusion.1
  20.3 1.9 collective-permute-start.1
  22.6 0.7 convert_reduce_fusion
  24.7 1.8 select_reduce_fusion.1.tap_code
  26.5 1.7 select_reduce_fusion.tap_amps
  28.3 0.7 fusion.344
  29.8 3.6 %collective-permute-start.4 = (f32[204,128]{1,0:T(8,128)S(1)}, f32[204,128]{1,0:T(8,128)S(1)}, u32[]{:S(2)}, u32[]{:S(2)}) collective-permute-start(f32[204,128]{1,0:T(8,128)S(1)} %pad_maximum_fusion.7), channel_id=1, source_target_pairs={{0,1},{1,2},{2,3},{3,4},{4,5},{5,6},{6,7},{8,9},{9,10},{10,11},{11... | collective-permute-start | bytes 313352 | tf_op jit(solution)/shard_map/ppermute | solution.py:28
  33.5 1.9 collective-permute-start.5
  35.8 5.1 %collective-permute-done.5 = f32[204,128]{1,0:T(8,128)S(1)} collective-permute-done((f32[204,128]{1,0:T(8,128)S(1)}, f32[204,128]{1,0:T(8,128)S(1)}, u32[]{:S(2)}, u32[]{:S(2)}) %collective-permute-start.5) | collective-permute-done | bytes 104480 | tf_op jit(solution)/shard_map/ppermute | solution.py:28
  41.2 0.7 slice.667
  42.0 5.2 %select_select_fusion = f32[2,56,278]{2,1,0:T(8,128)S(1)} fusion(f32[2,11,11]{2,1,0:T(8,128)S(1)} %slice.534, f32[2,32,11]{2,1,0:T(8,128)S(1)} %reshape.725, f32[2,11,11]{2,1,0:T(8,128)S(1)} %slice.532, f32[2,11,256]{2,1,0:T(8,128)S(1)} %reshape_reshape.7, f32[2,32,256]{2,1,0:T(8,128)S(1)} %add_convert_fusion, f32[2,11,256]{2,1,0:T(8,128)S(1)} %reshape_reshape.6, ...), kind=kLoop, calls=%fused_computation.138 | loop fusion | flops 1120896 | bytes 244672 | tf_op jit(solution)/shard_map/jit(_where)/select_n | solution.py:571
  49.8 0.7 broadcast_in_dim.149
  50.4 5.8 %all-to-all-start.1 = ((f32[32,8,128]{2,1,0:T(8,128)}), f32[32,8,128]{2,1,0:T(8,128)S(1)}, u32[]{:S(2)}, u32[]{:S(2)}) async-start(f32[32,8,128]{2,1,0:T(8,128)} %broadcast_in_dim.149), calls=%async_computation.1 | async-start | bytes 262144 | tf_op jit(solution)/shard_map/all_to_all | solution.py:609
  56.4 1.6 slice.646
  58.1 0.9 copy-done
  59.0 41.9 %fine_down.1 = (f32[16128,128]{1,0:T(8,128)}, f32[16128,128]{1,0:T(8,128)}, f32[3456,128]{1,0:T(8,128)S(1)}, f32[3456,128]{1,0:T(8,128)S(1)}, f32[512,128]{1,0:T(8,128)}) custom-call(s32[1]{0:T(128)} %bitcast.tap_count, s32[2048]{0:T(1024)S(1)} %select_reduce_fusion.1.tap_code, f32[2048]{0:T(1024)S(1)} %select_reduce_fusion.tap_amps, ...), custom_call_target="tpu_custom_call" | custom-call | tf_op jit(solution)/shard_map/fine_down/pallas_call | solution.py:621
  100.9 1.2 copy-done.1
  102.1 5.8 %all-to-all-start = ((f32[32,16,128]{2,1,0:T(8,128)}), f32[32,16,128]{2,1,0:T(8,128)S(1)}, u32[]{:S(2)}, u32[]{:S(2)}) async-start(f32[32,16,128]{2,1,0:T(8,128)} %bitcast.55), calls=%async_computation | async-start | bytes 524288 | tf_op jit(solution)/shard_map/all_to_all | solution.py:643
  110.9 0.6 pad_slice_fusion.77
  111.7 5.5 %coarse_factor.1 = (f32[5,5,8,256]{3,2,1,0:T(8,128)S(1)}, f32[8,256]{1,0:T(8,128)S(1)}) custom-call(f32[8,256]{1,0:T(8,128)S(1)} %sub.398.diag, f32[8,256]{1,0:T(8,128)S(1)} %select_n.244.right), custom_call_target="tpu_custom_call" | custom-call | tf_op jit(solution)/shard_map/coarse_factor/pallas_call | solution.py:415
  117.4 0.9 all-to-all-done
  118.7 1.1 copy.91
  119.9 1.4 reshape.737
  122.9 0.8 fusion.156
  123.7 0.9 fusion.166
  124.6 0.8 convolution_bitcast_fusion.5
  125.4 0.8 copy.85
  126.2 0.7 pad.167.clone
  126.9 1.0 reshape.739.source
  127.9 1.1 coarse_solve.1
  129.4 0.8 fusion.2
  130.2 0.8 fusion.182
  131.1 0.9 fusion.222
  132.0 0.9 fusion.1
  132.9 0.9 fusion.116
  133.8 1.2 fusion.66
  138.4 0.5 copy.80
  138.9 0.5 copy.81
  139.3 26.1 %all_to_all.15 = f32[32,48,128]{2,1,0:T(8,128)S(1)} all-to-all(f32[32,48,128]{2,1,0:T(8,128)S(1)} %copy.81), channel_id=1, replica_groups=mesh['grp'=4,'dev'=8] {'grp','dev'}, dimensions={0} | all-to-all | bytes 1572864 | tf_op jit(solution)/shard_map/all_to_all | solution.py:659
  165.4 31.0 %fine_up.1 = f32[256,32,128]{2,1,0:T(8,128)} custom-call(f32[1536,128]{1,0:T(8,128)S(1)} %bitcast.329, f32[16128,128]{1,0:T(8,128)S(1)} %bitcast.326, f32[16128,128]{1,0:T(8,128)} %get-tuple-element.16.p0, f32[3456,128]{1,0:T(8,128)S(1)} %get-tuple-element.17.s1, f32[3456,128]{1,0:T(8,128)S(1)} %copy-done.2, ...), custom_call_target="tpu_custom_call" | custom-call | tf_op jit(solution)/shard_map/fine_up/pallas_call | solution.py:661
  (222 shorter events, 15.4 us)
Async XLA Ops:
  2.1 27.0 %collective-permute-start.2 = (f32[326,128]{1,0:T(8,128)S(1)}, f32[326,128]{1,0:T(8,128)S(1)}, u32[]{:S(2)}, u32[]{:S(2)}) collective-permute-start(f32[326,128]{1,0:T(8,128)S(1)} %pad_maximum_fusion.3), channel_id=1, source_target_pairs={{0,8},{8,16},{16,24},{1,9},{9,17},{17,25},{2,10},{10,18},{18,26},{... | collective-permute-start | bytes 500744 | tf_op jit(solution)/shard_map/ppermute | solution.py:28
  6.2 23.0 %collective-permute-start.3 = (f32[326,128]{1,0:T(8,128)S(1)}, f32[326,128]{1,0:T(8,128)S(1)}, u32[]{:S(2)}, u32[]{:S(2)}) collective-permute-start(f32[326,128]{1,0:T(8,128)S(1)} %pad_maximum_fusion.4), channel_id=1, source_target_pairs={{8,0},{16,8},{24,16},{9,1},{17,9},{25,17},{10,2},{18,10},{26,18},{... | collective-permute-start | bytes 500744 | tf_op jit(solution)/shard_map/ppermute | solution.py:28
  14.6 26.5 %collective-permute-start = (f32[2604,128]{1,0:T(8,128)}, f32[2604,128]{1,0:T(8,128)}, u32[]{:S(2)}, u32[]{:S(2)}) collective-permute-start(f32[2604,128]{1,0:T(8,128)} %pad_maximum_fusion), channel_id=1, source_target_pairs={{0,1},{1,2},{2,3},{3,4},{4,5},{5,6},{6,7},{8,9},{9,10},{10,11},{11... | collective-permute-start | bytes 3999752 | tf_op jit(solution)/shard_map/ppermute | solution.py:28
  19.1 3.5 %copy-start.10 = (s32[128,16]{0,1:T(8,128)S(1)}, s32[128,16]{0,1:T(8,128)}, u32[]{:S(2)}) copy-start(s32[128,16]{0,1:T(8,128)} %param.10) | copy-start | bytes 24580
  19.1 5.1 %copy-start.9 = (f32[128,16]{0,1:T(8,128)S(1)}, f32[128,16]{0,1:T(8,128)}, u32[]{:S(2)}) copy-start(f32[128,16]{0,1:T(8,128)} %param.11) | copy-start | bytes 24580
  19.1 9.2 %copy-start.8 = (f32[8]{0:T(128)S(1)}, f32[8]{0:T(128)}, u32[]{:S(2)}) copy-start(f32[8]{0:T(128)} %param.9) | copy-start | bytes 100
  20.3 21.6 %collective-permute-start.1 = (f32[2604,128]{1,0:T(8,128)}, f32[2604,128]{1,0:T(8,128)S(1)}, u32[]{:S(2)}, u32[]{:S(2)}) collective-permute-start(f32[2604,128]{1,0:T(8,128)} %pad_maximum_fusion.1), channel_id=1, source_target_pairs={{1,0},{2,1},{3,2},{4,3},{5,4},{6,5},{7,6},{9,8},{10,9},{11,10},{12... | collective-permute-start | bytes 3999752 | tf_op jit(solution)/shard_map/ppermute | solution.py:28
  22.2 87.5 %copy-start.16 = (s32[128]{0:T(128)}, s32[128]{0:T(128)S(1)}, u32[]{:S(2)}) copy-start(s32[128]{0:T(128)S(1)} %and_select_fusion.2) | copy-start | bytes 1540
  22.3 100.1 %copy-start.11 = (s32[32]{0:T(128)}, s32[32]{0:T(128)S(1)}, u32[]{:S(2)}) copy-start(s32[32]{0:T(128)S(1)} %and_select_fusion.1) | copy-start | bytes 388
  22.3 88.1 %copy-start.12 = (s32[16]{0:T(128)}, s32[16]{0:T(128)S(1)}, u32[]{:S(2)}) copy-start(s32[16]{0:T(128)S(1)} %and_select_fusion) | copy-start | bytes 196
  22.5 86.8 %copy-start.14 = (s32[256]{0:T(256)}, s32[256]{0:T(256)S(1)}, u32[]{:S(2)}) copy-start(s32[256]{0:T(256)S(1)} %and_select_fusion.4) | copy-start | bytes 3076
  29.8 5.7 %collective-permute-start.4 = (f32[204,128]{1,0:T(8,128)S(1)}, f32[204,128]{1,0:T(8,128)S(1)}, u32[]{:S(2)}, u32[]{:S(2)}) collective-permute-start(f32[204,128]{1,0:T(8,128)S(1)} %pad_maximum_fusion.7), channel_id=1, source_target_pairs={{0,1},{1,2},{2,3},{3,4},{4,5},{5,6},{6,7},{8,9},{9,10},{10,11},{11... | collective-permute-start | bytes 313352 | tf_op jit(solution)/shard_map/ppermute | solution.py:28
  33.5 7.3 %collective-permute-start.5 = (f32[204,128]{1,0:T(8,128)S(1)}, f32[204,128]{1,0:T(8,128)S(1)}, u32[]{:S(2)}, u32[]{:S(2)}) collective-permute-start(f32[204,128]{1,0:T(8,128)S(1)} %pad_maximum_fusion.8), channel_id=1, source_target_pairs={{1,0},{2,1},{3,2},{4,3},{5,4},{6,5},{7,6},{9,8},{10,9},{11,10},{12... | collective-permute-start | bytes 313352 | tf_op jit(solution)/shard_map/ppermute | solution.py:28
  50.4 51.6 %all-to-all-start.1 = ((f32[32,8,128]{2,1,0:T(8,128)}), f32[32,8,128]{2,1,0:T(8,128)S(1)}, u32[]{:S(2)}, u32[]{:S(2)}) async-start(f32[32,8,128]{2,1,0:T(8,128)} %broadcast_in_dim.149), calls=%async_computation.1 | async-start | bytes 262144 | tf_op jit(solution)/shard_map/all_to_all | solution.py:609
  56.4 2.6 %copy-start = (f32[256,32,128]{2,1,0:T(8,128)S(1)}, f32[256,32,128]{2,1,0:T(8,128)}, u32[]{:S(2)}) copy-start(f32[256,32,128]{2,1,0:T(8,128)} %own.1) | copy-start | bytes 12582916
  100.9 1.2 copy-start.1
  102.1 16.3 %all-to-all-start = ((f32[32,16,128]{2,1,0:T(8,128)}), f32[32,16,128]{2,1,0:T(8,128)S(1)}, u32[]{:S(2)}, u32[]{:S(2)}) async-start(f32[32,16,128]{2,1,0:T(8,128)} %bitcast.55), calls=%async_computation | async-start | bytes 524288 | tf_op jit(solution)/shard_map/all_to_all | solution.py:643
  111.5 11.2 %copy-start.6 = (f32[16,64]{1,0:T(8,128)}, f32[16,64]{1,0:T(8,128)S(1)}, u32[]{:S(2)}) copy-start(f32[16,64]{1,0:T(8,128)S(1)} %get-tuple-element.56) | copy-start | bytes 12292
  117.3 5.1 %copy-start.3 = (f32[32,128]{1,0:T(8,128)}, f32[32,128]{1,0:T(8,128)S(1)}, u32[]{:S(2)}) copy-start(f32[32,128]{1,0:T(8,128)S(1)} %get-tuple-element.52) | copy-start | bytes 49156
  117.3 5.1 %copy-start.4 = (f32[32,128]{1,0:T(8,128)}, f32[32,128]{1,0:T(8,128)S(1)}, u32[]{:S(2)}) copy-start(f32[32,128]{1,0:T(8,128)S(1)} %get-tuple-element.53) | copy-start | bytes 49156
  117.3 5.1 %copy-start.5 = (f32[32,128]{1,0:T(8,128)}, f32[32,128]{1,0:T(8,128)S(1)}, u32[]{:S(2)}) copy-start(f32[32,128]{1,0:T(8,128)S(1)} %get-tuple-element.54) | copy-start | bytes 49156
  118.7 3.3 %copy-start.15 = (s32[256]{0:T(256)S(1)}, s32[256]{0:T(256)}, u32[]{:S(2)}) copy-start(s32[256]{0:T(256)} %copy-done.14) | copy-start | bytes 3076
  119.9 2.9 %copy-start.17 = (s32[128]{0:T(128)S(1)}, s32[128]{0:T(128)}, u32[]{:S(2)}) copy-start(s32[128]{0:T(128)} %copy-done.16) | copy-start | bytes 1540
  119.9 3.0 %copy-start.7 = (f32[16,64]{1,0:T(8,128)S(1)}, f32[16,64]{1,0:T(8,128)}, u32[]{:S(2)}) copy-start(f32[16,64]{1,0:T(8,128)} %get-tuple-element.57) | copy-start | bytes 12292
  119.9 3.8 %copy-start.13 = (s32[16]{0:T(128)S(1)}, s32[16]{0:T(128)}, u32[]{:S(2)}) copy-start(s32[16]{0:T(128)} %copy-done.12) | copy-start | bytes 196
  133.8 31.6 %slice-start = ((s8[8257536]{0:T(1024)(128)(4,1)}), s8[4194304]{0:T(1024)(128)(4,1)S(1)}, s32[]{:S(2)}) async-start(s8[8257536]{0:T(1024)(128)(4,1)} %bitcast.325), calls=%async_computation.3 | async-start | bytes 8388608
  137.7 27.7 %slice-start.1 = ((s8[8257536]{0:T(1024)(128)(4,1)}), s8[4063232]{0:T(1024)(128)(4,1)S(1)}, s32[]{:S(2)}) async-start(s8[8257536]{0:T(1024)(128)(4,1)} %bitcast.325), calls=%async_computation.4 | async-start | bytes 8126464
  138.4 27.0 %copy-start.2 = (f32[3456,128]{1,0:T(8,128)S(1)}, f32[3456,128]{1,0:T(8,128)}, u32[]{:S(2)}) copy-start(f32[3456,128]{1,0:T(8,128)} %copy-done.1) | copy-start | bytes 5308420

commit v3 on v2

v3 whole, which is shorter than its diff:
```python
import functools

import jax
import jax.numpy as jnp
from jax import lax
from jax.experimental import pallas as pl
from jax.experimental.pallas import tpu as pltpu
from jax.sharding import PartitionSpec as P

LEVELS = 5
RELAXATION = 0.8
KEEP = 1.0 - RELAXATION
SHUNT_CONDUCT = 0.01
AXES = ("grp", "dev")
HIGH = lax.Precision.HIGHEST

HALO = 10
PAD = 12
ROW_PAD = 16
LANES = 128
GROUP = 8


def exchange(tail, head, axis):
    count = lax.axis_size(axis)
    up = [(i, i + 1) for i in range(count - 1)]
    down = [(i + 1, i) for i in range(count - 1)]
    return lax.ppermute(tail, axis, up), lax.ppermute(head, axis, down)


RING = 4 * GROUP


def wave(groups, stop, width, coef, coef_first, shunt, rings, fill, source, middle, finish):
    ring_e, ring_n, ring_w, ring_a, ring_b, flux_b, again_b, flux_c, turn = rings
    low, high = groups
    per_tile = LANES // GROUP
    for ref in rings:
        ref[...] = jnp.zeros_like(ref)

    def at(ref, row, ahead=0):
        base = pl.multiple_of(lax.rem(row, RING) * width, GROUP)
        return ref[pl.ds(base + ahead, width), :]

    def put(ref, row, value):
        base = pl.multiple_of(lax.rem(row, RING) * width, GROUP)
        ref[pl.ds(base, width), :] = value

    def balance(ring, row, before, slot):
        here = at(ring, row)
        east = at(ring_e, row) * (at(ring, row + 1) - here)
        north = at(ring_n, row) * (at(ring, row, 1) - here)
        turn[slot, pl.ds(GROUP, width), :] = north
        south = turn[slot, pl.ds(GROUP - 1, width), :]
        total = (east - before) + (north - south) + (source(row) - shunt * here)
        return here, east, total

    def go(t, carry):
        g = jnp.minimum(t, high - 1)
        shift = lax.rem(LANES - lax.rem(g, per_tile) * GROUP, LANES)
        found = [
            pltpu.roll(coef[k, g // per_tile, pl.ds(coef_first, width), :], shift, 1)
            for k in range(3)
        ]
        for r in range(GROUP):
            row = g * GROUP + r
            east, north, weight = (
                jnp.broadcast_to(x[:, r : r + 1], (width, LANES)) for x in found
            )
            put(ring_e, row, east)
            put(ring_n, row, north)
            put(ring_w, row, weight)
            put(ring_a, row, fill(r, row, weight))
        g = jnp.clip(t - 1, low, high - 1)
        flux = jnp.where(t > high, again_b[...], flux_b[...])
        again_b[...] = flux
        for r in range(GROUP):
            row = g * GROUP + r
            here, flux, total = balance(ring_a, row, flux, r)
            value = here + at(ring_w, row) * total
            put(ring_b, row, value)
            middle(row, value)
        flux_b[...] = flux
        g = jnp.clip(t - 2, low, high - 1)
        flux = flux_c[...]
        for r in range(GROUP):
            row = g * GROUP + r
            here, flux, total = balance(ring_b, row, flux, GROUP + r)
            finish(g, r, row, here, total, lambda row=row: at(ring_w, row))
        flux_c[...] = flux
        return carry

    lax.fori_loop(low, stop + 2, go, 0)


def rings_for(width):
    ring = vmem(RING * width + GROUP, LANES)
    return [ring] * 5 + [vmem(width, LANES)] * 3 + [vmem(2 * GROUP, width + GROUP, LANES)]


def strip_kernel(
    dims, place, table, load, east_class, north_class,
    strip_e, strip_w, strip_n, strip_s, cond, shares, held,
):
    rows, cols, nd, pc = dims
    edge = HALO + 1

    def copy(i, carry):
        strip_e[pl.ds(i * HALO, HALO), :] = load[i, cols - HALO :, :]
        strip_w[pl.ds(i * HALO, HALO), :] = load[i, :HALO, :]
        return carry

    lax.fori_loop(0, rows, copy, 0, unroll=8)
    for i in range(HALO):
        strip_n[pl.ds(i * cols, cols), :] = load[rows - HALO + i]
        strip_s[pl.ds(i * cols, cols), :] = load[i]
    coarse = []
    for k, classes in enumerate((east_class, north_class)):
        kind = classes[...]
        value = jnp.zeros(kind.shape, jnp.float32)
        for c in range(table.shape[0]):
            value = jnp.where(kind == c, table[c], value)
        node = lax.broadcasted_iota(jnp.int32, kind.shape, k)
        value = jnp.where(node == place[k], 0.0, value)
        turned = jnp.pad(value, ((0, 0), (0, LANES - cols))).T[:cols]
        cond[k] = turned
        pieces = rows // LANES
        for h in range(pieces):
            at = pl.ds(rows * HALO + k * edge * pieces + h, edge, stride=pieces)
            part = turned[:, h * LANES : (h + 1) * LANES]
            strip_e[at, :] = part[cols - edge :]
            strip_w[at, :] = part[:edge]
        at = pl.ds(cols * HALO + k * cols, cols)
        strip_n[at, :] = pltpu.roll(turned, edge, 1)[:, :LANES]
        strip_s[at, :] = turned[:, :LANES]
        for _ in range(2):
            even, odd = row_pairs(held, turned)
            turned = halve_lanes(even + odd, odd=True) if k == 0 else halve_lanes(odd)
        coarse.append(turned)
    q_rows, q_cols = rows // 4, cols // 4
    per = LANES // q_rows
    group = q_cols // per
    for k, value in enumerate(coarse):
        for jl in range(per):
            shares[pl.ds(k * group, group), pl.ds(jl * q_rows, q_rows)] = value[
                jl * group : (jl + 1) * group, :q_rows
            ]
    mine = shares[pl.ds(0, 2 * group), :]
    for q in range(1, nd):
        shares[pl.ds(q * 2 * group, 2 * group), :] = mine


def corner_kernel(cols, north, south, out_e, out_w):
    edge = HALO + 1
    cond_at = 2 * HALO * HALO
    for ref in (out_e, out_w):
        ref[...] = jnp.zeros_like(ref)
    for end, strip in enumerate((north, south)):
        for i in range(HALO):
            at = pl.ds((end * HALO + i) * HALO, HALO)
            out_e[at, :] = strip[pl.ds((i + 1) * cols - HALO, HALO), :]
            out_w[at, :] = strip[pl.ds(i * cols, HALO), :]
        for k in range(2):
            at = pl.ds(cond_at + (end * 2 + k) * 2 * GROUP, edge)
            first = cols * HALO + k * cols
            out_e[at, :] = strip[pl.ds(first + cols - edge, edge), :]
            out_w[at, :] = strip[pl.ds(first, edge), :]


def coef_kernel(
    dims, cond, west, east, north, south, corner_w, corner_e, coef0, coef1, grid, held
):
    rows, cols, nd, pc = dims
    edge = HALO + 1
    wide0, wide1 = coef0.shape[2], coef1.shape[2]
    pieces = rows // LANES
    first = ROW_PAD - edge
    grids = []
    for k in range(2):
        grid[...] = jnp.zeros_like(grid)
        grid[pl.ds(PAD, cols), pl.ds(ROW_PAD, rows)] = cond[k]
        for strip, col in ((west, PAD - edge), (east, PAD + cols)):
            for h in range(pieces):
                at = pl.ds(rows * HALO + k * edge * pieces + h, edge, stride=pieces)
                grid[pl.ds(col, edge), pl.ds(ROW_PAD + h * LANES, LANES)] = strip[at, :]
        for end, (strip, row) in enumerate(((north, first), (south, ROW_PAD + rows))):
            at = pl.ds(cols * HALO + k * cols, cols)
            grid[pl.ds(PAD, cols), pl.ds(row, edge)] = strip[at, :][:, :edge]
            at = pl.ds(2 * HALO * HALO + (end * 2 + k) * 2 * GROUP, edge)
            for corner, col in ((corner_w, PAD - edge), (corner_e, PAD + cols)):
                grid[pl.ds(col, edge), pl.ds(row, edge)] = corner[at, :][:, :edge]
        grids.append(grid[...])

    def put(coef, east, west, north, south, shunt):
        weight = RELAXATION / (shunt + east + west + north + south)
        for i, value in enumerate((east, north, weight)):
            for t, piece in enumerate(lane_chunks(value)):
                coef[i, t] = piece

    east, north = grids
    put(coef0, east, pltpu.roll(east, 1, 1), north, pltpu.roll(north, 1, 0), SHUNT_CONDUCT)
    tiles = east.shape[1] // LANES

    def picked(start):
        at = pl.ds(start, wide1, stride=2)
        return jnp.concatenate([held[t, at, :] for t in range(tiles)], axis=1)

    start = PAD - (HALO - 2)
    for t, piece in enumerate(lane_chunks(east)):
        held[t] = piece
    east = halve_lanes(picked(start) + picked(start + 1), odd=True)
    for t, piece in enumerate(lane_chunks(north)):
        held[t] = piece
    north, south = halve_lanes(picked(start + 1)), halve_lanes(picked(start - 1))
    put(coef1, east, pltpu.roll(east, 1, 1), north, south, 4.0 * SHUNT_CONDUCT)


def tap_kernel(dims, all_cols, place, taps, currents, count, codes, amps):
    rows, cols, nd, pc = dims

    def turned(x):
        return jnp.pad(x, ((0, 0), (0, LANES - x.shape[1]))).T[: x.shape[1]]

    node = turned(taps[...].astype(jnp.float32)).astype(jnp.int32)
    current = turned(currents[...])
    lead = node.shape[0]
    row_at = node // all_cols
    i = row_at - place[2]
    j = node - row_at * all_cols - place[3]
    inside = (i >= -HALO) & (i < rows + HALO) & (j >= -HALO) & (j < cols + HALO)
    lane = lax.broadcasted_iota(jnp.int32, node.shape, 1)
    code = ((i + ROW_PAD) * (cols + 2 * PAD) + j + PAD) * LANES + lane
    flags = jnp.where(inside, 1.0, 0.0)
    at, to = iota2(LANES, LANES)
    upto = exact_dot(flags, (at <= to).astype(jnp.float32))
    at, to = iota2(lead, lead)
    before = exact_dot((at > to).astype(jnp.float32), upto)[:, LANES - 1 :]
    slot = jnp.where(inside, (upto + before).astype(jnp.int32) - 1, -1)
    total = jnp.sum(flags).astype(jnp.int32)
    count[0] = total
    codes[...] = jnp.zeros_like(codes)
    amps[...] = jnp.zeros_like(amps)
    wanted = lax.broadcasted_iota(jnp.int32, (LANES, LANES), 0)
    code = code.astype(jnp.float32)

    def fill(chunk, carry):
        found = jnp.zeros((LANES, LANES), jnp.float32)
        amount = jnp.zeros((LANES, LANES), jnp.float32)
        for k in range(lead):
            hit = wanted + chunk * LANES == jnp.broadcast_to(slot[k : k + 1], wanted.shape)
            found += jnp.where(hit, jnp.broadcast_to(code[k : k + 1], wanted.shape), 0.0)
            amount += jnp.where(hit, jnp.broadcast_to(current[k : k + 1], wanted.shape), 0.0)
        codes[pl.ds(chunk, 1), :] = jnp.sum(found.T, axis=0, keepdims=True).astype(jnp.int32)
        amps[pl.ds(chunk, 1), :] = jnp.sum(amount.T, axis=0, keepdims=True)
        return carry

    lax.fori_loop(0, (total + LANES - 1) // LANES, fill, 0)


def down_kernel(
    dims, shunts, tap_count, tap_code, tap_amps, own_hbm, west_hbm, east_hbm, north, south,
    corner_w, corner_e, coef0, coef1, s0, p0, s1, p1, slab, own, west, east, sems, s2, pair,
    pair1, *rings,
):
    rows, cols, nd, pc = dims
    wide = cols + 2 * PAD
    ext = s0.shape[0] // wide
    rings0, rings1 = rings[:9], rings[9:]

    moves = [
        pltpu.make_async_copy(source.at[pl.ds(0, here.shape[0])], here, sems.at[k])
        for k, (source, here) in enumerate(((own_hbm, own), (west_hbm, west), (east_hbm, east)))
    ]
    for move in moves:
        move.start()
    s0[...] = jnp.zeros_like(s0)
    for move in moves:
        move.wait()
    first = ROW_PAD - HALO

    def copy_own(i, carry):
        base = (i + ROW_PAD) * wide
        s0[pl.ds(base + PAD, cols), :] = -own[i]
        s0[pl.ds(base + PAD - HALO, HALO), :] = -west[pl.ds(i * HALO, HALO), :]
        s0[pl.ds(base + PAD + cols, HALO), :] = -east[pl.ds(i * HALO, HALO), :]
        return carry

    lax.fori_loop(0, rows, copy_own, 0, unroll=8)
    for k, (strip, base) in enumerate(((north, first), (south, ROW_PAD + rows))):
        for i in range(HALO):
            at = (base + i) * wide + PAD
            corner = pl.ds((k * HALO + i) * HALO, HALO)
            s0[pl.ds(at, cols), :] = -strip[i * cols : (i + 1) * cols, :]
            s0[pl.ds(at - HALO, HALO), :] = -corner_w[corner, :]
            s0[pl.ds(at + cols, HALO), :] = -corner_e[corner, :]

    lane = lax.broadcasted_iota(jnp.int32, (GROUP, LANES), 1)
    sub = lax.broadcasted_iota(jnp.int32, (GROUP, LANES), 0)

    def add_tap(k, carry):
        code = tap_code[k]
        node = code // LANES
        base = pl.multiple_of(node // GROUP * GROUP, GROUP)
        hit = (lane == lax.rem(code, LANES)) & (sub == node - base)
        s0[pl.ds(base, GROUP), :] += jnp.where(hit, tap_amps[k], 0.0)
        return carry

    lax.fori_loop(0, tap_count[0], add_tap, 0)

    def smooth_and_restrict(source, pre, coef, shunt, pair, rings, store):
        width = pair.shape[1]
        held = []

        def row_of(ref, row):
            return ref[pl.ds(pl.multiple_of(row * width, GROUP), width), :]

        def middle(row, value):
            pre[pl.ds(pl.multiple_of(row * width, GROUP), width), :] = value

        def finish(g, r, row, here, total, weight):
            if r % 2 == 0:
                held.append(total)
            else:
                pair[r // 2] = held.pop() + total
                store(g * (GROUP // 2) + r // 2, r // 2)

        groups = source.shape[0] // width // GROUP
        wave(
            (0, groups), groups - 1, width, coef, 0, shunt, rings,
            lambda r, row, weight: weight * row_of(source, row),
            lambda row: row_of(source, row), middle, finish,
        )

    half = pair1.shape[1]
    start = PAD - (HALO - 2)

    def store1(k, m):
        s1[pl.ds(pl.multiple_of(k * half, GROUP), half), :] = (
            pair[m, pl.ds(start, half, stride=2), :] + pair[m, pl.ds(start + 1, half, stride=2), :]
        )

    smooth_and_restrict(s0, p0, coef0, shunts[0], pair, rings0, store1)
    quarter = cols // 4

    def store2(k, m):
        s2[pl.ds(pl.multiple_of(k * quarter, quarter), quarter), :] = (
            pair1[m, pl.ds(4, quarter, stride=2), :] + pair1[m, pl.ds(5, quarter, stride=2), :]
        )

    smooth_and_restrict(s1, p1, coef1, shunts[1], pair1, rings1, store2)
    rows2 = rows // 4
    per = LANES // rows2
    groups = quarter // per
    for jp in range(groups):
        parts = [
            s2[pl.ds(ROW_PAD // 4 * quarter + jl * groups + jp, rows2, stride=quarter), :]
            for jl in range(per)
        ]
        turned = jnp.concatenate(parts, axis=0).T
        for p in range(pc):
            slab[pl.ds(jp * pc + p, nd, stride=groups * pc), :] = turned[p * nd : (p + 1) * nd]


def up_kernel(dims, shunts, back, s0, p0, s1, p1, coef0, coef1, out, x2, c1, twice1, twice0, *rings):
    rows, cols, nd, pc = dims
    wide = cols + 2 * PAD
    quarter = cols // 4
    wide2 = quarter + 4
    width1 = 2 * wide2
    width0 = 2 * width1
    rows2 = rows // 4 + 4
    pitch2 = x2.shape[0] // rows2
    rings0, rings1 = rings[:9], rings[9:]
    for jw in range(wide2):
        parts = [back[pl.ds(jw * pc + p, nd, stride=wide2 * pc), :] for p in range(pc)]
        turned = jnp.concatenate(parts, axis=0).T
        x2[pl.ds(jw, rows2, stride=pitch2), :] = turned[:rows2]

    def lifted(twice, slot, x):
        count = x.shape[0]
        twice[slot, pl.ds(0, count, stride=2), :] = x
        twice[slot, pl.ds(1, count, stride=2), :] = x
        return twice[slot]

    def fill1(r, row, weight):
        k = jnp.clip(row // 2 - 2, 0, rows2 - 1)
        x = x2[pl.ds(pl.multiple_of(k * pitch2, GROUP), pitch2), :][:wide2]
        return p1[pl.ds(pl.multiple_of(row * width1, GROUP), width1), :] + lifted(
            twice1, r, x
        )

    def source1(row):
        return s1[pl.ds(pl.multiple_of(row * width1, GROUP), width1), :]

    def finish1(g, r, row, here, total, weight):
        c1[pl.ds(pl.multiple_of(row * width1, GROUP), width1), :] = here + weight() * total

    groups1 = s1.shape[0] // width1 // GROUP
    wave(
        (0, groups1), groups1, width1, coef1, 0, shunts[1], rings1,
        fill1, source1, lambda row, value: None, finish1,
    )

    start = PAD - (HALO - 2)

    def fill0(r, row, weight):
        x = c1[pl.ds(pl.multiple_of(row // 2 * width1, GROUP), width1), :]
        return p0[pl.ds(row * wide + start, width0), :] + lifted(twice0, r, x)

    def source0(row):
        return s0[pl.ds(row * wide + start, width0), :]

    first, last = ROW_PAD // GROUP, (ROW_PAD + rows) // GROUP

    def finish0(g, r, row, here, total, weight):
        done = here + weight() * total
        row = jnp.clip(row - ROW_PAD, r, rows - GROUP + r)
        out[row] = done[HALO - 2 : HALO - 2 + cols]

    wave(
        (first - 1, last + 1), last, width0, coef0, start, shunts[0], rings0,
        fill0, source0, lambda row, value: None, finish0,
    )


VMEM = pl.BlockSpec(memory_space=pltpu.VMEM)
SMEM = pl.BlockSpec(memory_space=pltpu.SMEM)
HBM = pl.BlockSpec(memory_space=pltpu.HBM)
PARAMS = pltpu.CompilerParams(vmem_limit_bytes=40 * 2**20)


SMALL = pltpu.CompilerParams(vmem_limit_bytes=16 * 2**20)


def shape(*dims):
    return jax.ShapeDtypeStruct(dims, jnp.float32)


def vmem(*dims):
    return pltpu.VMEM(dims, jnp.float32)


def lane_chunks(x):
    return [x[:, i : i + LANES] for i in range(0, x.shape[1], LANES)]


def block_column(x, k):
    size = x.shape[0]
    lane = lax.broadcasted_iota(jnp.int32, (size, LANES), 1)
    at = lane // size * size + k
    take = functools.partial(jnp.take_along_axis, axis=1, mode="promise_in_bounds")
    return jnp.concatenate([take(c, at) for c in lane_chunks(x)], axis=1)


def block_rows(held, x):
    held[...] = x

    def row(k):
        return jnp.broadcast_to(held[pl.ds(k, 1), :], x.shape)

    return row


def over(size, step, start):
    return lax.fori_loop(0, size, step, start, unroll=size <= GROUP)


def block_product(held, x, *others):
    rows = [block_rows(h, y) for h, y in zip(held, others)]

    def step(k, totals):
        column = block_column(x, k)
        return tuple(t + column * row(k) for t, row in zip(totals, rows))

    return over(x.shape[0], step, tuple(jnp.zeros_like(x) for _ in others))


def block_inverse(held, x):
    size, count = x.shape
    inner = lax.broadcasted_iota(jnp.int32, x.shape, 1) % size
    row_id = lax.broadcasted_iota(jnp.int32, x.shape, 0)

    def step(k, x):
        row = block_rows(held[0], x)(k)
        column = block_column(x, k)
        pivot = block_rows(held[1], column)(k)
        scaled = jnp.where(inner == k, 1.0, row) / pivot
        rest = jnp.where(inner == k, 0.0, x) - column * scaled
        return jnp.where(row_id == k, scaled, rest)

    return over(size, step, x)


def ahead(x, blocks):
    lanes = x.shape[1]
    return pltpu.roll(x, (-blocks * x.shape[0]) % lanes, 1)


def exact_dot(x, y):
    return jnp.dot(x, y, precision=HIGH, preferred_element_type=jnp.float32)


def iota2(rows, cols):
    return (
        lax.broadcasted_iota(jnp.int32, (rows, cols), 0),
        lax.broadcasted_iota(jnp.int32, (rows, cols), 1),
    )


def lanes_for(count):
    return -(-count // LANES) * LANES


def halve_lanes(x, odd=False):
    count = x.shape[1]
    fine, coarse = iota2(count, lanes_for(count // 2))
    hit = fine == 2 * coarse + 1 if odd else fine // 2 == coarse
    return exact_dot(x, hit.astype(jnp.float32))


def double_lanes(x, count):
    coarse, fine = iota2(x.shape[1], count)
    return exact_dot(x, (fine // 2 == coarse).astype(jnp.float32))


def row_pairs(held, x):
    rows = x.shape[0]
    for t, piece in enumerate(lane_chunks(x)):
        held[t, pl.ds(0, rows), :] = piece
    return [
        jnp.concatenate(
            [held[t, pl.ds(k, rows // 2, stride=2), :] for t in range(x.shape[1] // LANES)], axis=1
        )
        for k in range(2)
    ]


def double_rows(held, x):
    rows = x.shape[0]
    for t, piece in enumerate(lane_chunks(x)):
        for k in range(2):
            held[t, pl.ds(k, rows, stride=2), :] = piece
    return jnp.concatenate(
        [held[t, pl.ds(0, 2 * rows), :] for t in range(x.shape[1] // LANES)], axis=1
    )


def place_blocks(dims, from_ref, pitch, to_ref, sets):
    ng, nd_axis, q_rows, q_cols = dims
    per = LANES // q_rows
    group = q_cols // per
    for g in range(ng):
        for d in range(nd_axis):
            for first, stride, base in sets:
                at = (g * nd_axis + d) * pitch + first
                piece = from_ref[pl.ds(at, group, stride=stride), :]
                for jl in range(per):
                    to_ref[
                        pl.ds(base + d * q_cols + jl * group, group), pl.ds(g * q_rows, q_rows)
                    ] = piece[:, jl * q_rows : (jl + 1) * q_rows]


def factor_kernel(dims, pc, gathered, *refs):
    levels = LEVELS - 2
    coefs, (parts, last), (grid, spare, *held) = refs[:levels], refs[levels:levels + 2], refs[levels + 2:]
    ng, nd_axis, q_rows, q_cols = dims
    nj, ni = nd_axis * q_cols, ng * q_rows
    group = q_cols * q_rows // LANES
    place_blocks(dims, gathered, 2 * group, grid, [(0, 1, 0), (group, 1, nj)])
    east, north = grid[pl.ds(0, nj), :], grid[pl.ds(nj, nj), :]
    for k in range(LEVELS - 1):
        shunt = SHUNT_CONDUCT * 4.0 ** (k + 2)
        west, south = pltpu.roll(east, 1, 1), pltpu.roll(north, 1, 0)
        diag = shunt + east + west + north + south
        if k == levels:
            break
        for i, part in enumerate((east, north, RELAXATION / diag)):
            for p in range(pc):
                coefs[k][i, pl.ds(p * nj, nj), :] = part
        even, odd = row_pairs(spare, east)
        east = halve_lanes(even + odd, odd=True)
        even, odd = row_pairs(spare, north)
        north = halve_lanes(odd)
        nj, ni = nj // 2, ni // 2
    size, count = nj, ni * nj
    at, lane = iota2(east.shape[1], count)
    repeat = (lane // size == at).astype(jnp.float32)
    row, col = iota2(size, count)
    col = col % size
    d = jnp.where(col == row, exact_dot(diag, repeat), 0.0)
    d = d - jnp.where(col == row + 1, exact_dot(north, repeat), 0.0)
    d = d - jnp.where(col == row - 1, exact_dot(south, repeat), 0.0)
    c = jnp.where(col == row, -exact_dot(east, repeat), 0.0)
    ct = c
    stride = 1
    level = 0
    while stride * size < count:
        inverse = block_inverse(held, d)
        (r,) = block_product(held, c, ahead(inverse, stride))
        (lx,) = block_product(held, ct, inverse)
        left, lead = ahead(lx, -stride), ahead(lx, stride)
        for i, part in enumerate((r, left, inverse, c, ahead(ct, -stride))):
            parts[level, i] = part
        first, new_c = block_product(held, r, ct, ahead(c, stride))
        (second,) = block_product(held, left, ahead(c, -stride))
        (new_ct,) = block_product(held, lead, ct)
        d = d - first - second
        c, ct = -new_c, -new_ct
        stride *= 2
        level += 1
    last[...] = block_inverse(held, d)


def reduce_and_solve(held, f, parts, last):
    size = f.shape[0]
    block = lax.broadcasted_iota(jnp.int32, f.shape, 1) // size
    levels = parts.shape[0]
    for level in range(levels):
        s = 2**level
        (a,) = block_product(held, parts[level, 0], ahead(f, s))
        (b,) = block_product(held, parts[level, 1], ahead(f, -s))
        f = jnp.where(block % (2 * s) == 0, f - a - b, f)
    (x,) = block_product(held, last[...], f)
    for level in reversed(range(levels)):
        s = 2**level
        (a,) = block_product(held, parts[level, 3], ahead(x, s))
        (b,) = block_product(held, parts[level, 4], ahead(x, -s))
        (new,) = block_product(held, parts[level, 2], f - a - b)
        x = jnp.where(block % (2 * s) == s, new, x)
    return x


def grid_residual(v, source, coef, shunt):
    lanes, rows = v.shape[1], v.shape[0]
    east = coef[0] * (pltpu.roll(v, lanes - 1, 1) - v)
    north = coef[1] * (pltpu.roll(v, rows - 1, 0) - v)
    total = (east - pltpu.roll(east, 1, 1)) + (north - pltpu.roll(north, 1, 0))
    return total + (source - shunt * v)


def coarse_kernel(dims, pc, got, *refs):
    levels = LEVELS - 2
    coefs, (parts, last, back) = refs[:levels], refs[levels : levels + 3]
    grid, spare, shifted, shifted_odd, *held = refs[levels + 3 :]
    ng, nd_axis, q_rows, q_cols = dims
    nj, ni = nd_axis * q_cols, ng * q_rows
    pitch = got.shape[0] // (ng * nd_axis)
    place_blocks(dims, got, pitch, grid, [(p, pc, p * nj) for p in range(pc)])
    source = grid[...]
    stored = []
    for k in range(levels):
        shunt = SHUNT_CONDUCT * 4.0 ** (k + 2)
        coef = coefs[k]
        start = coef[2] * source
        pre = start + coef[2] * grid_residual(start, source, coef, shunt)
        rest = grid_residual(pre, source, coef, shunt)
        stored.append((pre, source, shunt, coef))
        even, odd = row_pairs(spare, rest)
        source = halve_lanes(even + odd)
    size = source.shape[0] // pc
    blocks = ni // 2**levels
    at, lane = iota2(source.shape[1], size * blocks)
    f = None
    picks = [(lane == at * size + p).astype(jnp.float32) for p in range(pc)]
    for p, pick in enumerate(picks):
        part = exact_dot(source[p * size : (p + 1) * size], pick)
        f = part if f is None else f + part
    x = reduce_and_solve(held, f, parts, last)
    fix = jnp.concatenate([exact_dot(x, pick.T) for pick in picks], axis=0)
    for pre, source, shunt, coef in reversed(stored):
        lanes = pre.shape[1]
        v = pre + double_rows(spare, double_lanes(fix, lanes))
        for _ in range(2):
            v = v + coef[2] * grid_residual(v, source, coef, shunt)
        fix = v
    shifted[...] = jnp.zeros_like(shifted)
    rows_p = shifted.shape[0] // pc
    wide = jnp.concatenate([fix, jnp.zeros((fix.shape[0], LANES), jnp.float32)], axis=1)
    wide = pltpu.roll(wide, 2, 1)
    for p in range(pc):
        shifted[pl.ds(p * rows_p + 2, nj), :] = wide[p * nj : (p + 1) * nj]
    lanes = shifted.shape[1]
    shifted_odd[...] = pltpu.roll(shifted[...], lanes - LANES // 2, 1)
    window = q_cols + 4
    for g in range(ng):
        lane_at = g * q_rows
        ref = shifted if lane_at % LANES == 0 else shifted_odd
        lane_at = lane_at // LANES * LANES
        for d in range(nd_axis):
            for p in range(pc):
                piece = ref[pl.ds(p * rows_p + d * q_cols, window), pl.ds(lane_at, LANES)]
                at = (g * nd_axis + d) * window * pc + p
                back[pl.ds(at, window, stride=pc), :] = piece


def coarse_factor(dims, pc, gathered):
    ng, nd_axis, q_rows, q_cols = dims
    nj, ni = nd_axis * q_cols, ng * q_rows
    coefs = []
    for k in range(LEVELS - 2):
        coefs.append(shape(3, pc * nj >> k, lanes_for(ni >> k)))
    size, blocks = nj >> (LEVELS - 2), ni >> (LEVELS - 2)
    flat = (size, blocks * size)
    out = pl.pallas_call(
        functools.partial(factor_kernel, dims, pc),
        out_shape=coefs + [shape(blocks.bit_length() - 1, 5, *flat), shape(*flat)],
        in_specs=[VMEM],
        out_specs=[VMEM] * (len(coefs) + 2),
        scratch_shapes=[vmem(2 * nj, ni), vmem(ni // LANES, nj, LANES)] + [vmem(*flat)] * 2,
        compiler_params=SMALL,
        name="coarse_factor",
    )(gathered)
    return out


def coarse_levels(dims, pc, got, factor):
    ng, nd_axis, q_rows, q_cols = dims
    nj, ni = nd_axis * q_cols, ng * q_rows
    flat = factor[-1].shape
    padded = (pc * (nj + GROUP), ni + LANES)
    return pl.pallas_call(
        functools.partial(coarse_kernel, dims, pc),
        out_shape=shape(ng * nd_axis * (q_cols + 4) * pc, LANES),
        in_specs=[VMEM] * (len(factor) + 1),
        out_specs=VMEM,
        scratch_shapes=[
            vmem(pc * nj, ni), vmem(ni // LANES, pc * nj, LANES), vmem(*padded), vmem(*padded)
        ]
        + [vmem(*flat)] * 2,
        compiler_params=SMALL,
        name="coarse_levels",
    )(got, *factor)


def body(load, east_class, north_class, cond_table, taps, tap_current):
    rows, cols, cands = load.shape
    ng, nd_axis = lax.axis_size("grp"), lax.axis_size("dev")
    nd = ng * nd_axis
    pc = cands // nd
    row_start = lax.axis_index("grp") * rows
    col_start = lax.axis_index("dev") * cols
    all_rows, all_cols = ng * rows, nd_axis * cols
    edge = HALO + 1
    dims = (rows, cols, nd, pc)

    q_rows, q_cols = rows // 4, cols // 4
    coarse_dims = (ng, nd_axis, q_rows, q_cols)
    place = jnp.stack(
        [all_rows - 1 - row_start, all_cols - 1 - col_start, row_start, col_start]
    ).astype(jnp.int32)
    dev_rows = rows * HALO + 2 * edge * rows // LANES
    grp_rows = cols * HALO + 2 * cols
    corner_rows = 2 * HALO * HALO + 8 * GROUP
    share = 2 * q_rows * q_cols // LANES

    strip_e, strip_w, strip_n, strip_s, cond, shares = pl.pallas_call(
        functools.partial(strip_kernel, dims),
        out_shape=[shape(dev_rows, LANES)] * 2
        + [shape(grp_rows, LANES)] * 2
        + [shape(2, cols, rows), shape(nd * share, LANES)],
        in_specs=[SMEM] * 2 + [VMEM] * 3,
        out_specs=[VMEM] * 6,
        scratch_shapes=[vmem(rows // LANES, cols, LANES)],
        compiler_params=PARAMS,
        name="strips",
    )(place, cond_table, load, east_class, north_class)
    from_w, from_e = exchange(strip_e, strip_w, "dev")
    from_n, from_s = exchange(strip_n, strip_s, "grp")
    tap_count, tap_code, tap_amps = pl.pallas_call(
        functools.partial(tap_kernel, dims, all_cols),
        out_shape=[
            jax.ShapeDtypeStruct((1,), jnp.int32),
            jax.ShapeDtypeStruct((taps.shape[1], LANES), jnp.int32),
            shape(taps.shape[1], LANES),
        ],
        in_specs=[SMEM] + [VMEM] * 2,
        out_specs=[SMEM, VMEM, VMEM],
        compiler_params=SMALL,
        name="taps",
    )(place, taps, tap_current)
    corner_e_out, corner_w_out = pl.pallas_call(
        functools.partial(corner_kernel, cols),
        out_shape=[shape(corner_rows, LANES)] * 2,
        in_specs=[VMEM] * 2,
        out_specs=[VMEM] * 2,
        compiler_params=SMALL,
        name="corners",
    )(from_n, from_s)
    shares, corner_e_out, corner_w_out = lax.optimization_barrier(
        (shares, corner_e_out, corner_w_out)
    )
    corner_w, corner_e = exchange(corner_e_out, corner_w_out, "dev")
    gathered = lax.all_to_all(
        shares.reshape(nd, share, LANES), AXES, split_axis=0, concat_axis=0, tiled=True
    )
    factor = coarse_factor(coarse_dims, pc, gathered.reshape(-1, LANES))

    wide0 = cols + 2 * PAD
    ext_rows = rows + 2 * ROW_PAD
    wide1 = cols // 2 + HALO - 2
    rows1 = rows // 2 + ROW_PAD
    lanes0 = lanes_for(ext_rows)
    coef0, coef1 = pl.pallas_call(
        functools.partial(coef_kernel, dims),
        out_shape=[
            shape(3, lanes0 // LANES, wide0, LANES),
            shape(3, lanes_for(lanes0 // 2) // LANES, wide1, LANES),
        ],
        in_specs=[VMEM] * 7,
        out_specs=[VMEM] * 2,
        scratch_shapes=[vmem(wide0, lanes0), vmem(lanes0 // LANES, wide0, LANES)],
        compiler_params=SMALL,
        name="coefs",
    )(cond, from_w, from_e, from_n, from_s, corner_w, corner_e)

    s2_rows = rows1 // 2 * q_cols
    slab_rows = pc * q_rows * q_cols // LANES
    shunts = (SHUNT_CONDUCT, SHUNT_CONDUCT * 4.0)
    s0, p0, s1, p1, slab = pl.pallas_call(
        functools.partial(down_kernel, dims, shunts),
        out_shape=[
            shape(ext_rows * wide0, LANES),
            shape(ext_rows * wide0, LANES),
            shape(rows1 * wide1, LANES),
            shape(rows1 * wide1, LANES),
            shape(nd * slab_rows, LANES),
        ],
        in_specs=[SMEM] * 3 + [HBM] * 3 + [VMEM] * 6,
        out_specs=[VMEM] * 5,
        scratch_shapes=[
            vmem(rows, cols, LANES),
            vmem(rows * HALO, LANES),
            vmem(rows * HALO, LANES),
            pltpu.SemaphoreType.DMA((3,)),
            vmem(s2_rows, LANES),
            vmem(GROUP // 2, wide0, LANES),
            vmem(GROUP // 2, wide1, LANES),
        ]
        + rings_for(wide0)
        + rings_for(wide1),
        compiler_params=PARAMS,
        name="fine_down",
    )(tap_count, tap_code.reshape(-1), tap_amps.reshape(-1), load, from_w, from_e, from_n, from_s, corner_w, corner_e, coef0, coef1)

    got = lax.all_to_all(
        slab.reshape(nd, slab_rows, LANES), AXES, split_axis=0, concat_axis=0, tiled=True
    )
    back = coarse_levels(coarse_dims, pc, got.reshape(-1, LANES), factor)
    back = back.reshape(nd, (q_cols + 4) * pc, LANES)
    back = lax.all_to_all(back, AXES, split_axis=0, concat_axis=0, tiled=True)
    pitch2 = -(-(q_cols + 4) // GROUP) * GROUP
    return pl.pallas_call(
        functools.partial(up_kernel, dims, shunts),
        out_shape=shape(rows, cols, LANES),
        in_specs=[VMEM] * 7,
        out_specs=VMEM,
        scratch_shapes=[
            vmem((q_rows + 4) * pitch2, LANES),
            vmem(rows1 * wide1, LANES),
            vmem(GROUP, wide1, LANES),
            vmem(GROUP, 2 * wide1, LANES),
        ]
        + rings_for(2 * wide1)
        + rings_for(wide1),
        compiler_params=PARAMS,
        name="fine_up",
    )(back.reshape(-1, LANES), s0, p0, s1, p1, coef0, coef1)


def solution(mesh):
    return jax.shard_map(
        body,
        mesh=mesh,
        in_specs=(P("grp", "dev", None), P("grp", "dev"), P("grp", "dev"), P(), P(), P()),
        out_specs=P("grp", "dev", None),
        check_vma=False,
    )
```

time: 199 us -> 175 us (0.88)
  other arithmetic: 17.7 us -> 0.08 us
  Pallas kernels: 79.6 us -> 91.7 us
  matrix products: 11.5 us -> 0 us
  local copies, waits for them, and re-layouts: 25.9 us -> 17.3 us
  waiting for transfers between devices: 6.03 us -> 13.3 us
  blocking collectives: 26.1 us -> 24.1 us
    pallas_call x2 -> x6, Pallas kernels: 6.68 us -> 19 us  [the longest x1 7.55 us: coarse_factor(): pl.pallas_call(functools.partial(factor_kernel, dims, pc), out_shape=coef...]
    dot_general x34 -> x0, matrix products: 11.5 us -> none  [the longest x6 4.32 us: coarse_cycle(): v = pre + dot('pJI,jJ,iI->pji', fix, pj, pi)]
    unnamed x76 -> x40, local copies, waits for them, and re-layouts: 8.1 us -> 17.3 us
    slice x23 -> x0, local copies, waits for them, and re-layouts: 9.09 us -> none  [the longest x1 3.95 us: body(): strip_w = jnp.swapaxes(load[:, :HALO], 0, 1)]
    select_n x13 -> x0, other arithmetic: 5.61 us -> none  [the longest x1 5.16 us: body(): cond = jnp.where(whole == k, cond_table[k], cond)]
    reshape x27 -> x0, local copies, waits for them, and re-layouts: 5.54 us -> none  [the longest x2 1.46 us: body(): source2 = got.reshape(ng, nd_axis, q_cols // per, pc, per, q_rows)]
    ppermute x6, waiting for transfers between devices: 5.08 us -> 10.4 us  [exchange(): return (lax.ppermute(tail, axis, up), lax.ppermute(head, axis, down))]
    reduce_sum x3 -> x0, other arithmetic: 4.22 us -> none  [the longest x1 1.75 us: live_taps(): codes = jnp.sum(jnp.where(pick, code.reshape(-1)[None], 0), axis=1)]
  transfers between devices with their start and end apart: 8 -> 8, of which waited for: 2 -> 4; matrix products, arithmetic and copies ran while one was open for 12% -> 0% of each run, Pallas kernels for 24% -> 30%
where the time goes in v3:
time: 175 us; the launch traced here: 174 us
  Pallas kernels  91.7 us (52%)
  starting transfers between devices  27.1 us (15%)
  blocking collectives  24.1 us (14%)
  local copies, waits for them, and re-layouts  17.3 us (10%)
  waiting for transfers between devices  13.3 us (8%)
    pallas_call x1, Pallas kernels, body(): pl.pallas_call(functools.partial(down_kernel, dims, shunts), out_shape=[s...  41.6 us
    pallas_call x1, Pallas kernels, body(): pl.pallas_call(functools.partial(up_kernel, dims, shunts), out_shape=shap...  31.1 us
    all_to_all x1, blocking collectives, body(): back = lax.all_to_all(back, AXES, split_axis=0, concat_axis=0, tiled=True)  24.1 us
    unnamed x40, local copies, waits for them, and re-layouts  17.3 us
    ppermute x6, starting transfers between devices, exchange(): return (lax.ppermute(tail, axis, up), lax.ppermute(head, axis, down))  16.4 us
    ppermute x6, waiting for transfers between devices, exchange(): return (lax.ppermute(tail, axis, up), lax.ppermute(head, axis, down))  10.4 us
    pallas_call x1, Pallas kernels, coarse_factor(): pl.pallas_call(functools.partial(factor_kernel, dims, pc), out_shape=coef...  7.55 us
    pallas_call x1, Pallas kernels, coarse_levels(): pl.pallas_call(functools.partial(coarse_kernel, dims, pc), out_shape=shap...  6.22 us
  transfers between devices with their start and end apart: 8, of which 4 were waited for; matrix products, arithmetic and copies ran while one was open for 0% of the time, Pallas kernels for 30%

profile of v3, /device:TPU:1, one launch (start us, length us, event | category | flops | bytes accessed | tf_op | source)
XLA Modules:
  0.0 173.8 jit_solution(16280462677677431128)
XLA Ops:
  0.0 0.9 copy.9.east_class
  0.9 0.9 copy.10.north_class
  1.7 0.1 pad_add_fusion.place
  1.8 2.2 %copy-done = f32[256,32,128]{2,1,0:T(8,128)S(1)} copy-done((f32[256,32,128]{2,1,0:T(8,128)S(1)}, f32[256,32,128]{2,1,0:T(8,128)}, u32[]{:S(2)}) %copy-start) | copy-done | bytes 4194328
  4.0 0.7 copy-done.13
  4.6 2.7 %strips.1 = (f32[2604,128]{1,0:T(8,128)}, f32[2604,128]{1,0:T(8,128)}, f32[384,128]{1,0:T(8,128)S(1)}, f32[384,128]{1,0:T(8,128)S(1)}, f32[2,32,256]{2,1,0:T(8,128)S(1)}, /*index=5*/f32[256,128]{1,0:T(8,128)}) custom-call(s32[4]{0:T(128)S(1)} %pad_add_fusion.place, f32[8]{0:T(128)S(1)} %copy-done.13, f32[256,32,128]{2,1,0:T(8,128)S(1)} %copy-done, ...), custom_call_target="tpu_custom_call" | custom-call | tf_op jit(solution)/shard_map/strips/pallas_call | solution.py:756
  7.4 0.6 copy-done.11
  8.0 4.6 %collective-permute-start = (f32[2604,128]{1,0:T(8,128)}, f32[2604,128]{1,0:T(8,128)S(1)}, u32[]{:S(2)}, u32[]{:S(2)}) collective-permute-start(f32[2604,128]{1,0:T(8,128)} %get-tuple-element.34), channel_id=1, source_target_pairs={{0,1},{1,2},{2,3},{3,4},{4,5},{5,6},{6,7},{8,9},{9,10},{10,11},{11... | collective-permute-start | bytes 3999752 | tf_op jit(solution)/shard_map/ppermute | solution.py:28
  12.6 1.9 %collective-permute-start.1 = (f32[2604,128]{1,0:T(8,128)}, f32[2604,128]{1,0:T(8,128)S(1)}, u32[]{:S(2)}, u32[]{:S(2)}) collective-permute-start(f32[2604,128]{1,0:T(8,128)} %get-tuple-element.35), channel_id=1, source_target_pairs={{1,0},{2,1},{3,2},{4,3},{5,4},{6,5},{7,6},{9,8},{10,9},{11,10},{12... | collective-permute-start | bytes 3999752 | tf_op jit(solution)/shard_map/ppermute | solution.py:28
  14.5 3.1 %collective-permute-start.2 = (f32[384,128]{1,0:T(8,128)S(1)}, f32[384,128]{1,0:T(8,128)S(1)}, u32[]{:S(2)}, u32[]{:S(2)}) collective-permute-start(f32[384,128]{1,0:T(8,128)S(1)} %get-tuple-element.36), channel_id=1, source_target_pairs={{0,8},{8,16},{16,24},{1,9},{9,17},{17,25},{2,10},{10,18},{18,26},{... | collective-permute-start | bytes 589832 | tf_op jit(solution)/shard_map/ppermute | solution.py:28
  17.6 1.3 collective-permute-start.3
  18.9 2.0 %collective-permute-done.2.north = f32[384,128]{1,0:T(8,128)S(1)} collective-permute-done((f32[384,128]{1,0:T(8,128)S(1)}, f32[384,128]{1,0:T(8,128)S(1)}, u32[]{:S(2)}, u32[]{:S(2)}) %collective-permute-start.2) | collective-permute-done | bytes 196640 | tf_op jit(solution)/shard_map/ppermute | solution.py:28
  20.9 5.9 %collective-permute-done.3.south = f32[384,128]{1,0:T(8,128)S(1)} collective-permute-done((f32[384,128]{1,0:T(8,128)S(1)}, f32[384,128]{1,0:T(8,128)S(1)}, u32[]{:S(2)}, u32[]{:S(2)}) %collective-permute-start.3) | collective-permute-done | bytes 196640 | tf_op jit(solution)/shard_map/ppermute | solution.py:28
  26.8 0.0 copy-start.15
  26.8 0.6 copy-done.15
  27.4 5.8 %all-to-all-start.1 = ((f32[32,8,128]{2,1,0:T(8,128)}), f32[32,8,128]{2,1,0:T(8,128)}, u32[]{:S(2)}, u32[]{:S(2)}) async-start(f32[32,8,128]{2,1,0:T(8,128)} %bitcast.8), calls=%async_computation.1 | async-start | bytes 262144 | tf_op jit(solution)/shard_map/all_to_all | solution.py:793
  33.2 0.0 copy-done.14
  33.2 3.5 %collective-permute-start.4 = (f32[264,128]{1,0:T(8,128)}, f32[264,128]{1,0:T(8,128)S(1)}, u32[]{:S(2)}, u32[]{:S(2)}) collective-permute-start(f32[264,128]{1,0:T(8,128)} %copy-done.15), channel_id=1, source_target_pairs={{0,1},{1,2},{2,3},{3,4},{4,5},{5,6},{6,7},{8,9},{9,10},{10,11},{11... | collective-permute-start | bytes 405512 | tf_op jit(solution)/shard_map/ppermute | solution.py:28
  36.8 1.9 %collective-permute-start.5 = (f32[264,128]{1,0:T(8,128)}, f32[264,128]{1,0:T(8,128)S(1)}, u32[]{:S(2)}, u32[]{:S(2)}) collective-permute-start(f32[264,128]{1,0:T(8,128)} %copy-done.14), channel_id=1, source_target_pairs={{1,0},{2,1},{3,2},{4,3},{5,4},{6,5},{7,6},{9,8},{10,9},{11,10},{12... | collective-permute-start | bytes 405512 | tf_op jit(solution)/shard_map/ppermute | solution.py:28
  38.7 0.0 copy-done.16
  38.7 0.1 copy.7.taps
  38.8 0.0 copy-done.17
  38.8 0.1 copy.8.currents
  38.9 1.8 %taps.2 = (s32[1]{0:T(128)}, s32[16,128]{1,0:T(8,128)S(1)}, f32[16,128]{1,0:T(8,128)S(1)}) custom-call(s32[4]{0:T(128)S(1)} %pad_add_fusion.place, s32[128,16]{1,0:T(8,128)S(1)} %copy.7.taps, f32[128,16]{1,0:T(8,128)S(1)} %copy.8.currents), custom_call_target="tpu_custom_call" | custom-call | tf_op jit(solution)/shard_map/taps/pallas_call | solution.py:769
  40.7 0.0 collective-permute-done.4.corner_w
  40.8 2.6 %collective-permute-done.5.corner_e = f32[264,128]{1,0:T(8,128)S(1)} collective-permute-done((f32[264,128]{1,0:T(8,128)}, f32[264,128]{1,0:T(8,128)S(1)}, u32[]{:S(2)}, u32[]{:S(2)}) %collective-permute-start.5) | collective-permute-done | bytes 135200 | tf_op jit(solution)/shard_map/ppermute | solution.py:28
  43.3 0.6 copy-done.7
  44.0 0.0 collective-permute-done.west.west_hbm
  44.0 0.0 collective-permute-done.1.east.east_hbm
  44.0 0.9 copy-done.8
  44.9 0.8 copy-done.12
  45.7 0.7 coefs.1
  46.5 0.2 copy-done.9
  46.7 2.2 %copy-done.1 = f32[256,32,128]{2,1,0:T(8,128)S(1)} copy-done((f32[256,32,128]{2,1,0:T(8,128)S(1)}, f32[256,32,128]{2,1,0:T(8,128)}, u32[]{:S(2)}) %copy-start.1) | copy-done | bytes 4194328
  48.8 41.6 %fine_down.1 = (f32[16128,128]{1,0:T(8,128)}, f32[16128,128]{1,0:T(8,128)}, f32[3456,128]{1,0:T(8,128)S(1)}, f32[3456,128]{1,0:T(8,128)S(1)}, f32[512,128]{1,0:T(8,128)S(1)}) custom-call(s32[1]{0:T(128)} %get-tuple-element.31.tap_count, s32[2048]{0:T(1024)S(1)} %bitcast.16, f32[2048]{0:T(1024)S(1)} %bitcast.17, f32[256,32,128]{2,1,0:T(8,128)S(1)} %copy-done.1, ...), custom_call_target="tpu_custom_call" | custom-call | tf_op jit(solution)/shard_map/fine_down/pallas_call | solution.py:819
  90.5 0.0 copy-start.3
  90.5 1.2 copy-done.3
  91.7 1.2 copy-done.5
  93.0 0.7 copy-done.10
  93.7 0.0 all-to-all-done.1
  93.7 4.9 %all-to-all-start = ((f32[32,16,128]{2,1,0:T(8,128)}), f32[32,16,128]{2,1,0:T(8,128)S(1)}, u32[]{:S(2)}, u32[]{:S(2)}) async-start(f32[32,16,128]{2,1,0:T(8,128)} %bitcast.15), calls=%async_computation | async-start | bytes 524288 | tf_op jit(solution)/shard_map/all_to_all | solution.py:845
  98.6 7.6 %coarse_factor.1 = (f32[3,256,256]{2,1,0:T(8,128)S(1)}, f32[3,128,128]{2,1,0:T(8,128)S(1)}, f32[3,64,128]{2,1,0:T(8,128)S(1)}, f32[5,5,8,256]{3,2,1,0:T(8,128)S(1)}, f32[8,256]{1,0:T(8,128)S(1)}) custom-call(f32[256,128]{1,0:T(8,128)} %bitcast.9.gathered), custom_call_target="tpu_custom_call" | custom-call | tf_op jit(solution)/shard_map/coarse_factor/pallas_call | solution.py:704
  106.2 2.9 %all-to-all-done = f32[32,16,128]{2,1,0:T(8,128)S(1)} async-done(((f32[32,16,128]{2,1,0:T(8,128)}), f32[32,16,128]{2,1,0:T(8,128)S(1)}, u32[]{:S(2)}, u32[]{:S(2)}) %all-to-all-start) | async-done | bytes 262176 | tf_op jit(solution)/shard_map/all_to_all | solution.py:845
  109.1 6.2 %coarse_levels.1 = f32[1536,128]{1,0:T(8,128)S(1)} custom-call(f32[512,128]{1,0:T(8,128)S(1)} %bitcast.14, f32[3,256,256]{2,1,0:T(8,128)S(1)} %get-tuple-element.48.refs_0_, f32[3,128,128]{2,1,0:T(8,128)S(1)} %get-tuple-element.49.refs_1_, f32[3,64,128]{2,1,0:T(8,128)S(1)} %get-tuple-element.50.refs_2_, f32[5,5,8,256]{3,2,1,0:T(8,128)S(1)} %get-tuple-element.51.refs_3_, ...), custom_call_target="tpu_custom_call" | custom-call | tf_op jit(solution)/shard_map/coarse_levels/pallas_call | solution.py:721
  115.3 24.1 %all_to_all.15 = f32[32,48,128]{2,1,0:T(8,128)S(1)} all-to-all(f32[32,48,128]{2,1,0:T(8,128)S(1)} %bitcast.12), channel_id=1, replica_groups=mesh['grp'=4,'dev'=8] {'grp','dev'}, dimensions={0} | all-to-all | bytes 1572864 | tf_op jit(solution)/shard_map/all_to_all | solution.py:850
  139.4 0.0 copy-done.4
  139.4 3.3 %copy-done.2 = f32[16128,128]{1,0:T(8,128)S(1)} copy-done((f32[16128,128]{1,0:T(8,128)S(1)}, f32[16128,128]{1,0:T(8,128)}, u32[]{:S(2)}) %copy-start.2) | copy-done | bytes 8257560
  142.8 31.1 %fine_up.1 = f32[256,32,128]{2,1,0:T(8,128)} custom-call(f32[1536,128]{1,0:T(8,128)S(1)} %bitcast.13, f32[16128,128]{1,0:T(8,128)S(1)} %copy-done.2, f32[16128,128]{1,0:T(8,128)} %get-tuple-element.54.p0, f32[3456,128]{1,0:T(8,128)S(1)} %copy-done.4, f32[3456,128]{1,0:T(8,128)S(1)} %copy-done.6, f32[3,3,56,128]{3,2,1,0:T(8,128)S(1)} %get-tuple-element.44.coef0, ...), custom_call_target="tpu_custom_call" | custom-call | tf_op jit(solution)/shard_map/fine_up/pallas_call | solution.py:852
  (18 shorter events, 0.1 us)
Async XLA Ops:
  1.8 2.2 %copy-start = (f32[256,32,128]{2,1,0:T(8,128)S(1)}, f32[256,32,128]{2,1,0:T(8,128)}, u32[]{:S(2)}) copy-start(f32[256,32,128]{2,1,0:T(8,128)} %own_hbm.1) | copy-start | bytes 12582916
  4.0 0.7 copy-start.13
  4.6 34.1 %copy-start.16 = (s32[128,16]{0,1:T(8,128)S(1)}, s32[128,16]{0,1:T(8,128)}, u32[]{:S(2)}) copy-start(s32[128,16]{0,1:T(8,128)} %param.10) | copy-start | bytes 24580
  4.6 34.2 %copy-start.17 = (f32[128,16]{0,1:T(8,128)S(1)}, f32[128,16]{0,1:T(8,128)}, u32[]{:S(2)}) copy-start(f32[128,16]{0,1:T(8,128)} %param.11) | copy-start | bytes 24580
  7.4 0.6 copy-start.11
  8.0 36.0 %collective-permute-start = (f32[2604,128]{1,0:T(8,128)}, f32[2604,128]{1,0:T(8,128)S(1)}, u32[]{:S(2)}, u32[]{:S(2)}) collective-permute-start(f32[2604,128]{1,0:T(8,128)} %get-tuple-element.34), channel_id=1, source_target_pairs={{0,1},{1,2},{2,3},{3,4},{4,5},{5,6},{6,7},{8,9},{9,10},{10,11},{11... | collective-permute-start | bytes 3999752 | tf_op jit(solution)/shard_map/ppermute | solution.py:28
  12.6 31.4 %collective-permute-start.1 = (f32[2604,128]{1,0:T(8,128)}, f32[2604,128]{1,0:T(8,128)S(1)}, u32[]{:S(2)}, u32[]{:S(2)}) collective-permute-start(f32[2604,128]{1,0:T(8,128)} %get-tuple-element.35), channel_id=1, source_target_pairs={{1,0},{2,1},{3,2},{4,3},{5,4},{6,5},{7,6},{9,8},{10,9},{11,10},{12... | collective-permute-start | bytes 3999752 | tf_op jit(solution)/shard_map/ppermute | solution.py:28
  14.5 6.4 %collective-permute-start.2 = (f32[384,128]{1,0:T(8,128)S(1)}, f32[384,128]{1,0:T(8,128)S(1)}, u32[]{:S(2)}, u32[]{:S(2)}) collective-permute-start(f32[384,128]{1,0:T(8,128)S(1)} %get-tuple-element.36), channel_id=1, source_target_pairs={{0,8},{8,16},{16,24},{1,9},{9,17},{17,25},{2,10},{10,18},{18,26},{... | collective-permute-start | bytes 589832 | tf_op jit(solution)/shard_map/ppermute | solution.py:28
  17.6 9.1 %collective-permute-start.3 = (f32[384,128]{1,0:T(8,128)S(1)}, f32[384,128]{1,0:T(8,128)S(1)}, u32[]{:S(2)}, u32[]{:S(2)}) collective-permute-start(f32[384,128]{1,0:T(8,128)S(1)} %get-tuple-element.37), channel_id=1, source_target_pairs={{8,0},{16,8},{24,16},{9,1},{17,9},{25,17},{10,2},{18,10},{26,18},{... | collective-permute-start | bytes 589832 | tf_op jit(solution)/shard_map/ppermute | solution.py:28
  26.8 0.7 copy-start.15
  27.4 5.8 %copy-start.14 = (f32[264,128]{1,0:T(8,128)}, f32[264,128]{1,0:T(8,128)S(1)}, u32[]{:S(2)}) copy-start(f32[264,128]{1,0:T(8,128)S(1)} %get-tuple-element.42) | copy-start | bytes 405508
  27.4 66.2 %all-to-all-start.1 = ((f32[32,8,128]{2,1,0:T(8,128)}), f32[32,8,128]{2,1,0:T(8,128)}, u32[]{:S(2)}, u32[]{:S(2)}) async-start(f32[32,8,128]{2,1,0:T(8,128)} %bitcast.8), calls=%async_computation.1 | async-start | bytes 262144 | tf_op jit(solution)/shard_map/all_to_all | solution.py:793
  33.2 7.5 %collective-permute-start.4 = (f32[264,128]{1,0:T(8,128)}, f32[264,128]{1,0:T(8,128)S(1)}, u32[]{:S(2)}, u32[]{:S(2)}) collective-permute-start(f32[264,128]{1,0:T(8,128)} %copy-done.15), channel_id=1, source_target_pairs={{0,1},{1,2},{2,3},{3,4},{4,5},{5,6},{6,7},{8,9},{9,10},{10,11},{11... | collective-permute-start | bytes 405512 | tf_op jit(solution)/shard_map/ppermute | solution.py:28
  36.8 6.5 %collective-permute-start.5 = (f32[264,128]{1,0:T(8,128)}, f32[264,128]{1,0:T(8,128)S(1)}, u32[]{:S(2)}, u32[]{:S(2)}) collective-permute-start(f32[264,128]{1,0:T(8,128)} %copy-done.14), channel_id=1, source_target_pairs={{1,0},{2,1},{3,2},{4,3},{5,4},{6,5},{7,6},{9,8},{10,9},{11,10},{12... | collective-permute-start | bytes 405512 | tf_op jit(solution)/shard_map/ppermute | solution.py:28
  43.3 0.7 copy-start.7
  44.0 0.9 copy-start.8
  44.9 0.8 copy-start.12
  45.7 0.9 copy-start.9
  46.7 2.2 %copy-start.1 = (f32[256,32,128]{2,1,0:T(8,128)S(1)}, f32[256,32,128]{2,1,0:T(8,128)}, u32[]{:S(2)}) copy-start(f32[256,32,128]{2,1,0:T(8,128)} %own_hbm.1) | copy-start | bytes 12582916
  90.5 1.2 copy-start.3
  91.7 1.2 copy-start.5
  93.0 0.7 copy-start.10
  93.7 15.4 %all-to-all-start = ((f32[32,16,128]{2,1,0:T(8,128)}), f32[32,16,128]{2,1,0:T(8,128)S(1)}, u32[]{:S(2)}, u32[]{:S(2)}) async-start(f32[32,16,128]{2,1,0:T(8,128)} %bitcast.15), calls=%async_computation | async-start | bytes 524288 | tf_op jit(solution)/shard_map/all_to_all | solution.py:845
  109.1 30.3 %copy-start.4 = (f32[3456,128]{1,0:T(8,128)S(1)}, f32[3456,128]{1,0:T(8,128)}, u32[]{:S(2)}) copy-start(f32[3456,128]{1,0:T(8,128)} %copy-done.3) | copy-start | bytes 5308420
  109.1 30.3 %copy-start.6 = (f32[3456,128]{1,0:T(8,128)S(1)}, f32[3456,128]{1,0:T(8,128)}, u32[]{:S(2)}) copy-start(f32[3456,128]{1,0:T(8,128)} %copy-done.5) | copy-start | bytes 5308420
  139.4 3.3 %copy-start.2 = (f32[16128,128]{1,0:T(8,128)S(1)}, f32[16128,128]{1,0:T(8,128)}, u32[]{:S(2)}) copy-start(f32[16128,128]{1,0:T(8,128)} %get-tuple-element.53.s0) | copy-start | bytes 24772612

commit v4 on v3

--- a/solution.py
+++ b/solution.py
@@ -7,9 +7,9 @@
 from jax.experimental.pallas import tpu as pltpu
 from jax.sharding import PartitionSpec as P
 
+
 LEVELS = 5
 RELAXATION = 0.8
-KEEP = 1.0 - RELAXATION
 SHUNT_CONDUCT = 0.01
 AXES = ("grp", "dev")
 HIGH = lax.Precision.HIGHEST
@@ -102,7 +102,7 @@
     dims, place, table, load, east_class, north_class,
     strip_e, strip_w, strip_n, strip_s, cond, shares, held,
 ):
-    rows, cols, nd, pc = dims
+    rows, cols, nd, _ = dims
     edge = HALO + 1
 
     def copy(i, carry):
@@ -120,9 +120,8 @@
         value = jnp.zeros(kind.shape, jnp.float32)
         for c in range(table.shape[0]):
             value = jnp.where(kind == c, table[c], value)
-        node = lax.broadcasted_iota(jnp.int32, kind.shape, k)
-        value = jnp.where(node == place[k], 0.0, value)
-        turned = jnp.pad(value, ((0, 0), (0, LANES - cols))).T[:cols]
+        node = lax.broadcasted_iota(jnp.int32, kind.shape, 1 - k)
+        turned = jnp.where(node == place[k], 0.0, value)
         cond[k] = turned
         pieces = rows // LANES
         for h in range(pieces):
@@ -170,9 +169,9 @@
 def coef_kernel(
     dims, cond, west, east, north, south, corner_w, corner_e, coef0, coef1, grid, held
 ):
-    rows, cols, nd, pc = dims
+    rows, cols, _, _ = dims
     edge = HALO + 1
-    wide0, wide1 = coef0.shape[2], coef1.shape[2]
+    wide1 = coef1.shape[2]
     pieces = rows // LANES
     first = ROW_PAD - edge
     grids = []
@@ -216,13 +215,8 @@
 
 
 def tap_kernel(dims, all_cols, place, taps, currents, count, codes, amps):
-    rows, cols, nd, pc = dims
-
-    def turned(x):
-        return jnp.pad(x, ((0, 0), (0, LANES - x.shape[1]))).T[: x.shape[1]]
-
-    node = turned(taps[...].astype(jnp.float32)).astype(jnp.int32)
-    current = turned(currents[...])
+    rows, cols, _, _ = dims
+    node, current = taps[...], currents[...]
     lead = node.shape[0]
     row_at = node // all_cols
     i = row_at - place[2]
@@ -259,12 +253,11 @@
 
 def down_kernel(
     dims, shunts, tap_count, tap_code, tap_amps, own_hbm, west_hbm, east_hbm, north, south,
-    corner_w, corner_e, coef0, coef1, s0, p0, s1, p1, slab, own, west, east, sems, s2, pair,
-    pair1, *rings,
+    corner_w, corner_e, coef0, coef1, s0_out, p0_out, s1, p1, slab, s0, p0, own, west, east, sems,
+    s2, pair, pair1, *rings,
 ):
     rows, cols, nd, pc = dims
     wide = cols + 2 * PAD
-    ext = s0.shape[0] // wide
     rings0, rings1 = rings[:9], rings[9:]
 
     moves = [
@@ -306,6 +299,9 @@
         return carry
 
     lax.fori_loop(0, tap_count[0], add_tap, 0)
+    save_s0 = pltpu.make_async_copy(s0, s0_out, sems.at[3])
+    save_p0 = pltpu.make_async_copy(p0, p0_out, sems.at[4])
+    save_s0.start()
 
     def smooth_and_restrict(source, pre, coef, shunt, pair, rings, store):
         width = pair.shape[1]
@@ -340,6 +336,7 @@
         )
 
     smooth_and_restrict(s0, p0, coef0, shunts[0], pair, rings0, store1)
+    save_p0.start()
     quarter = cols // 4
 
     def store2(k, m):
@@ -359,9 +356,14 @@
         turned = jnp.concatenate(parts, axis=0).T
         for p in range(pc):
             slab[pl.ds(jp * pc + p, nd, stride=groups * pc), :] = turned[p * nd : (p + 1) * nd]
-
-
-def up_kernel(dims, shunts, back, s0, p0, s1, p1, coef0, coef1, out, x2, c1, twice1, twice0, *rings):
+    save_s0.wait()
+    save_p0.wait()
+
+
+def up_kernel(
+    dims, shunts, back, s0_hbm, p0_hbm, s1, p1, coef0, coef1, out, s0, p0, sems, x2, c1, twice1,
+    twice0, *rings,
+):
     rows, cols, nd, pc = dims
     wide = cols + 2 * PAD
     quarter = cols // 4
@@ -371,6 +373,12 @@
     rows2 = rows // 4 + 4
     pitch2 = x2.shape[0] // rows2
     rings0, rings1 = rings[:9], rings[9:]
+    moves = [
+        pltpu.make_async_copy(far, near, sems.at[k])
+        for k, (far, near) in enumerate(((s0_hbm, s0), (p0_hbm, p0)))
+    ]
+    for move in moves:
+        move.start()
     for jw in range(wide2):
         parts = [back[pl.ds(jw * pc + p, nd, stride=wide2 * pc), :] for p in range(pc)]
         turned = jnp.concatenate(parts, axis=0).T
@@ -411,6 +419,8 @@
         return s0[pl.ds(row * wide + start, width0), :]
 
     first, last = ROW_PAD // GROUP, (ROW_PAD + rows) // GROUP
+    for move in moves:
+        move.wait()
 
     def finish0(g, r, row, here, total, weight):
         done = here + weight() * total
@@ -426,7 +436,7 @@
 VMEM = pl.BlockSpec(memory_space=pltpu.VMEM)
 SMEM = pl.BlockSpec(memory_space=pltpu.SMEM)
 HBM = pl.BlockSpec(memory_space=pltpu.HBM)
-PARAMS = pltpu.CompilerParams(vmem_limit_bytes=40 * 2**20)
+PARAMS = pltpu.CompilerParams(vmem_limit_bytes=60 * 1024 * 2**10)
 
 
 SMALL = pltpu.CompilerParams(vmem_limit_bytes=16 * 2**20)
@@ -476,7 +486,7 @@
 
 
 def block_inverse(held, x):
-    size, count = x.shape
+    size, _ = x.shape
     inner = lax.broadcasted_iota(jnp.int32, x.shape, 1) % size
     row_id = lax.broadcasted_iota(jnp.int32, x.shape, 0)
 
@@ -763,9 +773,9 @@
         scratch_shapes=[vmem(rows // LANES, cols, LANES)],
         compiler_params=PARAMS,
         name="strips",
-    )(place, cond_table, load, east_class, north_class)
+    )(place, cond_table, load, east_class.T, north_class.T)
+    from_n, from_s = exchange(strip_n, strip_s, "grp")
     from_w, from_e = exchange(strip_e, strip_w, "dev")
-    from_n, from_s = exchange(strip_n, strip_s, "grp")
     tap_count, tap_code, tap_amps = pl.pallas_call(
         functools.partial(tap_kernel, dims, all_cols),
         out_shape=[
@@ -777,7 +787,7 @@
         out_specs=[SMEM, VMEM, VMEM],
         compiler_params=SMALL,
         name="taps",
-    )(place, taps, tap_current)
+    )(place, taps.T, tap_current.T)
     corner_e_out, corner_w_out = pl.pallas_call(
         functools.partial(corner_kernel, cols),
         out_shape=[shape(corner_rows, LANES)] * 2,
@@ -786,9 +796,6 @@
         compiler_params=SMALL,
         name="corners",
     )(from_n, from_s)
-    shares, corner_e_out, corner_w_out = lax.optimization_barrier(
-        (shares, corner_e_out, corner_w_out)
-    )
     corner_w, corner_e = exchange(corner_e_out, corner_w_out, "dev")
     gathered = lax.all_to_all(
         shares.reshape(nd, share, LANES), AXES, split_axis=0, concat_axis=0, tiled=True
@@ -826,12 +833,14 @@
             shape(nd * slab_rows, LANES),
         ],
         in_specs=[SMEM] * 3 + [HBM] * 3 + [VMEM] * 6,
-        out_specs=[VMEM] * 5,
+        out_specs=[HBM] * 2 + [VMEM] * 3,
         scratch_shapes=[
+            vmem(ext_rows * wide0, LANES),
+            vmem(ext_rows * wide0, LANES),
             vmem(rows, cols, LANES),
             vmem(rows * HALO, LANES),
             vmem(rows * HALO, LANES),
-            pltpu.SemaphoreType.DMA((3,)),
+            pltpu.SemaphoreType.DMA((5,)),
             vmem(s2_rows, LANES),
             vmem(GROUP // 2, wide0, LANES),
             vmem(GROUP // 2, wide1, LANES),
@@ -852,9 +861,12 @@
     return pl.pallas_call(
         functools.partial(up_kernel, dims, shunts),
         out_shape=shape(rows, cols, LANES),
-        in_specs=[VMEM] * 7,
+        in_specs=[VMEM] + [HBM] * 2 + [VMEM] * 4,
         out_specs=VMEM,
         scratch_shapes=[
+            vmem(ext_rows * wide0, LANES),
+            vmem(ext_rows * wide0, LANES),
+            pltpu.SemaphoreType.DMA((2,)),
             vmem((q_rows + 4) * pitch2, LANES),
             vmem(rows1 * wide1, LANES),
             vmem(GROUP, wide1, LANES),

time: 175 us -> 153 us (0.87)
  local copies, waits for them, and re-layouts: 17.3 us -> 2.29 us
  waiting for transfers between devices: 13.3 us -> 6.89 us
    unnamed x40 -> x28, local copies, waits for them, and re-layouts: 17.3 us -> 2.29 us
    ppermute x6, waiting for transfers between devices: 10.4 us -> 3.05 us  [exchange(): return (lax.ppermute(tail, axis, up), lax.ppermute(head, axis, down))]
    all_to_all x1, starting transfers between devices: 4.92 us -> 2.69 us  [body(): lax.all_to_all(slab.reshape(nd, slab_rows, LANES), AXES, split_axis=0, co...]
    all_to_all x1, starting transfers between devices: 5.8 us -> 7.58 us  [body(): lax.all_to_all(shares.reshape(nd, share, LANES), AXES, split_axis=0, conc...]
    pallas_call x1, Pallas kernels: 2.71 us -> 4.47 us  [body(): pl.pallas_call(functools.partial(strip_kernel, dims), out_shape=[shape(de...]
  transfers between devices with their start and end apart: 8 -> 8, of which waited for: 4 -> 3; matrix products, arithmetic and copies ran while one was open for 0% -> 0% of each run, Pallas kernels for 30% -> 33%
where the time goes in v4:
time: 153 us; the launch traced here: 152 us
  Pallas kernels  90.1 us (59%)
  starting transfers between devices  28.3 us (18%)
  blocking collectives  23.6 us (15%)
  waiting for transfers between devices  6.89 us (5%)
  local copies, waits for them, and re-layouts  2.29 us (1%)
    pallas_call x1, Pallas kernels, body(): pl.pallas_call(functools.partial(down_kernel, dims, shunts), out_shape=[s...  40.5 us
    pallas_call x1, Pallas kernels, body(): pl.pallas_call(functools.partial(up_kernel, dims, shunts), out_shape=shap...  29.8 us
    all_to_all x1, blocking collectives, body(): back = lax.all_to_all(back, AXES, split_axis=0, concat_axis=0, tiled=True)  23.6 us
    ppermute x6, starting transfers between devices, exchange(): return (lax.ppermute(tail, axis, up), lax.ppermute(head, axis, down))  18 us
    all_to_all x1, starting transfers between devices, body(): lax.all_to_all(shares.reshape(nd, share, LANES), AXES, split_axis=0, conc...  7.58 us
    pallas_call x1, Pallas kernels, coarse_factor(): pl.pallas_call(functools.partial(factor_kernel, dims, pc), out_shape=coef...  6.65 us
    pallas_call x1, Pallas kernels, coarse_levels(): pl.pallas_call(functools.partial(coarse_kernel, dims, pc), out_shape=shap...  6.22 us
    pallas_call x1, Pallas kernels, body(): pl.pallas_call(functools.partial(strip_kernel, dims), out_shape=[shape(de...  4.47 us
  transfers between devices with their start and end apart: 8, of which 3 were waited for; matrix products, arithmetic and copies ran while one was open for 0% of the time, Pallas kernels for 33%

profile of v4, /device:TPU:1, one launch (start us, length us, event | category | flops | bytes accessed | tf_op | source)
XLA Modules:
  0.0 152.1 jit_solution(15534551354127767815)
XLA Ops:
  0.0 0.6 pad_add_fusion.place
  0.6 0.0 copy-start.9
  0.6 0.0 copy-start.10
  0.6 4.5 %strips.1 = (f32[2604,128]{1,0:T(8,128)}, f32[2604,128]{1,0:T(8,128)}, f32[384,128]{1,0:T(8,128)}, f32[384,128]{1,0:T(8,128)}, f32[2,32,256]{2,1,0:T(8,128)}, /*index=5*/f32[256,128]{1,0:T(8,128)}) custom-call(s32[4]{0:T(128)} %pad_add_fusion.place, f32[8]{0:T(128)} %table.1, f32[256,32,128]{2,1,0:T(8,128)} %own_hbm.1, s32[32,256]{1,0:T(8,128)} %bitcast.26, ...), custom_call_target="tpu_custom_call" | custom-call | tf_op jit(solution)/shard_map/strips/pallas_call | solution.py:766
  5.1 4.6 %collective-permute-start = (f32[2604,128]{1,0:T(8,128)}, f32[2604,128]{1,0:T(8,128)S(1)}, u32[]{:S(2)}, u32[]{:S(2)}) collective-permute-start(f32[2604,128]{1,0:T(8,128)} %get-tuple-element.31), channel_id=1, source_target_pairs={{0,1},{1,2},{2,3},{3,4},{4,5},{5,6},{6,7},{8,9},{9,10},{10,11},{11... | collective-permute-start | bytes 3999752 | tf_op jit(solution)/shard_map/ppermute | solution.py:28
  9.7 1.9 %collective-permute-start.1 = (f32[2604,128]{1,0:T(8,128)}, f32[2604,128]{1,0:T(8,128)S(1)}, u32[]{:S(2)}, u32[]{:S(2)}) collective-permute-start(f32[2604,128]{1,0:T(8,128)} %get-tuple-element.32), channel_id=1, source_target_pairs={{1,0},{2,1},{3,2},{4,3},{5,4},{6,5},{7,6},{9,8},{10,9},{11,10},{12... | collective-permute-start | bytes 3999752 | tf_op jit(solution)/shard_map/ppermute | solution.py:28
  11.6 3.1 %collective-permute-start.2 = (f32[384,128]{1,0:T(8,128)}, f32[384,128]{1,0:T(8,128)S(1)}, u32[]{:S(2)}, u32[]{:S(2)}) collective-permute-start(f32[384,128]{1,0:T(8,128)} %get-tuple-element.33), channel_id=1, source_target_pairs={{0,8},{8,16},{16,24},{1,9},{9,17},{17,25},{2,10},{10,18},{18,26},{... | collective-permute-start | bytes 589832 | tf_op jit(solution)/shard_map/ppermute | solution.py:28
  14.7 1.3 collective-permute-start.3
  16.0 7.6 %all-to-all-start.1 = ((f32[32,8,128]{2,1,0:T(8,128)}), f32[32,8,128]{2,1,0:T(8,128)S(1)}, u32[]{:S(2)}, u32[]{:S(2)}) async-start(f32[32,8,128]{2,1,0:T(8,128)} %bitcast.25), calls=%async_computation.1 | async-start | bytes 262144 | tf_op jit(solution)/shard_map/all_to_all | solution.py:800
  23.6 0.0 collective-permute-done.2.north
  23.6 0.0 copy-start.2
  23.6 0.4 collective-permute-done.3.south
  24.1 5.2 %collective-permute-start.4 = (f32[264,128]{1,0:T(8,128)S(1)}, f32[264,128]{1,0:T(8,128)S(1)}, u32[]{:S(2)}, u32[]{:S(2)}) collective-permute-start(f32[264,128]{1,0:T(8,128)S(1)} %get-tuple-element.35), channel_id=1, source_target_pairs={{0,1},{1,2},{2,3},{3,4},{4,5},{5,6},{6,7},{8,9},{9,10},{10,11},{11... | collective-permute-start | bytes 405512 | tf_op jit(solution)/shard_map/ppermute | solution.py:28
  29.3 1.9 %collective-permute-start.5 = (f32[264,128]{1,0:T(8,128)S(1)}, f32[264,128]{1,0:T(8,128)S(1)}, u32[]{:S(2)}, u32[]{:S(2)}) collective-permute-start(f32[264,128]{1,0:T(8,128)S(1)} %get-tuple-element.36), channel_id=1, source_target_pairs={{1,0},{2,1},{3,2},{4,3},{5,4},{6,5},{7,6},{9,8},{10,9},{11,10},{12... | collective-permute-start | bytes 405512 | tf_op jit(solution)/shard_map/ppermute | solution.py:28
  31.3 0.0 copy-done.9
  31.3 0.0 copy-done.10
  31.3 0.0 copy-done.13
  31.3 1.7 %taps.1 = (s32[1]{0:T(128)}, s32[16,128]{1,0:T(8,128)S(1)}, f32[16,128]{1,0:T(8,128)S(1)}) custom-call(s32[4]{0:T(128)S(1)} %copy-done.13, s32[16,128]{1,0:T(8,128)S(1)} %bitcast.19, f32[16,128]{1,0:T(8,128)S(1)} %bitcast.20), custom_call_target="tpu_custom_call" | custom-call | tf_op jit(solution)/shard_map/taps/pallas_call | solution.py:779
  33.0 0.0 copy-start.11
  33.0 0.0 copy-start.12
  33.0 0.0 collective-permute-done.4.corner_w
  33.0 0.0 copy-start.5
  33.0 2.6 %collective-permute-done.5.corner_e = f32[264,128]{1,0:T(8,128)S(1)} collective-permute-done((f32[264,128]{1,0:T(8,128)S(1)}, f32[264,128]{1,0:T(8,128)S(1)}, u32[]{:S(2)}, u32[]{:S(2)}) %collective-permute-start.5) | collective-permute-done | bytes 135200 | tf_op jit(solution)/shard_map/ppermute | solution.py:28
  35.7 0.0 collective-permute-done.west.west_hbm
  35.7 0.0 collective-permute-done.1.east.east_hbm
  35.7 0.0 copy-start.1
  35.7 0.0 copy-start.8
  35.7 0.9 copy-done.8
  36.6 0.7 coefs.1
  37.3 0.0 copy-done.2
  37.4 0.0 copy-done.3
  37.4 0.0 copy-start.4
  37.4 0.7 copy-done.4
  38.1 0.6 copy-done.7
  38.7 0.0 copy-done.11
  38.7 0.0 copy-done.12
  38.7 0.0 copy-done.5
  38.7 0.0 copy-done.6
  38.7 0.0 copy-done
  38.7 0.0 copy-done.1
  38.7 40.5 %fine_down.1 = (f32[16128,128]{1,0:T(8,128)}, f32[16128,128]{1,0:T(8,128)}, f32[3456,128]{1,0:T(8,128)}, f32[3456,128]{1,0:T(8,128)}, f32[512,128]{1,0:T(8,128)}) custom-call(s32[1]{0:T(128)} %get-tuple-element.28.tap_count, s32[2048]{0:T(1024)} %bitcast.21, f32[2048]{0:T(1024)} %bitcast.22, f32[256,32,128]{2,1,0:T(8,128)} %own_hbm.1, f32[2604,128]{1,0:T(8,128)} %copy-done, ...), custom_call_target="tpu_custom_call" | custom-call | tf_op jit(solution)/shard_map/fine_down/pallas_call | solution.py:826
  79.2 0.0 all-to-all-done.1
  79.2 2.7 %all-to-all-start = ((f32[32,16,128]{2,1,0:T(8,128)}), f32[32,16,128]{2,1,0:T(8,128)S(1)}, u32[]{:S(2)}, u32[]{:S(2)}) async-start(f32[32,16,128]{2,1,0:T(8,128)} %bitcast.24), calls=%async_computation | async-start | bytes 524288 | tf_op jit(solution)/shard_map/all_to_all | solution.py:854
  81.9 6.6 %coarse_factor.1 = (f32[3,256,256]{2,1,0:T(8,128)S(1)}, f32[3,128,128]{2,1,0:T(8,128)S(1)}, f32[3,64,128]{2,1,0:T(8,128)S(1)}, f32[5,5,8,256]{3,2,1,0:T(8,128)S(1)}, f32[8,256]{1,0:T(8,128)S(1)}) custom-call(f32[256,128]{1,0:T(8,128)S(1)} %bitcast.18), custom_call_target="tpu_custom_call" | custom-call | tf_op jit(solution)/shard_map/coarse_factor/pallas_call | solution.py:714
  88.6 3.8 %all-to-all-done = f32[32,16,128]{2,1,0:T(8,128)S(1)} async-done(((f32[32,16,128]{2,1,0:T(8,128)}), f32[32,16,128]{2,1,0:T(8,128)S(1)}, u32[]{:S(2)}, u32[]{:S(2)}) %all-to-all-start) | async-done | bytes 262176 | tf_op jit(solution)/shard_map/all_to_all | solution.py:854
  92.4 6.2 %coarse_levels.1 = f32[1536,128]{1,0:T(8,128)S(1)} custom-call(f32[512,128]{1,0:T(8,128)S(1)} %bitcast.17, f32[3,256,256]{2,1,0:T(8,128)S(1)} %get-tuple-element.42.refs_0_, f32[3,128,128]{2,1,0:T(8,128)S(1)} %get-tuple-element.43.refs_1_, f32[3,64,128]{2,1,0:T(8,128)S(1)} %get-tuple-element.44.refs_2_, f32[5,5,8,256]{3,2,1,0:T(8,128)S(1)} %get-tuple-element.45.refs_3_, ...), custom_call_target="tpu_custom_call" | custom-call | tf_op jit(solution)/shard_map/coarse_levels/pallas_call | solution.py:731
  98.6 23.6 %all_to_all.15 = f32[32,48,128]{2,1,0:T(8,128)} all-to-all(f32[32,48,128]{2,1,0:T(8,128)S(1)} %bitcast.16), channel_id=1, replica_groups=mesh['grp'=4,'dev'=8] {'grp','dev'}, dimensions={0} | all-to-all | bytes 1572864 | tf_op jit(solution)/shard_map/all_to_all | solution.py:859
  122.3 29.8 %fine_up.1 = f32[256,32,128]{2,1,0:T(8,128)} custom-call(f32[1536,128]{1,0:T(8,128)} %bitcast.23, f32[16128,128]{1,0:T(8,128)} %get-tuple-element.47.s0_hbm, f32[16128,128]{1,0:T(8,128)} %get-tuple-element.48.p0_hbm, f32[3456,128]{1,0:T(8,128)} %get-tuple-element.49.s1, f32[3456,128]{1,0:T(8,128)} %get-tuple-element.50.p1, f32[3,3,56,128]{3,2,1,0:T(8,128)} %copy-done.4, ...), custom_call_target="tpu_custom_call" | custom-call | tf_op jit(solution)/shard_map/fine_up/pallas_call | solution.py:861
  (6 shorter events, 0.0 us)
Async XLA Ops:
  0.6 30.6 %copy-start.9 = (s32[128,16]{0,1:T(8,128)S(1)}, s32[128,16]{0,1:T(8,128)}, u32[]{:S(2)}) copy-start(s32[128,16]{0,1:T(8,128)} %param.10) | copy-start | bytes 24580
  0.6 30.7 %copy-start.10 = (f32[128,16]{0,1:T(8,128)S(1)}, f32[128,16]{0,1:T(8,128)}, u32[]{:S(2)}) copy-start(f32[128,16]{0,1:T(8,128)} %param.11) | copy-start | bytes 24580
  0.6 30.7 %copy-start.13 = (s32[4]{0:T(128)S(1)}, s32[4]{0:T(128)}, u32[]{:S(2)}) copy-start(s32[4]{0:T(128)} %pad_add_fusion.place) | copy-start | bytes 52
  5.1 30.6 %collective-permute-start = (f32[2604,128]{1,0:T(8,128)}, f32[2604,128]{1,0:T(8,128)S(1)}, u32[]{:S(2)}, u32[]{:S(2)}) collective-permute-start(f32[2604,128]{1,0:T(8,128)} %get-tuple-element.31), channel_id=1, source_target_pairs={{0,1},{1,2},{2,3},{3,4},{4,5},{5,6},{6,7},{8,9},{9,10},{10,11},{11... | collective-permute-start | bytes 3999752 | tf_op jit(solution)/shard_map/ppermute | solution.py:28
  9.7 26.0 %collective-permute-start.1 = (f32[2604,128]{1,0:T(8,128)}, f32[2604,128]{1,0:T(8,128)S(1)}, u32[]{:S(2)}, u32[]{:S(2)}) collective-permute-start(f32[2604,128]{1,0:T(8,128)} %get-tuple-element.32), channel_id=1, source_target_pairs={{1,0},{2,1},{3,2},{4,3},{5,4},{6,5},{7,6},{9,8},{10,9},{11,10},{12... | collective-permute-start | bytes 3999752 | tf_op jit(solution)/shard_map/ppermute | solution.py:28
  11.6 12.0 %collective-permute-start.2 = (f32[384,128]{1,0:T(8,128)}, f32[384,128]{1,0:T(8,128)S(1)}, u32[]{:S(2)}, u32[]{:S(2)}) collective-permute-start(f32[384,128]{1,0:T(8,128)} %get-tuple-element.33), channel_id=1, source_target_pairs={{0,8},{8,16},{16,24},{1,9},{9,17},{17,25},{2,10},{10,18},{18,26},{... | collective-permute-start | bytes 589832 | tf_op jit(solution)/shard_map/ppermute | solution.py:28
  14.7 9.3 %collective-permute-start.3 = (f32[384,128]{1,0:T(8,128)}, f32[384,128]{1,0:T(8,128)S(1)}, u32[]{:S(2)}, u32[]{:S(2)}) collective-permute-start(f32[384,128]{1,0:T(8,128)} %get-tuple-element.34), channel_id=1, source_target_pairs={{8,0},{16,8},{24,16},{9,1},{17,9},{25,17},{10,2},{18,10},{26,18},{... | collective-permute-start | bytes 589832 | tf_op jit(solution)/shard_map/ppermute | solution.py:28
  16.0 63.2 %all-to-all-start.1 = ((f32[32,8,128]{2,1,0:T(8,128)}), f32[32,8,128]{2,1,0:T(8,128)S(1)}, u32[]{:S(2)}, u32[]{:S(2)}) async-start(f32[32,8,128]{2,1,0:T(8,128)} %bitcast.25), calls=%async_computation.1 | async-start | bytes 262144 | tf_op jit(solution)/shard_map/all_to_all | solution.py:800
  23.6 13.7 %copy-start.2 = (f32[384,128]{1,0:T(8,128)}, f32[384,128]{1,0:T(8,128)S(1)}, u32[]{:S(2)}) copy-start(f32[384,128]{1,0:T(8,128)S(1)} %collective-permute-done.2.north) | copy-start | bytes 589828
  24.1 13.3 %copy-start.3 = (f32[384,128]{1,0:T(8,128)}, f32[384,128]{1,0:T(8,128)S(1)}, u32[]{:S(2)}) copy-start(f32[384,128]{1,0:T(8,128)S(1)} %collective-permute-done.3.south) | copy-start | bytes 589828
  24.1 8.9 %collective-permute-start.4 = (f32[264,128]{1,0:T(8,128)S(1)}, f32[264,128]{1,0:T(8,128)S(1)}, u32[]{:S(2)}, u32[]{:S(2)}) collective-permute-start(f32[264,128]{1,0:T(8,128)S(1)} %get-tuple-element.35), channel_id=1, source_target_pairs={{0,1},{1,2},{2,3},{3,4},{4,5},{5,6},{6,7},{8,9},{9,10},{10,11},{11... | collective-permute-start | bytes 405512 | tf_op jit(solution)/shard_map/ppermute | solution.py:28
  29.3 6.3 %collective-permute-start.5 = (f32[264,128]{1,0:T(8,128)S(1)}, f32[264,128]{1,0:T(8,128)S(1)}, u32[]{:S(2)}, u32[]{:S(2)}) collective-permute-start(f32[264,128]{1,0:T(8,128)S(1)} %get-tuple-element.36), channel_id=1, source_target_pairs={{1,0},{2,1},{3,2},{4,3},{5,4},{6,5},{7,6},{9,8},{10,9},{11,10},{12... | collective-permute-start | bytes 405512 | tf_op jit(solution)/shard_map/ppermute | solution.py:28
  33.0 5.7 %copy-start.11 = (s32[16,128]{1,0:T(8,128)}, s32[16,128]{1,0:T(8,128)S(1)}, u32[]{:S(2)}) copy-start(s32[16,128]{1,0:T(8,128)S(1)} %get-tuple-element.29) | copy-start | bytes 24580
  33.0 5.7 %copy-start.12 = (f32[16,128]{1,0:T(8,128)}, f32[16,128]{1,0:T(8,128)S(1)}, u32[]{:S(2)}) copy-start(f32[16,128]{1,0:T(8,128)S(1)} %get-tuple-element.30) | copy-start | bytes 24580
  33.0 5.7 %copy-start.5 = (f32[264,128]{1,0:T(8,128)}, f32[264,128]{1,0:T(8,128)S(1)}, u32[]{:S(2)}) copy-start(f32[264,128]{1,0:T(8,128)S(1)} %collective-permute-done.4.corner_w) | copy-start | bytes 405508
  35.7 3.0 %copy-start.6 = (f32[264,128]{1,0:T(8,128)}, f32[264,128]{1,0:T(8,128)S(1)}, u32[]{:S(2)}) copy-start(f32[264,128]{1,0:T(8,128)S(1)} %collective-permute-done.5.corner_e) | copy-start | bytes 405508
  35.7 3.0 %copy-start = (f32[2604,128]{1,0:T(8,128)}, f32[2604,128]{1,0:T(8,128)S(1)}, u32[]{:S(2)}) copy-start(f32[2604,128]{1,0:T(8,128)S(1)} %collective-permute-done.west.west_hbm) | copy-start | bytes 3999748
  35.7 3.0 %copy-start.1 = (f32[2604,128]{1,0:T(8,128)}, f32[2604,128]{1,0:T(8,128)S(1)}, u32[]{:S(2)}) copy-start(f32[2604,128]{1,0:T(8,128)S(1)} %collective-permute-done.1.east.east_hbm) | copy-start | bytes 3999748
  35.7 0.9 copy-start.8
  37.4 0.7 copy-start.4
  38.1 0.6 copy-start.7
  79.2 13.2 %all-to-all-start = ((f32[32,16,128]{2,1,0:T(8,128)}), f32[32,16,128]{2,1,0:T(8,128)S(1)}, u32[]{:S(2)}, u32[]{:S(2)}) async-start(f32[32,16,128]{2,1,0:T(8,128)} %bitcast.24), calls=%async_computation | async-start | bytes 524288 | tf_op jit(solution)/shard_map/all_to_all | solution.py:854

commit v5 on v4

--- a/solution.py
+++ b/solution.py
@@ -31,7 +31,9 @@
 RING = 4 * GROUP
 
 
-def wave(groups, stop, width, coef, coef_first, shunt, rings, fill, source, middle, finish):
+def wave(
+    groups, stop, width, coef, coef_first, spread_weight, shunt, rings, fill, source, middle, finish
+):
     ring_e, ring_n, ring_w, ring_a, ring_b, flux_b, again_b, flux_c, turn = rings
     low, high = groups
     per_tile = LANES // GROUP
@@ -58,15 +60,23 @@
     def go(t, carry):
         g = jnp.minimum(t, high - 1)
         shift = lax.rem(LANES - lax.rem(g, per_tile) * GROUP, LANES)
+        kinds = 3 if spread_weight else 2
         found = [
             pltpu.roll(coef[k, g // per_tile, pl.ds(coef_first, width), :], shift, 1)
-            for k in range(3)
+            for k in range(kinds)
         ]
+        east = at(ring_e, g * GROUP + RING - 1)
         for r in range(GROUP):
             row = g * GROUP + r
-            east, north, weight = (
+            west = east
+            east, north, *rest = (
                 jnp.broadcast_to(x[:, r : r + 1], (width, LANES)) for x in found
             )
+            if spread_weight:
+                (weight,) = rest
+            else:
+                south = pltpu.roll(north, 1, 0)
+                weight = RELAXATION / ((shunt + east + west) + (north + south))
             put(ring_e, row, east)
             put(ring_n, row, north)
             put(ring_w, row, weight)
@@ -303,7 +313,7 @@
     save_p0 = pltpu.make_async_copy(p0, p0_out, sems.at[4])
     save_s0.start()
 
-    def smooth_and_restrict(source, pre, coef, shunt, pair, rings, store):
+    def smooth_and_restrict(source, pre, coef, spread_weight, shunt, pair, rings, store):
         width = pair.shape[1]
         held = []
 
@@ -322,7 +332,7 @@
 
         groups = source.shape[0] // width // GROUP
         wave(
-            (0, groups), groups - 1, width, coef, 0, shunt, rings,
+            (0, groups), groups - 1, width, coef, 0, spread_weight, shunt, rings,
             lambda r, row, weight: weight * row_of(source, row),
             lambda row: row_of(source, row), middle, finish,
         )
@@ -335,7 +345,7 @@
             pair[m, pl.ds(start, half, stride=2), :] + pair[m, pl.ds(start + 1, half, stride=2), :]
         )
 
-    smooth_and_restrict(s0, p0, coef0, shunts[0], pair, rings0, store1)
+    smooth_and_restrict(s0, p0, coef0, False, shunts[0], pair, rings0, store1)
     save_p0.start()
     quarter = cols // 4
 
@@ -344,7 +354,7 @@
             pair1[m, pl.ds(4, quarter, stride=2), :] + pair1[m, pl.ds(5, quarter, stride=2), :]
         )
 
-    smooth_and_restrict(s1, p1, coef1, shunts[1], pair1, rings1, store2)
+    smooth_and_restrict(s1, p1, coef1, True, shunts[1], pair1, rings1, store2)
     rows2 = rows // 4
     per = LANES // rows2
     groups = quarter // per
@@ -405,7 +415,7 @@
 
     groups1 = s1.shape[0] // width1 // GROUP
     wave(
-        (0, groups1), groups1, width1, coef1, 0, shunts[1], rings1,
+        (0, groups1), groups1, width1, coef1, 0, True, shunts[1], rings1,
         fill1, source1, lambda row, value: None, finish1,
     )
 
@@ -428,7 +438,7 @@
         out[row] = done[HALO - 2 : HALO - 2 + cols]
 
     wave(
-        (first - 1, last + 1), last, width0, coef0, start, shunts[0], rings0,
+        (first - 1, last + 1), last, width0, coef0, start, False, shunts[0], rings0,
         fill0, source0, lambda row, value: None, finish0,
     )
 

time: 153 us -> 149 us (0.974)
  Pallas kernels: 90.1 us -> 85.6 us
    pallas_call x1, Pallas kernels: 40.5 us -> 37.7 us  [body(): pl.pallas_call(functools.partial(down_kernel, dims, shunts), out_shape=[s...]
    pallas_call x1, Pallas kernels: 29.8 us -> 28.1 us  [body(): pl.pallas_call(functools.partial(up_kernel, dims, shunts), out_shape=shap...]
  transfers between devices with their start and end apart: 8 -> 8, of which waited for: 3 -> 3; matrix products, arithmetic and copies ran while one was open for 0% -> 0% of each run, Pallas kernels for 33% -> 32%
where the time goes in v5:
time: 149 us; the launch traced here: 148 us
  Pallas kernels  85.6 us (57%)
  starting transfers between devices  28.3 us (19%)
  blocking collectives  23.6 us (16%)
  waiting for transfers between devices  6.89 us (5%)
  local copies, waits for them, and re-layouts  2.29 us (2%)
    pallas_call x1, Pallas kernels, body(): pl.pallas_call(functools.partial(down_kernel, dims, shunts), out_shape=[s...  37.7 us
    pallas_call x1, Pallas kernels, body(): pl.pallas_call(functools.partial(up_kernel, dims, shunts), out_shape=shap...  28.1 us
    all_to_all x1, blocking collectives, body(): back = lax.all_to_all(back, AXES, split_axis=0, concat_axis=0, tiled=True)  23.6 us
    ppermute x6, starting transfers between devices, exchange(): return (lax.ppermute(tail, axis, up), lax.ppermute(head, axis, down))  18 us
    all_to_all x1, starting transfers between devices, body(): lax.all_to_all(shares.reshape(nd, share, LANES), AXES, split_axis=0, conc...  7.58 us
    pallas_call x1, Pallas kernels, coarse_factor(): pl.pallas_call(functools.partial(factor_kernel, dims, pc), out_shape=coef...  6.65 us
    pallas_call x1, Pallas kernels, coarse_levels(): pl.pallas_call(functools.partial(coarse_kernel, dims, pc), out_shape=shap...  6.22 us
    pallas_call x1, Pallas kernels, body(): pl.pallas_call(functools.partial(strip_kernel, dims), out_shape=[shape(de...  4.47 us
  transfers between devices with their start and end apart: 8, of which 3 were waited for; matrix products, arithmetic and copies ran while one was open for 0% of the time, Pallas kernels for 32%

profile of v5, /device:TPU:1, one launch (start us, length us, event | category | flops | bytes accessed | tf_op | source)
XLA Modules:
  0.0 147.6 jit_solution(630052401792078914)
XLA Ops:
  0.0 0.6 pad_add_fusion.place
  0.6 0.0 copy-start.9
  0.6 0.0 copy-start.10
  0.6 4.5 %strips.1 = (f32[2604,128]{1,0:T(8,128)}, f32[2604,128]{1,0:T(8,128)}, f32[384,128]{1,0:T(8,128)}, f32[384,128]{1,0:T(8,128)}, f32[2,32,256]{2,1,0:T(8,128)}, /*index=5*/f32[256,128]{1,0:T(8,128)}) custom-call(s32[4]{0:T(128)} %pad_add_fusion.place, f32[8]{0:T(128)} %table.1, f32[256,32,128]{2,1,0:T(8,128)} %own_hbm.1, s32[32,256]{1,0:T(8,128)} %bitcast.26, ...), custom_call_target="tpu_custom_call" | custom-call | tf_op jit(solution)/shard_map/strips/pallas_call | solution.py:776
  5.1 4.6 %collective-permute-start = (f32[2604,128]{1,0:T(8,128)}, f32[2604,128]{1,0:T(8,128)S(1)}, u32[]{:S(2)}, u32[]{:S(2)}) collective-permute-start(f32[2604,128]{1,0:T(8,128)} %get-tuple-element.31), channel_id=1, source_target_pairs={{0,1},{1,2},{2,3},{3,4},{4,5},{5,6},{6,7},{8,9},{9,10},{10,11},{11... | collective-permute-start | bytes 3999752 | tf_op jit(solution)/shard_map/ppermute | solution.py:28
  9.7 1.9 %collective-permute-start.1 = (f32[2604,128]{1,0:T(8,128)}, f32[2604,128]{1,0:T(8,128)S(1)}, u32[]{:S(2)}, u32[]{:S(2)}) collective-permute-start(f32[2604,128]{1,0:T(8,128)} %get-tuple-element.32), channel_id=1, source_target_pairs={{1,0},{2,1},{3,2},{4,3},{5,4},{6,5},{7,6},{9,8},{10,9},{11,10},{12... | collective-permute-start | bytes 3999752 | tf_op jit(solution)/shard_map/ppermute | solution.py:28
  11.6 3.1 %collective-permute-start.2 = (f32[384,128]{1,0:T(8,128)}, f32[384,128]{1,0:T(8,128)S(1)}, u32[]{:S(2)}, u32[]{:S(2)}) collective-permute-start(f32[384,128]{1,0:T(8,128)} %get-tuple-element.33), channel_id=1, source_target_pairs={{0,8},{8,16},{16,24},{1,9},{9,17},{17,25},{2,10},{10,18},{18,26},{... | collective-permute-start | bytes 589832 | tf_op jit(solution)/shard_map/ppermute | solution.py:28
  14.7 1.3 collective-permute-start.3
  16.0 7.6 %all-to-all-start.1 = ((f32[32,8,128]{2,1,0:T(8,128)}), f32[32,8,128]{2,1,0:T(8,128)S(1)}, u32[]{:S(2)}, u32[]{:S(2)}) async-start(f32[32,8,128]{2,1,0:T(8,128)} %bitcast.25), calls=%async_computation.1 | async-start | bytes 262144 | tf_op jit(solution)/shard_map/all_to_all | solution.py:810
  23.6 0.0 collective-permute-done.2.north
  23.6 0.0 copy-start.2
  23.6 0.4 collective-permute-done.3.south
  24.1 5.2 %collective-permute-start.4 = (f32[264,128]{1,0:T(8,128)S(1)}, f32[264,128]{1,0:T(8,128)S(1)}, u32[]{:S(2)}, u32[]{:S(2)}) collective-permute-start(f32[264,128]{1,0:T(8,128)S(1)} %get-tuple-element.35), channel_id=1, source_target_pairs={{0,1},{1,2},{2,3},{3,4},{4,5},{5,6},{6,7},{8,9},{9,10},{10,11},{11... | collective-permute-start | bytes 405512 | tf_op jit(solution)/shard_map/ppermute | solution.py:28
  29.3 1.9 %collective-permute-start.5 = (f32[264,128]{1,0:T(8,128)S(1)}, f32[264,128]{1,0:T(8,128)S(1)}, u32[]{:S(2)}, u32[]{:S(2)}) collective-permute-start(f32[264,128]{1,0:T(8,128)S(1)} %get-tuple-element.36), channel_id=1, source_target_pairs={{1,0},{2,1},{3,2},{4,3},{5,4},{6,5},{7,6},{9,8},{10,9},{11,10},{12... | collective-permute-start | bytes 405512 | tf_op jit(solution)/shard_map/ppermute | solution.py:28
  31.3 0.0 copy-done.9
  31.3 0.0 copy-done.10
  31.3 0.0 copy-done.13
  31.3 1.7 %taps.1 = (s32[1]{0:T(128)}, s32[16,128]{1,0:T(8,128)S(1)}, f32[16,128]{1,0:T(8,128)S(1)}) custom-call(s32[4]{0:T(128)S(1)} %copy-done.13, s32[16,128]{1,0:T(8,128)S(1)} %bitcast.19, f32[16,128]{1,0:T(8,128)S(1)} %bitcast.20), custom_call_target="tpu_custom_call" | custom-call | tf_op jit(solution)/shard_map/taps/pallas_call | solution.py:789
  33.0 0.0 copy-start.11
  33.0 0.0 copy-start.12
  33.0 0.0 collective-permute-done.4.corner_w
  33.0 0.0 copy-start.5
  33.0 2.6 %collective-permute-done.5.corner_e = f32[264,128]{1,0:T(8,128)S(1)} collective-permute-done((f32[264,128]{1,0:T(8,128)S(1)}, f32[264,128]{1,0:T(8,128)S(1)}, u32[]{:S(2)}, u32[]{:S(2)}) %collective-permute-start.5) | collective-permute-done | bytes 135200 | tf_op jit(solution)/shard_map/ppermute | solution.py:28
  35.7 0.0 collective-permute-done.west.west_hbm
  35.7 0.0 collective-permute-done.1.east.east_hbm
  35.7 0.0 copy-start.1
  35.7 0.0 copy-start.8
  35.7 0.9 copy-done.8
  36.6 0.7 coefs.1
  37.3 0.0 copy-done.2
  37.4 0.0 copy-done.3
  37.4 0.0 copy-start.4
  37.4 0.7 copy-done.4
  38.1 0.6 copy-done.7
  38.7 0.0 copy-done.11
  38.7 0.0 copy-done.12
  38.7 0.0 copy-done.5
  38.7 0.0 copy-done.6
  38.7 0.0 copy-done
  38.7 0.0 copy-done.1
  38.7 37.7 %fine_down.1 = (f32[16128,128]{1,0:T(8,128)}, f32[16128,128]{1,0:T(8,128)}, f32[3456,128]{1,0:T(8,128)}, f32[3456,128]{1,0:T(8,128)}, f32[512,128]{1,0:T(8,128)}) custom-call(s32[1]{0:T(128)} %get-tuple-element.28.tap_count, s32[2048]{0:T(1024)} %bitcast.21, f32[2048]{0:T(1024)} %bitcast.22, f32[256,32,128]{2,1,0:T(8,128)} %own_hbm.1, f32[2604,128]{1,0:T(8,128)} %copy-done, ...), custom_call_target="tpu_custom_call" | custom-call | tf_op jit(solution)/shard_map/fine_down/pallas_call | solution.py:836
  76.5 0.0 all-to-all-done.1
  76.5 2.7 %all-to-all-start = ((f32[32,16,128]{2,1,0:T(8,128)}), f32[32,16,128]{2,1,0:T(8,128)S(1)}, u32[]{:S(2)}, u32[]{:S(2)}) async-start(f32[32,16,128]{2,1,0:T(8,128)} %bitcast.24), calls=%async_computation | async-start | bytes 524288 | tf_op jit(solution)/shard_map/all_to_all | solution.py:864
  79.2 6.6 %coarse_factor.1 = (f32[3,256,256]{2,1,0:T(8,128)S(1)}, f32[3,128,128]{2,1,0:T(8,128)S(1)}, f32[3,64,128]{2,1,0:T(8,128)S(1)}, f32[5,5,8,256]{3,2,1,0:T(8,128)S(1)}, f32[8,256]{1,0:T(8,128)S(1)}) custom-call(f32[256,128]{1,0:T(8,128)S(1)} %bitcast.18), custom_call_target="tpu_custom_call" | custom-call | tf_op jit(solution)/shard_map/coarse_factor/pallas_call | solution.py:724
  85.8 3.8 %all-to-all-done = f32[32,16,128]{2,1,0:T(8,128)S(1)} async-done(((f32[32,16,128]{2,1,0:T(8,128)}), f32[32,16,128]{2,1,0:T(8,128)S(1)}, u32[]{:S(2)}, u32[]{:S(2)}) %all-to-all-start) | async-done | bytes 262176 | tf_op jit(solution)/shard_map/all_to_all | solution.py:864
  89.7 6.2 %coarse_levels.1 = f32[1536,128]{1,0:T(8,128)S(1)} custom-call(f32[512,128]{1,0:T(8,128)S(1)} %bitcast.17, f32[3,256,256]{2,1,0:T(8,128)S(1)} %get-tuple-element.42.refs_0_, f32[3,128,128]{2,1,0:T(8,128)S(1)} %get-tuple-element.43.refs_1_, f32[3,64,128]{2,1,0:T(8,128)S(1)} %get-tuple-element.44.refs_2_, f32[5,5,8,256]{3,2,1,0:T(8,128)S(1)} %get-tuple-element.45.refs_3_, ...), custom_call_target="tpu_custom_call" | custom-call | tf_op jit(solution)/shard_map/coarse_levels/pallas_call | solution.py:741
  95.9 23.6 %all_to_all.15 = f32[32,48,128]{2,1,0:T(8,128)} all-to-all(f32[32,48,128]{2,1,0:T(8,128)S(1)} %bitcast.16), channel_id=1, replica_groups=mesh['grp'=4,'dev'=8] {'grp','dev'}, dimensions={0} | all-to-all | bytes 1572864 | tf_op jit(solution)/shard_map/all_to_all | solution.py:869
  119.5 28.1 %fine_up.1 = f32[256,32,128]{2,1,0:T(8,128)} custom-call(f32[1536,128]{1,0:T(8,128)} %bitcast.23, f32[16128,128]{1,0:T(8,128)} %get-tuple-element.47.s0_hbm, f32[16128,128]{1,0:T(8,128)} %get-tuple-element.48.p0_hbm, f32[3456,128]{1,0:T(8,128)} %get-tuple-element.49.s1, f32[3456,128]{1,0:T(8,128)} %get-tuple-element.50.p1, f32[3,3,56,128]{3,2,1,0:T(8,128)} %copy-done.4, ...), custom_call_target="tpu_custom_call" | custom-call | tf_op jit(solution)/shard_map/fine_up/pallas_call | solution.py:871
  (6 shorter events, 0.0 us)
Async XLA Ops:
  0.6 30.6 %copy-start.9 = (s32[128,16]{0,1:T(8,128)S(1)}, s32[128,16]{0,1:T(8,128)}, u32[]{:S(2)}) copy-start(s32[128,16]{0,1:T(8,128)} %param.10) | copy-start | bytes 24580
  0.6 30.7 %copy-start.10 = (f32[128,16]{0,1:T(8,128)S(1)}, f32[128,16]{0,1:T(8,128)}, u32[]{:S(2)}) copy-start(f32[128,16]{0,1:T(8,128)} %param.11) | copy-start | bytes 24580
  0.6 30.7 %copy-start.13 = (s32[4]{0:T(128)S(1)}, s32[4]{0:T(128)}, u32[]{:S(2)}) copy-start(s32[4]{0:T(128)} %pad_add_fusion.place) | copy-start | bytes 52
  5.1 30.6 %collective-permute-start = (f32[2604,128]{1,0:T(8,128)}, f32[2604,128]{1,0:T(8,128)S(1)}, u32[]{:S(2)}, u32[]{:S(2)}) collective-permute-start(f32[2604,128]{1,0:T(8,128)} %get-tuple-element.31), channel_id=1, source_target_pairs={{0,1},{1,2},{2,3},{3,4},{4,5},{5,6},{6,7},{8,9},{9,10},{10,11},{11... | collective-permute-start | bytes 3999752 | tf_op jit(solution)/shard_map/ppermute | solution.py:28
  9.7 26.0 %collective-permute-start.1 = (f32[2604,128]{1,0:T(8,128)}, f32[2604,128]{1,0:T(8,128)S(1)}, u32[]{:S(2)}, u32[]{:S(2)}) collective-permute-start(f32[2604,128]{1,0:T(8,128)} %get-tuple-element.32), channel_id=1, source_target_pairs={{1,0},{2,1},{3,2},{4,3},{5,4},{6,5},{7,6},{9,8},{10,9},{11,10},{12... | collective-permute-start | bytes 3999752 | tf_op jit(solution)/shard_map/ppermute | solution.py:28
  11.6 12.0 %collective-permute-start.2 = (f32[384,128]{1,0:T(8,128)}, f32[384,128]{1,0:T(8,128)S(1)}, u32[]{:S(2)}, u32[]{:S(2)}) collective-permute-start(f32[384,128]{1,0:T(8,128)} %get-tuple-element.33), channel_id=1, source_target_pairs={{0,8},{8,16},{16,24},{1,9},{9,17},{17,25},{2,10},{10,18},{18,26},{... | collective-permute-start | bytes 589832 | tf_op jit(solution)/shard_map/ppermute | solution.py:28
  14.7 9.3 %collective-permute-start.3 = (f32[384,128]{1,0:T(8,128)}, f32[384,128]{1,0:T(8,128)S(1)}, u32[]{:S(2)}, u32[]{:S(2)}) collective-permute-start(f32[384,128]{1,0:T(8,128)} %get-tuple-element.34), channel_id=1, source_target_pairs={{8,0},{16,8},{24,16},{9,1},{17,9},{25,17},{10,2},{18,10},{26,18},{... | collective-permute-start | bytes 589832 | tf_op jit(solution)/shard_map/ppermute | solution.py:28
  16.0 60.4 %all-to-all-start.1 = ((f32[32,8,128]{2,1,0:T(8,128)}), f32[32,8,128]{2,1,0:T(8,128)S(1)}, u32[]{:S(2)}, u32[]{:S(2)}) async-start(f32[32,8,128]{2,1,0:T(8,128)} %bitcast.25), calls=%async_computation.1 | async-start | bytes 262144 | tf_op jit(solution)/shard_map/all_to_all | solution.py:810
  23.6 13.7 %copy-start.2 = (f32[384,128]{1,0:T(8,128)}, f32[384,128]{1,0:T(8,128)S(1)}, u32[]{:S(2)}) copy-start(f32[384,128]{1,0:T(8,128)S(1)} %collective-permute-done.2.north) | copy-start | bytes 589828
  24.1 13.3 %copy-start.3 = (f32[384,128]{1,0:T(8,128)}, f32[384,128]{1,0:T(8,128)S(1)}, u32[]{:S(2)}) copy-start(f32[384,128]{1,0:T(8,128)S(1)} %collective-permute-done.3.south) | copy-start | bytes 589828
  24.1 8.9 %collective-permute-start.4 = (f32[264,128]{1,0:T(8,128)S(1)}, f32[264,128]{1,0:T(8,128)S(1)}, u32[]{:S(2)}, u32[]{:S(2)}) collective-permute-start(f32[264,128]{1,0:T(8,128)S(1)} %get-tuple-element.35), channel_id=1, source_target_pairs={{0,1},{1,2},{2,3},{3,4},{4,5},{5,6},{6,7},{8,9},{9,10},{10,11},{11... | collective-permute-start | bytes 405512 | tf_op jit(solution)/shard_map/ppermute | solution.py:28
  29.3 6.3 %collective-permute-start.5 = (f32[264,128]{1,0:T(8,128)S(1)}, f32[264,128]{1,0:T(8,128)S(1)}, u32[]{:S(2)}, u32[]{:S(2)}) collective-permute-start(f32[264,128]{1,0:T(8,128)S(1)} %get-tuple-element.36), channel_id=1, source_target_pairs={{1,0},{2,1},{3,2},{4,3},{5,4},{6,5},{7,6},{9,8},{10,9},{11,10},{12... | collective-permute-start | bytes 405512 | tf_op jit(solution)/shard_map/ppermute | solution.py:28
  33.0 5.7 %copy-start.11 = (s32[16,128]{1,0:T(8,128)}, s32[16,128]{1,0:T(8,128)S(1)}, u32[]{:S(2)}) copy-start(s32[16,128]{1,0:T(8,128)S(1)} %get-tuple-element.29) | copy-start | bytes 24580
  33.0 5.7 %copy-start.12 = (f32[16,128]{1,0:T(8,128)}, f32[16,128]{1,0:T(8,128)S(1)}, u32[]{:S(2)}) copy-start(f32[16,128]{1,0:T(8,128)S(1)} %get-tuple-element.30) | copy-start | bytes 24580
  33.0 5.7 %copy-start.5 = (f32[264,128]{1,0:T(8,128)}, f32[264,128]{1,0:T(8,128)S(1)}, u32[]{:S(2)}) copy-start(f32[264,128]{1,0:T(8,128)S(1)} %collective-permute-done.4.corner_w) | copy-start | bytes 405508
  35.7 3.0 %copy-start.6 = (f32[264,128]{1,0:T(8,128)}, f32[264,128]{1,0:T(8,128)S(1)}, u32[]{:S(2)}) copy-start(f32[264,128]{1,0:T(8,128)S(1)} %collective-permute-done.5.corner_e) | copy-start | bytes 405508
  35.7 3.0 %copy-start = (f32[2604,128]{1,0:T(8,128)}, f32[2604,128]{1,0:T(8,128)S(1)}, u32[]{:S(2)}) copy-start(f32[2604,128]{1,0:T(8,128)S(1)} %collective-permute-done.west.west_hbm) | copy-start | bytes 3999748
  35.7 3.0 %copy-start.1 = (f32[2604,128]{1,0:T(8,128)}, f32[2604,128]{1,0:T(8,128)S(1)}, u32[]{:S(2)}) copy-start(f32[2604,128]{1,0:T(8,128)S(1)} %collective-permute-done.1.east.east_hbm) | copy-start | bytes 3999748
  35.7 0.9 copy-start.8
  37.4 0.7 copy-start.4
  38.1 0.6 copy-start.7
  76.5 13.2 %all-to-all-start = ((f32[32,16,128]{2,1,0:T(8,128)}), f32[32,16,128]{2,1,0:T(8,128)S(1)}, u32[]{:S(2)}, u32[]{:S(2)}) async-start(f32[32,16,128]{2,1,0:T(8,128)} %bitcast.24), calls=%async_computation | async-start | bytes 524288 | tf_op jit(solution)/shard_map/all_to_all | solution.py:864
